TPU v7x, 32 devices: a whole 2x2x4 slice. The times are simulated.
32 devices in a mesh: rep: 8 (over z, x), tp: 4 (over y, core).
Axes of the slice: x: 2, y: 2, z: 4, core: 2. Of those that a mesh axis runs over, the one named last changes fastest.
Arguments:
- tokens: bfloat16 [64, 4096], P(('rep', 'tp')), may hold values from -6 to 6
- conv_state: bfloat16 [3, 64, 8192], P(None, 'rep', 'tp'), may hold values from -6 to 6
- ssm_state: float32 [64, 16, 8192], P('rep', None, 'tp'), may hold values from -6 to 6
- norm_gains: bfloat16 [2, 4096], P(None, ('rep', 'tp')), may hold values from 0.5 to 1.5
- conv_weight: bfloat16 [4, 8192], P(None, ('rep', 'tp')), may hold values from -3 to 3
- conv_skip: bfloat16 [2, 8192], P(None, ('rep', 'tp')), may hold values from -3 to 3
- step_bias: bfloat16 [8192], P(('rep', 'tp')), may hold values from -5 to -1
- decay_log: bfloat16 [16, 8192], P(None, ('rep', 'tp')), may hold values from 0 to 2.796875
- input_proj: bfloat16 [4096, 2, 8192], P(('rep', 'tp')), may hold values from -0.09375 to 0.09375
- select_proj: bfloat16 [8192, 288], P('tp', 'rep'), may hold values from -0.0625 to 0.0625
- step_proj: bfloat16 [256, 8192], P(('rep', 'tp')), may hold values from -0.375 to 0.375
- output_proj: bfloat16 [8192, 4096], P(None, ('rep', 'tp')), may hold values from -0.0625 to 0.0625
- router: bfloat16 [4096, 16], P(('rep', 'tp')), may hold values from -0.09375 to 0.09375
- expert_proj: bfloat16 [4096, 2, 2, 12288], P(('rep', 'tp')), may hold values from -0.09375 to 0.09375
- expert_ids: int32 [64, 2], P(('rep', 'tp')), may hold values from 0 to 15, as said below
Outputs:
- mamba_out: bfloat16 [64, 4096], P(('rep', 'tp'))
- conv_next: bfloat16 [3, 64, 8192], P(None, 'rep', 'tp')
- ssm_next: float32 [64, 16, 8192], P('rep', None, 'tp')
- expert_hidden: bfloat16 [128, 12288], P('rep', 'tp')
Inputs may be any that keep to these rules, and one draw needn't show every extreme that they name: `expert_ids`: each row names two different experts. Within each aligned block of 2 rows (the rows of one device) each expert e < 2 is named by at most 2 rows.
All inputs are finite; a program needn't handle non-finite values.
Results may differ from a plain program's by a relative error of at most 0.04.
Values may be sent and summed in bfloat16 or wider, within the bound.
A program may use at most 192 MiB of HBM per device.

v0:
```python
import functools

import jax
import jax.numpy as jnp
from jax import lax
from jax.experimental import pallas as pl
from jax.experimental.pallas import tpu as pltpu
from jax.sharding import PartitionSpec as P

CAPACITY = 2
LANES = 128


epsilon = 1e-05
MESH = pl.DeviceIdType.MESH


def send_kernel(plan, *refs):
    arrays = len(plan)
    sources, targets, sems = refs[:arrays], refs[arrays : 2 * arrays], refs[2 * arrays :]
    barrier = pltpu.get_barrier_semaphore()
    greeted = 0
    for axis, count in dict((axis, count) for axis, count, _ in plan).items():
        me = lax.axis_index(axis)
        for step in range(1, count):
            pl.semaphore_signal(
                barrier, inc=1, device_id={axis: lax.rem(me + step, count)}, device_id_type=MESH
            )
        greeted += count - 1
    pl.semaphore_wait(barrier, greeted)
    copies = []
    for which, (axis, count, mode) in enumerate(plan):
        me = lax.axis_index(axis)
        for step in range(1, count):
            peer = lax.rem(me + step, count)
            source = sources[which]
            if mode == "lanes":
                lanes = source.shape[-1] // count
                source = source.at[:, pl.ds(pl.multiple_of(peer * lanes, lanes), lanes)]
            elif mode == "lead":
                source = source.at[peer]
            copy = pltpu.make_async_remote_copy(
                src_ref=source,
                dst_ref=targets[which].at[me],
                send_sem=sems[2 * which].at[step - 1],
                recv_sem=sems[2 * which + 1].at[step - 1],
                device_id={axis: peer},
                device_id_type=MESH,
            )
            copy.start()
            copies.append(copy)
    for copy in copies:
        copy.wait()


def send(items, collective_id):
    shapes, plan, scratch = [], [], []
    for x, axis, mode in items:
        count = lax.axis_size(axis)
        if mode == "lanes":
            piece = x.shape[:-1] + (x.shape[-1] // count,)
        elif mode == "lead":
            piece = x.shape[1:]
        else:
            piece = x.shape
        shapes.append(jax.ShapeDtypeStruct((count,) + piece, x.dtype))
        plan.append((axis, count, mode))
        scratch += [pltpu.SemaphoreType.DMA((count - 1,))] * 2
    return pl.pallas_call(
        functools.partial(send_kernel, tuple(plan)),
        out_shape=shapes,
        in_specs=[pl.BlockSpec(memory_space=pl.ANY)] * len(items),
        out_specs=[pl.BlockSpec(memory_space=pl.ANY)] * len(items),
        scratch_shapes=scratch,
        compiler_params=pltpu.CompilerParams(collective_id=collective_id, has_side_effects=True),
    )(*[x for x, _, _ in items])


def own_piece(x, axis, mode):
    me = lax.axis_index(axis)
    if mode == "lanes":
        lanes = x.shape[-1] // lax.axis_size(axis)
        return lax.dynamic_slice_in_dim(x, me * lanes, lanes, x.ndim - 1)
    if mode == "lead":
        return lax.dynamic_index_in_dim(x, me, 0, keepdims=False)
    return x


def sum_of(item, got):
    total = own_piece(*item).astype(jnp.float32)
    me = lax.axis_index(item[1])
    for sender in range(got.shape[0]):
        total += jnp.where(me == sender, 0.0, got[sender].astype(jnp.float32))
    return total


def all_of(item, got):
    return lax.dynamic_update_index_in_dim(got, own_piece(*item), lax.axis_index(item[1]), 0)


def gather(x, axis, collective_id):
    item = (x, axis, "whole")
    return all_of(item, send([item], collective_id)[0])


def shards(
    tokens,
    conv_state,
    ssm_state,
    norm_gains,
    conv_weight,
    conv_skip,
    step_bias,
    decay_log,
    input_proj,
    select_proj,
    step_proj,
    output_proj,
    router,
    expert_proj,
    expert_ids,
):
    f32, bf16 = jnp.float32, jnp.bfloat16
    both = ("rep", "tp")
    tp_count = lax.axis_size("tp")
    rep_count = lax.axis_size("rep")
    count = tp_count * rep_count
    tp_index = lax.axis_index("tp")
    rep_index = lax.axis_index("rep")
    tok_dev, width = tokens.shape
    slice_dev = width // count
    token_count = tok_dev * count
    req = tok_dev * tp_count
    inner_all = input_proj.shape[2]
    inner_dev = ssm_state.shape[2]
    state_count = ssm_state.shape[1]
    step_rank = step_proj.shape[0] * count
    expert_total = router.shape[1]
    window_count = expert_proj.shape[1]

    tok = tokens.astype(f32)
    scale = lax.rsqrt(jnp.mean(tok * tok, axis=-1, keepdims=True) + epsilon)
    extra = jnp.concatenate([scale, expert_ids.astype(f32)], axis=1)
    extra = jnp.pad(extra, ((0, 0), (0, LANES - 3)))
    sent = jnp.concatenate(
        [
            tok.reshape(tok_dev, count, slice_dev),
            jnp.broadcast_to(extra[:, None, :], (tok_dev, count, LANES)),
        ],
        axis=2,
    ).transpose(1, 0, 2)
    got = lax.all_to_all(sent, both, split_axis=0, concat_axis=0, tiled=True)
    got = got.reshape(token_count, slice_dev + LANES)
    tok_slice = got[:, :slice_dev]
    scale_all = got[:, slice_dev : slice_dev + 1]
    ids_all = got[:, slice_dev + 1 : slice_dev + 3].astype(jnp.int32)

    gains = norm_gains.astype(f32)
    normed = (tok_slice * scale_all * gains[0]).astype(bf16)
    branches = input_proj.shape[1]
    diagonal = jnp.eye(branches, dtype=bf16)
    wide = (diagonal[:, None, None, :] * normed[None, :, :, None]).reshape(
        branches * token_count, slice_dev * branches
    )
    partial_in = jnp.dot(
        wide, input_proj.reshape(slice_dev * branches, inner_all), preferred_element_type=f32
    ).astype(bf16)
    packed = jnp.concatenate([conv_weight, conv_skip, step_bias[None], decay_log], axis=0)
    packed_rows = packed.shape[0]
    packed = jnp.pad(packed, ((0, -packed_rows % 16), (0, 0)))
    items = [
        (partial_in, "tp", "lanes"),
        (packed, "rep", "whole"),
        (step_proj, "rep", "whole"),
        (select_proj.T, "rep", "whole"),
    ]
    received = send(items, 0)
    partial_in = sum_of(items[0], received[0])
    packed, step_rows, select_rows = [
        all_of(item, got) for item, got in zip(items[1:], received[1:])
    ]
    select_rows = select_rows.reshape(-1, inner_dev)
    partial_in = partial_in.astype(bf16).reshape(branches, rep_count, req, inner_dev)
    items = [
        (partial_in[0], "rep", "lead"),
        (partial_in[1], "rep", "lead"),
        (packed, "tp", "whole"),
        (step_rows.reshape(-1, inner_all), "tp", "lanes"),
    ]
    received = send(items, 1)
    conv_input, gate_z = [sum_of(item, got) for item, got in zip(items[:2], received[:2])]
    packed = all_of(items[2], received[2])
    packed = packed.transpose(2, 1, 0, 3).reshape(-1, inner_all)[:packed_rows]
    step_rows = all_of(items[3], received[3])
    step_rows = step_rows.reshape(tp_count, rep_count, -1, inner_dev)
    step_rows = step_rows.transpose(1, 0, 2, 3).reshape(step_rank, inner_dev)
    packed = lax.dynamic_slice_in_dim(packed, tp_index * inner_dev, inner_dev, 1).astype(f32)
    taps = conv_weight.shape[0]
    conv_taps = packed[:taps]
    skip_rows = packed[taps : taps + 2]
    shift_dev = packed[taps + 2]
    decay_dev = packed[taps + 3 :]
    history = conv_state.astype(f32)
    conv_mix = (
        jnp.sum(conv_taps[:-1, None, :] * history, axis=0)
        + conv_taps[-1] * conv_input
        + skip_rows[0]
    )
    conv_next = jnp.concatenate([conv_state[1:], conv_input.astype(bf16)[None]], axis=0)
    activated = jax.nn.silu(conv_mix)
    select_part = lax.dot_general(
        activated.astype(bf16), select_rows, (((1,), (1,)), ((), ())), preferred_element_type=f32
    )
    selected = lax.psum(select_part.astype(bf16), "tp").astype(f32)
    step_low = selected[:, :step_rank].astype(bf16)
    input_map = selected[:, step_rank : step_rank + state_count]
    output_map = selected[:, step_rank + state_count :]
    step_size = jax.nn.softplus(
        jnp.dot(step_low, step_rows, preferred_element_type=f32) + shift_dev
    )
    decay_rate = -jnp.exp(decay_dev)
    factor = jnp.exp(step_size[:, None, :] * decay_rate[None])
    ssm_next = factor * ssm_state + (step_size * activated)[:, None, :] * input_map[:, :, None]
    readout = jnp.sum(ssm_next * output_map[:, :, None], axis=1) + skip_rows[1] * activated
    gated_out = (readout * jax.nn.silu(gate_z)).astype(bf16)

    gated_all = gather(gated_out, "rep", 2).reshape(token_count, inner_dev)
    gated_all = gather(gated_all, "tp", 3)
    gated_all = gated_all.transpose(1, 0, 2).reshape(token_count, inner_all)
    mixer_out = jnp.dot(gated_all, output_proj, preferred_element_type=f32)
    residual = tok_slice + mixer_out
    home = residual.astype(bf16).reshape(count, tok_dev, slice_dev)
    home = lax.all_to_all(home, both, split_axis=0, concat_axis=0, tiled=True)
    mamba_out = home.transpose(1, 0, 2).reshape(tok_dev, width)

    gained = residual * gains[1]
    logit_part = jnp.dot(
        gained, router.astype(f32), preferred_element_type=f32, precision=lax.Precision.HIGHEST
    )
    square_part = jnp.sum(residual * residual, axis=1, keepdims=True)
    summed = jnp.concatenate([logit_part, square_part], axis=1)
    summed = jnp.pad(summed, ((0, 0), (0, LANES - summed.shape[1])))
    summed = jnp.sum(gather(summed, "tp", 4), axis=0)
    summed = jnp.sum(gather(summed, "rep", 5), axis=0)
    scale_two = lax.rsqrt(summed[:, expert_total : expert_total + 1] / width + epsilon)
    logits = summed[:, :expert_total] * scale_two
    moe_in = (gained * scale_two).astype(bf16)

    choose = (
        ids_all[:, :, None] == jnp.arange(expert_total, dtype=jnp.int32)[None, None, :]
    ).astype(f32)
    picked = jnp.sum(choose * logits[:, None, :], axis=2)
    first_gate = jax.nn.sigmoid(picked[:, 0] - picked[:, 1])
    second_gate = jax.nn.sigmoid(picked[:, 1] - picked[:, 0])
    window = jnp.arange(window_count, dtype=jnp.int32)
    names_first = ids_all[:, 0:1] == window[None, :]
    names_second = ids_all[:, 1:2] == window[None, :]
    zero = jnp.zeros((), f32)
    gate_w = jnp.where(names_first, first_gate[:, None], zero) + jnp.where(
        names_second, second_gate[:, None], zero
    )
    routed = (names_first | names_second).astype(jnp.int32)
    routed = routed.reshape(count, tok_dev, window_count)
    position = jnp.cumsum(routed, axis=1) - routed
    slot_of = (position[..., None] == jnp.arange(CAPACITY, dtype=jnp.int32)) & (
        routed[..., None] > 0
    )
    slot_of = slot_of.astype(f32)
    blocks_x = moe_in.reshape(count, tok_dev, slice_dev).astype(f32)
    slot_x = jnp.sum(slot_of[..., None] * blocks_x[:, :, None, None, :], axis=1).astype(bf16)
    slot_gate = jnp.sum(slot_of * gate_w.reshape(count, tok_dev, window_count)[..., None], axis=1)
    slot_gate = slot_gate.astype(bf16)

    rows = count * CAPACITY
    pairs = window_count * 2
    diagonal = jnp.eye(pairs, dtype=bf16).reshape(window_count, 2, pairs)
    rows_of = slot_x.transpose(1, 0, 2, 3).reshape(window_count, rows, slice_dev)
    wide = diagonal[:, :, None, None, :] * rows_of[:, None, :, :, None]
    partial_up = jnp.dot(
        wide.reshape(pairs * rows, slice_dev * pairs),
        expert_proj.reshape(slice_dev * pairs, expert_proj.shape[3]),
        preferred_element_type=f32,
    ).astype(bf16)
    hidden_dev = expert_proj.shape[3] // tp_count
    own = rows // rep_count
    gate_up, waiting = [], []
    for expert in range(window_count + 1):
        items = list(waiting)
        if expert < window_count:
            half = partial_up[expert * 2 * rows : (expert + 1) * 2 * rows]
            items.append((half, "tp", "lanes"))
        received = send(items, 6 + expert)
        gate_up += [sum_of(item, got) for item, got in zip(waiting, received)]
        if expert < window_count:
            half = sum_of(items[-1], received[-1]).astype(bf16)
            half = half.reshape(2, rep_count, own, hidden_dev)
            waiting = [(half[0], "rep", "lead"), (half[1], "rep", "lead")]
    gate_up = jnp.stack(gate_up).reshape(
        window_count, 2, own // CAPACITY, CAPACITY, hidden_dev
    ).transpose(1, 2, 0, 3, 4)
    gate_up = gate_up.reshape(2, window_count * own, hidden_dev)
    own_slots = window_count * own
    gate_own = lax.dynamic_slice_in_dim(slot_gate.reshape(-1), rep_index * own_slots, own_slots, 0)
    hidden = (
        gate_own.astype(f32)[:, None]
        * jax.nn.silu(gate_up[0])
        * gate_up[1]
    )
    expert_hidden = hidden.astype(bf16)
    return (mamba_out, conv_next, ssm_next, expert_hidden)


def solution(mesh):
    in_specs = (
        P(("rep", "tp"), None),
        P(None, "rep", "tp"),
        P("rep", None, "tp"),
        P(None, ("rep", "tp")),
        P(None, ("rep", "tp")),
        P(None, ("rep", "tp")),
        P(("rep", "tp")),
        P(None, ("rep", "tp")),
        P(("rep", "tp"), None, None),
        P("tp", "rep"),
        P(("rep", "tp"), None),
        P(None, ("rep", "tp")),
        P(("rep", "tp"), None),
        P(("rep", "tp"), None, None, None),
        P(("rep", "tp"), None),
    )
    out_specs = (P(("rep", "tp"), None), P(None, "rep", "tp"), P("rep", None, "tp"), P("rep", "tp"))
    return jax.shard_map(shards, mesh=mesh, in_specs=in_specs, out_specs=out_specs, check_vma=False)
```

profile of v0, /device:TPU:0, one launch (start us, length us, event | category | flops | bytes accessed | tf_op | source)
XLA Modules:
  0.0 345.0 jit_solution(16532648257033114700)
XLA Ops:
  0.6 1.0 fusion.14
  1.7 0.7 convert_bitcast_fusion
  3.9 7.3 %all-to-all-start = ((f32[32,2,256]{2,1,0:T(2,128)}), f32[32,2,256]{2,1,0:T(2,128)S(1)}, u32[]{:S(2)}, u32[]{:S(2)}) async-start(f32[32,2,256]{2,1,0:T(2,128)} %maximum_bitcast_fusion), calls=%async_computation | async-start | bytes 131072 | tf_op jit(solution)/shard_map/all_to_all | solution.py:152
  13.0 7.2 %reshape.428 = bf16[256,8192]{1,0:T(8,128)(2,1)} reshape(bf16[128,2,8192]{2,1,0:T(2,128)(2,1)} %param.23) | data formatting | bytes 8388608 | tf_op jit(solution)/shard_map/reshape | solution.py:166
  20.3 25.0 %reshape.437 = bf16[512,12288]{1,0:T(8,128)(2,1)} reshape(bf16[128,2,2,12288]{3,2,1,0:T(2,128)(2,1)} %param.28) | data formatting | bytes 25165824 | tf_op jit(solution)/shard_map/reshape | solution.py:281
  46.6 4.3 %convolution_convert_fusion.1.refs_0_ = bf16[128,8192]{1,0:T(8,128)(2,1)} fusion(bf16[128,256]{0,1:T(8,128)(2,1)S(1)} %mul.267, bf16[256,8192]{1,0:T(8,128)(2,1)} %reshape.428), kind=kOutput, calls=%fused_computation.1 | convolution fusion | flops 537919488 | bytes 6356992 | tf_op jit(solution)/shard_map/dot_general | solution.py:165
  50.8 50.4 %shard_map.174 = (bf16[4,128,2048]{2,1,0:T(8,128)(2,1)}, bf16[8,32,256]{2,1,0:T(8,128)(2,1)}, bf16[8,8,8192]{2,1,0:T(8,128)(2,1)}, bf16[8,36,2048]{2,1,0:T(8,128)(2,1)}) custom-call(bf16[128,8192]{1,0:T(8,128)(2,1)} %convolution_convert_fusion.1.refs_0_, bf16[32,256]{1,0:T(8,128)(2,1)} %fusion.30.refs_1_, bf16[8,8192]{1,0:T(8,128)(2,1)} %refs_2_.1, ...), custom_call_target="tpu_custom_call" | custom-call | tf_op jit(solution)/shard_map/pallas_call | solution.py:69
  101.2 2.2 fusion.2
  103.4 0.8 slice_bitcast_fusion.4
  105.5 29.8 %shard_map.175 = (bf16[8,8,2048]{2,1,0:T(8,128)(2,1)}, bf16[8,8,2048]{2,1,0:T(8,128)(2,1)}, bf16[4,8,32,256]{3,2,1,0:T(8,128)(2,1)}, bf16[4,64,2048]{2,1,0:T(8,128)(2,1)}) custom-call(bf16[8,8,2048]{2,1,0:T(8,128)(2,1)} %get-tuple-element.47.refs_0_, bf16[8,8,2048]{2,1,0:T(8,128)(2,1)} %get-tuple-element.46.refs_1_, ...), custom_call_target="tpu_custom_call" | custom-call | tf_op jit(solution)/shard_map/pallas_call | solution.py:69
  136.0 1.1 slice.393
  137.4 1.0 slice.306
  138.4 0.9 dynamic-slice_convert_fusion
  140.6 0.9 slice_convert_fusion
  143.9 1.0 bitcast_dynamic-update-slice_fusion.1
  144.9 1.1 copy.98
  146.7 1.4 reshape.430
  148.1 1.6 fusion.38
  149.7 1.0 convolution_convert_fusion.2
  150.8 8.0 %psum.7 = bf16[8,288]{1,0:T(8,128)(2,1)S(1)} all-reduce(bf16[8,288]{1,0:T(8,128)(2,1)} %convolution_convert_fusion.2), channel_id=1, replica_groups=mesh['rep'=8,'tp'=4] {'tp'}, use_global_device_ids=true, to_apply=%region_2.3 | all-reduce | flops 2304 | bytes 9216 | tf_op jit(solution)/shard_map/psum | solution.py:214
  158.8 1.5 fusion.37
  160.4 1.5 multiply_reduce_fusion
  161.9 1.5 fusion.13
  163.4 8.7 %shard_map.176 = bf16[8,8,2048]{2,1,0:T(8,128)(2,1)} custom-call(bf16[8,2048]{1,0:T(8,128)(2,1)} %get-tuple-element.36.refs_0_), custom_call_target="tpu_custom_call" | custom-call | tf_op jit(solution)/shard_map/pallas_call | solution.py:69
  172.1 1.4 fusion.15
  173.4 12.5 %shard_map.177 = bf16[4,64,2048]{2,1,0:T(8,128)(2,1)} custom-call(bf16[64,2048]{1,0:T(8,128)(2,1)} %bitcast.181), custom_call_target="tpu_custom_call" | custom-call | tf_op jit(solution)/shard_map/pallas_call | solution.py:69
  186.0 1.7 bitcast_dynamic-update-slice_fusion
  187.7 1.3 copy.115
  190.6 5.9 %shard_map.178 = f32[4,64,128]{2,1,0:T(8,128)} custom-call(f32[64,128]{1,0:T(8,128)} %pad.14.refs_0_), custom_call_target="tpu_custom_call" | custom-call | tf_op jit(solution)/shard_map/pallas_call | solution.py:69
  197.1 1.5 reduce_sum.91.refs_0_
  198.7 9.2 %shard_map.179 = f32[8,64,128]{2,1,0:T(8,128)} custom-call(f32[64,128]{1,0:T(8,128)} %reduce_sum.91.refs_0_), custom_call_target="tpu_custom_call" | custom-call | tf_op jit(solution)/shard_map/pallas_call | solution.py:69
  207.9 1.4 bitcast_dynamic-update-slice_fusion.5
  209.3 1.0 reduce_sum.92
  213.0 8.3 %convolution_convert_fusion = bf16[256,12288]{1,0:T(8,128)(2,1)S(1)} fusion(bf16[256,512]{0,1:T(8,128)(2,1)S(1)} %mul.319, bf16[512,12288]{1,0:T(8,128)(2,1)} %reshape.437), kind=kOutput, calls=%fused_computation | convolution fusion | flops 3224371200 | bytes 19136512 | tf_op jit(solution)/shard_map/dot_general | solution.py:279
  221.4 3.1 fusion.39
  224.4 35.3 %shard_map.180 = bf16[4,128,3072]{2,1,0:T(8,128)(2,1)} custom-call(bf16[128,12288]{1,0:T(8,128)(2,1)} %get-tuple-element.41.refs_0_), custom_call_target="tpu_custom_call" | custom-call | tf_op jit(solution)/shard_map/pallas_call | solution.py:69
  259.7 2.8 fusion.1
  262.5 0.9 slice_bitcast_fusion.2
  263.5 40.4 %shard_map.181 = (bf16[8,8,3072]{2,1,0:T(8,128)(2,1)}, bf16[8,8,3072]{2,1,0:T(8,128)(2,1)}, bf16[4,128,3072]{2,1,0:T(8,128)(2,1)}) custom-call(bf16[8,8,3072]{2,1,0:T(8,128)(2,1)} %get-tuple-element.45.refs_0_, bf16[8,8,3072]{2,1,0:T(8,128)(2,1)} %get-tuple-element.44.refs_1_, bf16[128,12288]{1,0:T(8,128)(2,1)} %get-tuple-element.40.refs_2_), custom_call_target="tpu_custom_call" | custom-call | tf_op jit(solution)/shard_map/pallas_call | solution.py:69
  303.9 1.1 select_add_fusion.3
  305.0 1.1 select_add_fusion.2
  306.1 2.8 fusion
  308.9 0.9 slice_bitcast_fusion
  309.8 19.8 %shard_map.182 = (bf16[8,8,3072]{2,1,0:T(8,128)(2,1)}, bf16[8,8,3072]{2,1,0:T(8,128)(2,1)}) custom-call(bf16[8,8,3072]{2,1,0:T(8,128)(2,1)} %get-tuple-element.43.refs_0_, bf16[8,8,3072]{2,1,0:T(8,128)(2,1)} %get-tuple-element.42.refs_1_), custom_call_target="tpu_custom_call" | custom-call | tf_op jit(solution)/shard_map/pallas_call | solution.py:69
  329.6 1.1 select_add_fusion.1
  330.7 1.1 select_add_fusion
  332.4 4.9 %all-to-all-start.1 = ((bf16[32,2,128]{2,1,0:T(2,128)(2,1)}), bf16[32,2,128]{2,1,0:T(2,128)(2,1)S(1)}, u32[]{:S(2)}, u32[]{:S(2)}) async-start(bf16[32,2,128]{2,1,0:T(2,128)(2,1)} %bitcast.33), calls=%async_computation.1 | async-start | bytes 32768 | tf_op jit(solution)/shard_map/all_to_all | solution.py:233
  338.8 5.6 %all-to-all-done.1 = bf16[32,2,128]{2,1,0:T(2,128)(2,1)S(1)} async-done(((bf16[32,2,128]{2,1,0:T(2,128)(2,1)}), bf16[32,2,128]{2,1,0:T(2,128)(2,1)S(1)}, u32[]{:S(2)}, u32[]{:S(2)}) %all-to-all-start.1) | async-done | bytes 16416 | tf_op jit(solution)/shard_map/all_to_all | solution.py:233
  (134 shorter events, 18.8 us)
Async XLA Ops:
  0.6 188.4 %copy-start = (bf16[8192,128]{1,0:T(8,128)(2,1)S(1)}, bf16[8192,128]{1,0:T(8,128)(2,1)}, u32[]{:S(2)}) copy-start(bf16[8192,128]{1,0:T(8,128)(2,1)} %param.26) | copy-start | bytes 6291460
  3.9 41.9 %all-to-all-start = ((f32[32,2,256]{2,1,0:T(2,128)}), f32[32,2,256]{2,1,0:T(2,128)S(1)}, u32[]{:S(2)}, u32[]{:S(2)}) async-start(f32[32,2,256]{2,1,0:T(2,128)} %maximum_bitcast_fusion), calls=%async_computation | async-start | bytes 131072 | tf_op jit(solution)/shard_map/all_to_all | solution.py:152
  13.0 7.2 %copy-start.27 = (bf16[256]{0:T(256)(128)(2,1)S(1)}, bf16[256]{0:T(256)(128)(2,1)}, u32[]{:S(2)}) copy-start(bf16[256]{0:T(256)(128)(2,1)} %param.21) | copy-start | bytes 1540
  20.2 25.0 %copy-start.14 = (bf16[16,256]{1,0:T(8,128)(2,1)S(1)}, bf16[16,256]{1,0:T(8,128)(2,1)}, u32[]{:S(2)}) copy-start(bf16[16,256]{1,0:T(8,128)(2,1)} %param.22) | copy-start | bytes 24580
  20.2 25.0 %copy-start.22 = (bf16[4,256]{1,0:T(4,128)(2,1)S(1)}, bf16[4,256]{1,0:T(4,128)(2,1)}, u32[]{:S(2)}) copy-start(bf16[4,256]{1,0:T(4,128)(2,1)} %param.19) | copy-start | bytes 6148
  20.3 25.0 %copy-start.25 = (bf16[2,256]{1,0:T(2,128)(2,1)S(1)}, bf16[2,256]{1,0:T(2,128)(2,1)}, u32[]{:S(2)}) copy-start(bf16[2,256]{1,0:T(2,128)(2,1)} %param.20) | copy-start | bytes 3076
  45.9 4.9 %copy-start.5 = (f32[64,256]{1,0:T(8,128)}, f32[64,256]{1,0:T(8,128)S(1)}, u32[]{:S(2)}) copy-start(f32[64,256]{1,0:T(8,128)S(1)} %reshape.427) | copy-start | bytes 196612
  101.2 3.6 %copy-start.7 = (bf16[8,8192]{1,0:T(8,128)(2,1)S(1)}, bf16[8,8192]{1,0:T(8,128)(2,1)}, u32[]{:S(2)}) copy-start(bf16[8,8192]{1,0:T(8,128)(2,1)} %refs_2_.1) | copy-start | bytes 393220
  104.9 30.5 %copy-start.9 = (bf16[8,32,256]{2,1,0:T(8,128)(2,1)S(1)}, bf16[8,32,256]{2,1,0:T(8,128)(2,1)}, u32[]{:S(2)}) copy-start(bf16[8,32,256]{2,1,0:T(8,128)(2,1)} %bitcast_dynamic-update-slice_fusion.7.refs_2_) | copy-start | bytes 393220
  136.0 7.9 %copy-start.3 = (bf16[4,64,2048]{2,1,0:T(8,128)(2,1)S(1)}, bf16[4,64,2048]{2,1,0:T(8,128)(2,1)}, u32[]{:S(2)}) copy-start(bf16[4,64,2048]{2,1,0:T(8,128)(2,1)} %get-tuple-element.23) | copy-start | bytes 3145732
  139.9 6.0 %copy-start.10 = (bf16[3,8,2048]{2,1,0:T(8,128)(2,1)S(1)}, bf16[3,8,2048]{2,1,0:T(8,128)(2,1)}, u32[]{:S(2)}) copy-start(bf16[3,8,2048]{2,1,0:T(8,128)(2,1)} %param.16) | copy-start | bytes 294916
  140.6 5.4 %copy-start.4 = (bf16[2048,36]{0,1:T(8,128)(2,1)S(1)}, bf16[2048,36]{0,1:T(8,128)(2,1)}, u32[]{:S(2)}) copy-start(bf16[2048,36]{0,1:T(8,128)(2,1)} %param.24) | copy-start | bytes 442372
  142.5 3.5 %copy-start.16 = (s32[32,2]{0,1:T(2,128)}, s32[32,2]{0,1:T(2,128)S(1)}, u32[]{:S(2)}) copy-start(s32[32,2]{0,1:T(2,128)S(1)} %copy.101) | copy-start | bytes 772
  142.7 3.3 copy-start.18
  148.1 12.2 %copy-start.8 = (f32[16,2048]{1,0:T(8,128)S(1)}, f32[16,2048]{1,0:T(8,128)}, u32[]{:S(2)}) copy-start(f32[16,2048]{1,0:T(8,128)} %fusion.3) | copy-start | bytes 393220
  150.8 9.6 %copy-start.2 = (f32[8,16,2048]{2,1,0:T(8,128)S(1)}, f32[8,16,2048]{2,1,0:T(8,128)}, u32[]{:S(2)}) copy-start(f32[8,16,2048]{2,1,0:T(8,128)} %param.17) | copy-start | bytes 3145732
  158.8 3.1 copy-start.11
  158.8 3.1 copy-start.13
  186.0 3.0 copy-start.6
  189.0 0.7 copy-start.23
  189.0 0.7 copy-start.24
  189.0 22.1 %copy-start.26 = (s32[64,2]{0,1:T(2,128)S(1)}, s32[64,2]{0,1:T(2,128)}, u32[]{:S(2)}) copy-start(s32[64,2]{0,1:T(2,128)} %copy.103) | copy-start | bytes 1540
  189.0 22.5 %copy-start.17 = (s32[32,2]{0,1:T(2,128)S(1)}, s32[32,2]{0,1:T(2,128)}, u32[]{:S(2)}) copy-start(s32[32,2]{0,1:T(2,128)} %copy-done.16) | copy-start | bytes 772
  189.0 22.5 %copy-start.19 = (s32[32,2]{0,1:T(2,128)S(1)}, s32[32,2]{0,1:T(2,128)}, u32[]{:S(2)}) copy-start(s32[32,2]{0,1:T(2,128)} %copy-done.18) | copy-start | bytes 772
  189.1 22.5 %copy-start.15 = (s32[32,2,2]{0,2,1:T(2,128)S(1)}, s32[32,2,2]{0,2,1:T(2,128)}, u32[]{:S(2)}) copy-start(s32[32,2,2]{0,2,1:T(2,128)} %reduce-window_subtract_fusion) | copy-start | bytes 1540
  189.1 22.5 %copy-start.20 = (pred[32,2,2]{0,2,1:T(4,128)(4,1)S(1)}, pred[32,2,2]{0,2,1:T(4,128)(4,1)}, u32[]{:S(2)}) copy-start(pred[32,2,2]{0,2,1:T(4,128)(4,1)} %fusion.34) | copy-start | bytes 388
  189.7 22.5 %copy-start.21 = (bf16[2,2,4]{1,0,2:T(2,128)(2,1)S(1)}, bf16[2,2,4]{1,0,2:T(2,128)(2,1)}, u32[]{:S(2)}) copy-start(bf16[2,2,4]{1,0,2:T(2,128)(2,1)} %compare_convert_fusion) | copy-start | bytes 100
  331.8 13.3 %copy-start.1 = (bf16[8192,128]{1,0:T(8,128)(2,1)S(1)}, bf16[8192,128]{1,0:T(8,128)(2,1)}, u32[]{:S(2)}) copy-start(bf16[8192,128]{1,0:T(8,128)(2,1)} %param.26) | copy-start | bytes 6291460
  332.0 6.1 %slice-start = ((bf16[3,8,2048]{2,1,0:T(8,128)(2,1)}), bf16[2,8,2048]{2,1,0:T(8,128)(2,1)S(1)}, s32[]{:S(2)}) async-start(bf16[3,8,2048]{2,1,0:T(8,128)(2,1)} %param.16), calls=%async_computation.2 | async-start | bytes 131072 | tf_op jit(solution)/shard_map/slice | solution.py:209
  332.0 6.1 %copy-start.12 = (bf16[1,8,2048]{2,1,0:T(8,128)(2,1)S(1)}, bf16[1,8,2048]{2,1,0:T(8,128)(2,1)}, u32[]{:S(2)}) copy-start(bf16[1,8,2048]{2,1,0:T(8,128)(2,1)} %get-tuple-element.34) | copy-start | bytes 98308
  332.4 12.0 %all-to-all-start.1 = ((bf16[32,2,128]{2,1,0:T(2,128)(2,1)}), bf16[32,2,128]{2,1,0:T(2,128)(2,1)S(1)}, u32[]{:S(2)}, u32[]{:S(2)}) async-start(bf16[32,2,128]{2,1,0:T(2,128)(2,1)} %bitcast.33), calls=%async_computation.1 | async-start | bytes 32768 | tf_op jit(solution)/shard_map/all_to_all | solution.py:233
where the time goes:
time: 347 us; the launch traced here: 345 us
  Pallas kernels  212 us (61%)
  local copies, waits for them, and re-layouts  56.9 us (16%)
  other arithmetic  33.1 us (10%)
  matrix products  15.9 us (5%)
  starting transfers between devices  12.2 us (4%)
  blocking collectives  7.95 us (2%)
  waiting for transfers between devices  5.64 us (2%)
    pallas_call x9, Pallas kernels, send(): pl.pallas_call(functools.partial(send_kernel, tuple(plan)), out_shape=sha...  212 us
    reshape x1, local copies, waits for them, and re-layouts, shards(): expert_proj.reshape(slice_dev * pairs, expert_proj.shape[3])  25 us
    dot_general x1, matrix products, shards(): jnp.dot(wide.reshape(pairs * rows, slice_dev * pairs), expert_proj.reshap...  8.35 us
    psum x1, blocking collectives, shards(): selected = lax.psum(select_part.astype(bf16), 'tp').astype(f32)  7.95 us
    all_to_all x1, starting transfers between devices, shards(): got = lax.all_to_all(sent, both, split_axis=0, concat_axis=0, tiled=True)  7.33 us
    reshape x1, local copies, waits for them, and re-layouts, shards(): input_proj.reshape(slice_dev * branches, inner_all)  7.22 us
  transfers between devices with their start and end apart: 2, of which 1 were waited for; matrix products, arithmetic and copies ran while one was open for 10% of the time, Pallas kernels for 0%

commit v1 on v0

v1 whole, which is shorter than its diff:
```python
import functools

import jax
import jax.numpy as jnp
from jax import lax
from jax.experimental import pallas as pl
from jax.experimental.pallas import tpu as pltpu
from jax.sharding import PartitionSpec as P

CAPACITY = 2
LANES = 128


epsilon = 1e-05
MESH = pl.DeviceIdType.MESH


def send_kernel(plan, *refs):
    arrays = len(plan)
    sources, targets, sems = refs[:arrays], refs[arrays : 2 * arrays], refs[2 * arrays :]
    barrier = pltpu.get_barrier_semaphore()
    greeted = 0
    for axis, count in dict((axis, count) for axis, count, _ in plan).items():
        me = lax.axis_index(axis)
        for step in range(1, count):
            pl.semaphore_signal(
                barrier, inc=1, device_id={axis: lax.rem(me + step, count)}, device_id_type=MESH
            )
        greeted += count - 1
    pl.semaphore_wait(barrier, greeted)
    copies = []
    for which, (axis, count, mode) in enumerate(plan):
        me = lax.axis_index(axis)
        for step in range(1, count):
            peer = lax.rem(me + step, count)
            source = sources[which]
            if mode == "lanes":
                lanes = source.shape[-1] // count
                source = source.at[:, pl.ds(pl.multiple_of(peer * lanes, lanes), lanes)]
            elif mode == "lead":
                source = source.at[peer]
            copy = pltpu.make_async_remote_copy(
                src_ref=source,
                dst_ref=targets[which].at[me],
                send_sem=sems[2 * which].at[step - 1],
                recv_sem=sems[2 * which + 1].at[step - 1],
                device_id={axis: peer},
                device_id_type=MESH,
            )
            copy.start()
            copies.append(copy)
    for copy in copies:
        copy.wait()


def send(items, collective_id):
    shapes, plan, scratch = [], [], []
    for x, axis, mode in items:
        count = lax.axis_size(axis)
        if mode == "lanes":
            piece = x.shape[:-1] + (x.shape[-1] // count,)
        elif mode == "lead":
            piece = x.shape[1:]
        else:
            piece = x.shape
        shapes.append(jax.ShapeDtypeStruct((count,) + piece, x.dtype))
        plan.append((axis, count, mode))
        scratch += [pltpu.SemaphoreType.DMA((count - 1,))] * 2
    return pl.pallas_call(
        functools.partial(send_kernel, tuple(plan)),
        out_shape=shapes,
        in_specs=[pl.BlockSpec(memory_space=pl.ANY)] * len(items),
        out_specs=[pl.BlockSpec(memory_space=pl.ANY)] * len(items),
        scratch_shapes=scratch,
        compiler_params=pltpu.CompilerParams(collective_id=collective_id, has_side_effects=True),
    )(*[x for x, _, _ in items])


def own_piece(x, axis, mode):
    me = lax.axis_index(axis)
    if mode == "lanes":
        lanes = x.shape[-1] // lax.axis_size(axis)
        return lax.dynamic_slice_in_dim(x, me * lanes, lanes, x.ndim - 1)
    if mode == "lead":
        return lax.dynamic_index_in_dim(x, me, 0, keepdims=False)
    return x


def sum_of(item, got):
    total = own_piece(*item).astype(jnp.float32)
    me = lax.axis_index(item[1])
    for sender in range(got.shape[0]):
        total += jnp.where(me == sender, 0.0, got[sender].astype(jnp.float32))
    return total


def all_of(item, got):
    return lax.dynamic_update_index_in_dim(got, own_piece(*item), lax.axis_index(item[1]), 0)


def gather(x, axis, collective_id):
    item = (x, axis, "whole")
    return all_of(item, send([item], collective_id)[0])


CORES = 2
LANE_PAIR = 2
ROOM = 40 * 2**20


def split_of(rep_count, tp_count):
    return rep_count // CORES, CORES, tp_count // CORES, CORES


def start_all(copies):
    for copy in copies:
        copy.start()


class Reduce:
    def __init__(self, rep_count, tp_count, rows, dev_cols, total_chunks):
        self.z, self.x, self.y, self.c = split_of(rep_count, tp_count)
        self.rows = rows
        self.half = 2 * LANES if dev_cols % (4 * LANES) == 0 else LANES
        self.per = dev_cols // (2 * self.half)
        self.dev_cols = dev_cols
        self.chunks = total_chunks
        self.blocks = self.z * self.x * self.y

    def chunk_bytes(self):
        return self.c * 2 * self.blocks * self.rows * self.half * 2 * 2

    def scratch(self, depth):
        n, z, x, y, rows, half = self.chunks, self.z, self.x, self.y, self.rows, self.half
        bf16 = jnp.bfloat16
        groups = self.c * y * 2 * (half // LANES)
        dma = pltpu.SemaphoreType.DMA
        buffers = dict(
            w=pltpu.VMEM((n, groups, depth // 2, 2, LANES), bf16),
            b0=pltpu.VMEM((n, self.c, 2, self.blocks, rows, half), bf16),
            r0=pltpu.VMEM((n, 2, self.blocks, rows, half), bf16),
            r1a=pltpu.VMEM((n, y - 1, x * z, rows, half), bf16),
            r1b=pltpu.VMEM((n, x - 1, y * z, rows, half), bf16),
            r2a=pltpu.VMEM((n, x - 1, z, rows, half), bf16),
            r2b=pltpu.VMEM((n, y - 1, z, rows, half), bf16),
            b3=pltpu.VMEM((n, z, 2, rows, half), bf16),
            r3=pltpu.VMEM((n, z - 1, 2, rows, half), bf16),
            ws=dma((n,)),
            s0=dma((2, n)),
            s1a=dma((2, n, y - 1)),
            s1b=dma((2, n, x - 1)),
            s2a=dma((2, n, x - 1)),
            s2b=dma((2, n, y - 1)),
            s3=dma((2, n, z - 1)),
        )
        return buffers

    def place(self):
        rep, tp = lax.axis_index("rep"), lax.axis_index("tp")
        self.rep, self.tp = rep, tp
        self.mz, self.mx = lax.div(rep, self.x), lax.rem(rep, self.x)
        self.my, self.mc = lax.div(tp, self.c), lax.rem(tp, self.c)

    def peer_z(self, to):
        return {"rep": to * self.x + self.mx}

    def peer_x(self, to):
        return {"rep": self.mz * self.x + to}

    def peer_y(self, to):
        return {"tp": to * self.c + self.mc}

    def peer_c(self):
        return {"tp": self.my * self.c + 1 - self.mc}

    def peers(self):
        out = [self.peer_c()]
        out += [self.peer_y(lax.rem(self.my + s, self.y)) for s in range(1, self.y)]
        out += [self.peer_x(lax.rem(self.mx + s, self.x)) for s in range(1, self.x)]
        out += [self.peer_z(lax.rem(self.mz + s, self.z)) for s in range(1, self.z)]
        return out

    def exchange(self, source, count, me, size, target, sems, i, peer):
        copies = []
        for step in range(1, count):
            to = lax.rem(me + step, count)
            copies.append(
                pltpu.make_async_remote_copy(
                    src_ref=source.at[pl.ds(to * size, size)],
                    dst_ref=target.at[i, step - 1],
                    send_sem=sems.at[0, i, step - 1],
                    recv_sem=sems.at[1, i, step - 1],
                    device_id=peer(to),
                    device_id_type=MESH,
                )
            )
        return copies

    def copies(self, s, i, stage):
        z, x, y = self.z, self.x, self.y
        if stage == 0:
            return [
                pltpu.make_async_remote_copy(
                    src_ref=s["b0"].at[i, 1 - self.mc],
                    dst_ref=s["r0"].at[i],
                    send_sem=s["s0"].at[0, i],
                    recv_sem=s["s0"].at[1, i],
                    device_id=self.peer_c(),
                    device_id_type=MESH,
                )
            ]
        if stage == 1:
            return self.exchange(
                s["r0"].at[i, 0], y, self.my, x * z, s["r1a"], s["s1a"], i, self.peer_y
            ) + self.exchange(
                s["r0"].at[i, 1], x, self.mx, y * z, s["r1b"], s["s1b"], i, self.peer_x
            )
        if stage == 2:
            return self.exchange(
                s["r1a"].at[i, 0], x, self.mx, z, s["r2a"], s["s2a"], i, self.peer_x
            ) + self.exchange(
                s["r1b"].at[i, 0], y, self.my, z, s["r2b"], s["s2b"], i, self.peer_y
            )
        third = []
        for step in range(1, z):
            to = lax.rem(self.mz + step, z)
            third.append(
                pltpu.make_async_remote_copy(
                    src_ref=s["b3"].at[i, to],
                    dst_ref=s["r3"].at[i, step - 1],
                    send_sem=s["s3"].at[0, i, step - 1],
                    recv_sem=s["s3"].at[1, i, step - 1],
                    device_id=self.peer_z(to),
                    device_id_type=MESH,
                )
            )
        return third

    def fetch(self, s, w_ref, i, column, pick):
        wide = 2 * self.half
        for y in range(self.y):
            for c in range(self.c):
                for k in range(wide // LANES):
                    at = (y * self.c + c) * self.dev_cols + column + k * LANES
                    at = pl.ds(pl.multiple_of(at, LANES), LANES)
                    pltpu.make_async_copy(
                        pick(w_ref, at),
                        s["w"].at[i, (y * self.c + c) * (wide // LANES) + k],
                        s["ws"].at[i],
                    ).start()

    def multiply(self, s, i, left):
        w = s["w"]
        pltpu.make_async_copy(w.at[i], w.at[i], s["ws"].at[i]).wait()
        depth = w.shape[2] * 2
        pieces = self.half // LANES
        for y in range(self.y):
            for c in range(self.c):
                for h in range(2):
                    first = ((y * self.c + c) * 2 + h) * pieces
                    right = [
                        w.at[i, first + k].reshape(depth, LANES)[...] for k in range(pieces)
                    ]
                    right = jnp.concatenate(right, axis=1) if pieces > 1 else right[0]
                    got = jnp.dot(left, right, preferred_element_type=jnp.float32)
                    got = got.astype(jnp.bfloat16)
                    got = got.reshape(self.z, self.x, self.rows, self.half)
                    for x in range(self.x):
                        at = (y * self.x + x) if h == 0 else (x * self.y + y)
                        s["b0"][i, c, h, at * self.z : (at + 1) * self.z] = got[:, x]
        start_all(self.copies(s, i, 0))

    def add(self, target, others):
        def piece(k, _):
            total = target[k].astype(jnp.float32)
            for other in others:
                total += other[k].astype(jnp.float32)
            target[k] = total.astype(jnp.bfloat16)
            return 0

        lax.fori_loop(0, target.shape[0], piece, 0, unroll=min(4, target.shape[0]))

    def after_core(self, s, i):
        for copy in self.copies(s, i, 0):
            copy.wait_recv()
        for h in range(2):
            self.add(s["r0"].at[i, h], [s["b0"].at[i, self.mc, h]])
        start_all(self.copies(s, i, 1))

    def after_first(self, s, i):
        for copy in self.copies(s, i, 1):
            copy.wait_recv()
        z = self.z
        for h, name, me, size, count in (
            (0, "r1a", self.my, self.x * z, self.y),
            (1, "r1b", self.mx, self.y * z, self.x),
        ):
            others = [s[name].at[i, k] for k in range(1, count - 1)]
            others.append(s["r0"].at[i, h, pl.ds(me * size, size)])
            self.add(s[name].at[i, 0], others)
        start_all(self.copies(s, i, 2))

    def after_second(self, s, i):
        for copy in self.copies(s, i, 2):
            copy.wait_recv()
        for h, name, came, me, count in (
            (0, "r2a", "r1a", self.mx, self.x),
            (1, "r2b", "r1b", self.my, self.y),
        ):
            for k in range(self.z):
                total = s[came][i, 0, me * self.z + k].astype(jnp.float32)
                for j in range(count - 1):
                    total += s[name][i, j, k].astype(jnp.float32)
                s["b3"][i, k, h] = total.astype(jnp.bfloat16)
        start_all(self.copies(s, i, 3))

    def after_third(self, s, i, store):
        for copy in self.copies(s, i, 3):
            copy.wait_recv()
        for h in range(2):
            total = s["b3"][i, self.mz, h].astype(jnp.float32)
            for k in range(self.z - 1):
                total += s["r3"][i, k, h].astype(jnp.float32)
            store(i, h, total)

    def finish(self, s):
        def one(i, _):
            for stage in range(4):
                for copy in self.copies(s, i, stage):
                    copy.wait_send()
            return 0

        lax.fori_loop(0, self.chunks, one, 0)

    def run(self, s, left_of, store, lags, extras=()):
        n = self.chunks
        stages = (
            (lags[3], lambda i: self.after_third(s, i, store)),
            (lags[2], lambda i: self.after_second(s, i)),
            (lags[1], lambda i: self.after_first(s, i)),
            (lags[0], lambda i: self.after_core(s, i)),
            (0, lambda i: self.multiply(s, i, left_of(i))),
        )

        def step(t, _):
            for lag, work in stages:
                @pl.when((t >= lag) & (t < n + lag))
                def _(lag=lag, work=work):
                    work(t - lag)
            for when, work in extras:
                pl.when(t == when)(work)
            return 0

        lax.fori_loop(0, n + lags[3], step, 0)
        self.finish(s)


def spread(rows, per, pairs):
    count, depth = rows.shape
    lane = lax.broadcasted_iota(jnp.int32, (depth, depth * pairs), 1)
    source = lax.broadcasted_iota(jnp.int32, (depth, depth * pairs), 0)
    parts = []
    for j in range(pairs):
        moves = (lane == source * pairs + j).astype(jnp.bfloat16)
        part = jnp.dot(rows, moves, preferred_element_type=jnp.float32)
        parts.append(part.reshape(count // per, 1, per, depth * pairs))
    wide = jnp.concatenate(parts, axis=1)
    return wide.reshape(count * pairs, depth * pairs).astype(jnp.bfloat16)


def greet(ids):
    barrier = pltpu.get_barrier_semaphore()
    for device in ids:
        pl.semaphore_signal(barrier, inc=1, device_id=device, device_id_type=MESH)
    pl.semaphore_wait(barrier, len(ids))


def device_of(index, tp_count):
    return {"rep": lax.div(index, tp_count), "tp": lax.rem(index, tp_count)}


def greet_all(count, me, tp_count):
    barrier = pltpu.get_barrier_semaphore()

    def one(step, _):
        to = device_of(lax.rem(me + step, count), tp_count)
        pl.semaphore_signal(barrier, inc=1, device_id=to, device_id_type=MESH)
        return 0

    lax.fori_loop(1, count, one, 0)
    pl.semaphore_wait(barrier, count - 1)


def scatter_start(source, target, sems, count, me, tp_count):
    whole = len(source.shape) == len(target.shape) - 1

    def one(step, _):
        to = lax.rem(me + step, count)
        pltpu.make_async_remote_copy(
            src_ref=source if whole else source.at[to],
            dst_ref=target.at[me],
            send_sem=sems.at[0],
            recv_sem=sems.at[1],
            device_id=device_of(to, tp_count),
            device_id_type=MESH,
        ).start()
        return 0

    lax.fori_loop(1, count, one, 0)


def scatter_wait(target, sems, which, count):
    part = target.at[pl.ds(0, count - 1)]
    pltpu.make_async_copy(part, part, sems.at[which]).wait()


def first_kernel(
    red, names, tok_ref, ids_ref, gain_ref, packed_ref, step_ref, sel_ref, w_ref,
    proj_ref, tokall_ref, idsall_ref, packall_ref, stepall_ref, selall_ref, *scratch
):
    s = dict(zip(names, scratch))
    red.place()
    tp_count, rep_count = red.y * red.c, red.z * red.x
    count = tp_count * rep_count
    rep, tp = red.rep, red.tp
    me = rep * tp_count + tp
    inner_dev = red.dev_cols
    for i in range(red.chunks):
        red.fetch(s, w_ref, i, i * 2 * red.half, lambda w, at: w.at[:, :, at])
    tok = tok_ref[...].astype(jnp.float32)
    width = tok.shape[0] * tok.shape[2]
    square = jnp.sum(jnp.sum(tok * tok, axis=0), axis=-1, keepdims=True)
    s["scale"][...] = jnp.broadcast_to(
        lax.rsqrt(square / width + epsilon), s["scale"].shape
    )
    greet_all(count, me, tp_count)
    scatter_start(tok_ref, tokall_ref, s["toks"], count, me, tp_count)
    scatter_start(ids_ref, idsall_ref, s["idss"], count, me, tp_count)
    tokall_ref[me] = tok_ref[me]
    idsall_ref[me] = ids_ref[...]
    peers = [lax.rem(tp + step, tp_count) for step in range(1, tp_count)]
    scale_copies, step_copies = [], []
    for k, to in enumerate(peers):
        scale_copies.append(
            pltpu.make_async_remote_copy(
                src_ref=s["scale"],
                dst_ref=s["scales"].at[tp],
                send_sem=s["scs"].at[0, k],
                recv_sem=s["scs"].at[1, k],
                device_id={"tp": to},
                device_id_type=MESH,
            )
        )
        columns = pl.ds(pl.multiple_of(to * inner_dev, LANES), inner_dev)
        step_copies.append(
            pltpu.make_async_remote_copy(
                src_ref=step_ref.at[:, columns],
                dst_ref=stepall_ref.at[rep, tp],
                send_sem=s["sts"].at[0, k],
                recv_sem=s["sts"].at[1, k],
                device_id={"tp": to},
                device_id_type=MESH,
            )
        )
    start_all(scale_copies)
    s["scales"][tp] = s["scale"][...]
    start_all(step_copies)
    columns = pl.ds(pl.multiple_of(tp * inner_dev, LANES), inner_dev)
    own_step = pltpu.make_async_copy(step_ref.at[:, columns], stepall_ref.at[rep, tp], s["own"].at[0])
    own_sel = pltpu.make_async_copy(sel_ref, selall_ref.at[rep], s["own"].at[1])
    own_step.start()
    own_sel.start()
    to_x = {"rep": red.mz * red.x + lax.rem(red.mx + 1, red.x)}
    slot = lax.rem(me, rep_count)
    home_tp = lax.div(me, rep_count)

    def pack_copy(to_rep):
        return pltpu.make_async_remote_copy(
            src_ref=packed_ref,
            dst_ref=packall_ref.at[slot],
            send_sem=s["pks"].at[0, to_rep],
            recv_sem=s["pks"].at[1, slot],
            device_id={"rep": to_rep, "tp": home_tp},
            device_id_type=MESH,
        )

    def is_me(to_rep):
        return (to_rep == rep) & (home_tp == tp)

    def pack_start(to_rep, _):
        @pl.when(is_me(to_rep))
        def _():
            packall_ref[slot] = packed_ref[...]

        @pl.when(jnp.logical_not(is_me(to_rep)))
        def _():
            pack_copy(to_rep).start()

        return 0

    def relay(ref, sems, source_rep, device, which):
        return pltpu.make_async_remote_copy(
            src_ref=ref.at[source_rep],
            dst_ref=ref.at[source_rep],
            send_sem=sems.at[0, which],
            recv_sem=sems.at[1, which],
            device_id=device,
            device_id_type=MESH,
        )

    z, x, mz, mx = red.z, red.x, red.mz, red.mx

    def up(ref, sems, k, sx, base):
        return relay(ref, sems, (mz - k + 1) * x + sx, {"rep": (mz + 1) * x + mx}, base + k - 1)

    def down(ref, sems, k, sx, base):
        return relay(ref, sems, (mz + k - 1) * x + sx, {"rep": (mz - 1) * x + mx}, base + k - 1)

    def up_came(ref, sems, k, sx, base):
        return relay(ref, sems, (mz - k) * x + sx, to_x, base + k - 1)

    def down_came(ref, sems, k, sx, base):
        return relay(ref, sems, (mz + k) * x + sx, to_x, base + k - 1)

    def round_start(ref, sems, k, columns):
        for n, sx in enumerate(columns):
            base = n * 2 * (z - 1)

            @pl.when((mz - k + 1 >= 0) & (mz + 1 < z))
            def _():
                up(ref, sems, k, sx, base).start()

            @pl.when((mz + k - 1 < z) & (mz - 1 >= 0))
            def _():
                down(ref, sems, k, sx, base + z - 1).start()

    def round_wait(ref, sems, k, columns, sent):
        for n, sx in enumerate(columns):
            base = n * 2 * (z - 1)

            if sent:
                @pl.when((mz - k + 1 >= 0) & (mz + 1 < z))
                def _():
                    up(ref, sems, k, sx, base).wait_send()

                @pl.when((mz + k - 1 < z) & (mz - 1 >= 0))
                def _():
                    down(ref, sems, k, sx, base + z - 1).wait_send()
            else:
                @pl.when(mz - k >= 0)
                def _():
                    up_came(ref, sems, k, sx, base).wait_recv()

                @pl.when(mz + k < z)
                def _():
                    down_came(ref, sems, k, sx, base + z - 1).wait_recv()

    both = list(range(x))
    mine = [mx]
    own_sel.wait()
    sel_x = relay(selall_ref, s["sxs"], rep, to_x, 0)
    sel_x.start()
    lax.fori_loop(0, rep_count, pack_start, 0)

    scatter_wait(tokall_ref, s["toks"], 1, count)
    tok_all = tokall_ref.reshape(count * tok_ref.shape[1], tok_ref.shape[2])[...]
    x_rows = (tok_all.astype(jnp.float32) * gain_ref[...].astype(jnp.float32)).astype(jnp.bfloat16)
    s["left"][...] = spread(x_rows, red.rows // 2, 2)
    for copy in scale_copies:
        copy.wait_recv()
    came = s["scales"].reshape(red.rows // 2, LANES)[:, :1]
    came = jnp.concatenate([came, came], axis=0)

    def store(i, h, total):
        at = pl.multiple_of(i * 2 * red.half + h * red.half, LANES)
        proj_ref[:, pl.ds(at, red.half)] = total * came

    def sel_first():
        relay(selall_ref, s["sxs"], red.mz * red.x + lax.rem(red.mx + 1, red.x), to_x, 0).wait_recv()
        round_start(selall_ref, s["szs"], 1, both)

    def step_first():
        own_step.wait()
        for copy in step_copies:
            copy.wait_recv()
        round_start(stepall_ref, s["tzs"], 1, mine)

    def next_round(ref, sems, k, columns):
        def work():
            round_wait(ref, sems, k - 1, columns, False)
            round_start(ref, sems, k, columns)
        return work

    sel_first()
    step_first()
    n = red.chunks
    extras = []
    lags = (1, 2, 3, 4)
    last = n + lags[3] - 1
    for k in range(2, z):
        extras.append((min(last, 2 * (k - 1)), next_round(stepall_ref, s["tzs"], k, mine)))
        extras.append((min(last, 2 * (k - 1) + 1), next_round(selall_ref, s["szs"], k, both)))
    red.run(s, lambda i: s["left"][...], store, lags, extras)
    round_wait(stepall_ref, s["tzs"], z - 1, mine, False)

    def step_x(source_z):
        return pltpu.make_async_remote_copy(
            src_ref=stepall_ref.at[source_z * x + mx],
            dst_ref=stepall_ref.at[source_z * x + mx],
            send_sem=s["txs"].at[0, source_z],
            recv_sem=s["txs"].at[1, source_z],
            device_id=to_x,
            device_id_type=MESH,
        )

    for k in range(z):
        step_x(k).start()
    round_wait(selall_ref, s["szs"], z - 1, both, False)
    for k in range(1, z):
        round_wait(selall_ref, s["szs"], k, both, True)
        round_wait(stepall_ref, s["tzs"], k, mine, True)
    for k in range(z):
        step_x(k).wait()
    sel_x.wait_send()
    for copy in step_copies + scale_copies:
        copy.wait_send()

    def pack_wait(k, _):
        @pl.when(jnp.logical_not(is_me(k)))
        def _():
            pack_copy(k).wait_send()

        @pl.when(tp * rep_count + k != me)
        def _():
            pltpu.make_async_copy(
                packall_ref.at[k], packall_ref.at[k], s["pks"].at[1, k]
            ).wait()

        return 0

    lax.fori_loop(0, rep_count, pack_wait, 0)
    scatter_wait(idsall_ref, s["idss"], 1, count)
    scatter_wait(idsall_ref, s["idss"], 0, count)
    scatter_wait(tokall_ref, s["toks"], 0, count)


def in_vmem(count):
    return [pl.BlockSpec(memory_space=pltpu.VMEM)] * count


def first_stage(tok, ids, gain, packed, step_proj, sel, w, rep_count, tp_count, inner_dev):
    f32, bf16 = jnp.float32, jnp.bfloat16
    count, tok_dev, slice_dev = tok.shape
    rows = 2 * tok_dev * tp_count
    red = Reduce(rep_count, tp_count, rows, inner_dev, 0)
    red.chunks = red.per
    dma = pltpu.SemaphoreType.DMA
    z, x = red.z, red.x
    scratch = red.scratch(2 * slice_dev)
    scratch.update(
        left=pltpu.VMEM((rep_count * rows, 2 * slice_dev), bf16),
        scale=pltpu.VMEM((tok_dev, LANES), f32),
        scales=pltpu.VMEM((tp_count, tok_dev, LANES), f32),
        toks=dma((2,)),
        idss=dma((2,)),
        scs=dma((2, tp_count - 1)),
        sts=dma((2, tp_count - 1)),
        pks=dma((2, rep_count)),
        own=dma((2,)),
        sxs=dma((2, 1)),
        txs=dma((2, z)),
        szs=dma((2, 2 * x * (z - 1))),
        tzs=dma((2, 2 * (z - 1))),
    )
    shape = jax.ShapeDtypeStruct
    return pl.pallas_call(
        functools.partial(first_kernel, red, tuple(scratch)),
        out_shape=[
            shape((rows, inner_dev), f32),
            shape((count, tok_dev, slice_dev), bf16),
            shape((count,) + ids.shape, bf16),
            shape((rep_count,) + packed.shape, bf16),
            shape((rep_count, tp_count, step_proj.shape[0], inner_dev), bf16),
            shape((rep_count,) + sel.shape, bf16),
        ],
        in_specs=in_vmem(4) + [pl.BlockSpec(memory_space=pl.ANY)] * 3,
        out_specs=in_vmem(6),
        scratch_shapes=list(scratch.values()),
        compiler_params=pltpu.CompilerParams(
            collective_id=0, has_side_effects=True, vmem_limit_bytes=62 * 2**20
        ),
        name="first_stage",
    )(tok, ids, gain, packed, step_proj, sel, w)


def last_kernel(
    red, names, begin, extra, x_ref, home_ref, stat_ref, w_ref, up_ref, *refs
):
    outs = 2 if extra else 0
    s = dict(zip(names, refs[outs:]))
    red.place()
    tp_count, rep_count = red.y * red.c, red.z * red.x
    count = tp_count * rep_count
    rep, tp = red.rep, red.tp
    me = rep * tp_count + tp
    wide = 2 * red.half
    for i in range(red.chunks):
        expert, column = divmod(begin + i, red.per)
        red.fetch(
            s, w_ref, i, column * wide, lambda w, at, expert=expert: w.at[:, expert, :, at]
        )
    for expert in range(x_ref.shape[0]):
        s["left"][expert] = spread(x_ref[expert], red.rows // 2, 2)
    if extra:
        homes_ref, stats_ref = refs[:2]
        greet_all(count, me, tp_count)
    else:
        greet(red.peers())

    def left_of(i):
        return s["left"][lax.div(begin + i, red.per)]

    def store(i, h, total):
        expert = lax.div(begin + i, red.per)
        column = lax.rem(begin + i, red.per) * wide + h * red.half
        up_ref[expert, :, pl.ds(pl.multiple_of(column, LANES), red.half)] = total

    def send_extra():
        scatter_start(home_ref, homes_ref, s["hos"], count, me, tp_count)
        homes_ref[me] = home_ref[me]

        def one(step, _):
            to = lax.rem(me + step, count)
            pltpu.make_async_remote_copy(
                src_ref=stat_ref.at[lax.div(to, tp_count)],
                dst_ref=stats_ref.at[me],
                send_sem=s["sas"].at[0],
                recv_sem=s["sas"].at[1],
                device_id=device_of(to, tp_count),
                device_id_type=MESH,
            ).start()
            return 0

        lax.fori_loop(1, count, one, 0)
        stats_ref[me] = stat_ref[rep]

    extras = [(2, send_extra)] if extra else []
    red.run(s, left_of, store, (1, 3, 5, 7), extras)
    if extra:
        for name, ref in (("hos", homes_ref), ("sas", stats_ref)):
            for which in range(2):
                scatter_wait(ref, s[name], which, count)


def last_stage(slots, home, stat, w, rep_count, tp_count, hidden_dev):
    f32, bf16 = jnp.float32, jnp.bfloat16
    experts, total_rows, slice_dev = slots.shape
    rows = 2 * total_rows // rep_count
    shape = jax.ShapeDtypeStruct
    dma = pltpu.SemaphoreType.DMA
    full = Reduce(rep_count, tp_count, rows, hidden_dev, 0)
    total = full.per * experts
    weights = w.size // experts // full.per * experts * 2 // experts
    most = max(1, ROOM // (full.chunk_bytes() + weights))
    begin, ups = 0, None
    while begin < total:
        red = Reduce(rep_count, tp_count, rows, hidden_dev, min(most, total - begin))
        extra = begin == 0
        scratch = red.scratch(2 * slice_dev)
        scratch["left"] = pltpu.VMEM((experts, rep_count * rows, 2 * slice_dev), bf16)
        outs = [shape((experts, rows, hidden_dev), f32)]
        if extra:
            scratch["hos"] = dma((2,))
            scratch["sas"] = dma((2,))
            count = rep_count * tp_count
            outs += [shape(home.shape, bf16), shape((count,) + stat.shape[1:], f32)]
        got = pl.pallas_call(
            functools.partial(last_kernel, red, tuple(scratch), begin, extra),
            out_shape=outs,
            in_specs=in_vmem(3) + [pl.BlockSpec(memory_space=pl.ANY)],
            out_specs=in_vmem(len(outs)),
            scratch_shapes=list(scratch.values()),
            compiler_params=pltpu.CompilerParams(
                collective_id=10 + begin, has_side_effects=True, vmem_limit_bytes=62 * 2**20
            ),
            name="last_stage",
        )(slots, home, stat, w)
        if extra:
            ups, homes, stats = got
        else:
            edge = begin // full.per
            column = (begin % full.per) * 2 * full.half
            at = lax.broadcasted_iota(jnp.int32, (experts, 1, hidden_dev), 2)
            order = lax.broadcasted_iota(jnp.int32, (experts, 1, hidden_dev), 0)
            older = (order < edge) | ((order == edge) & (at < column))
            ups = jnp.where(older, ups, got[0])
        begin += red.chunks
    return ups, homes, stats


def shards(
    tokens,
    conv_state,
    ssm_state,
    norm_gains,
    conv_weight,
    conv_skip,
    step_bias,
    decay_log,
    input_proj,
    select_proj,
    step_proj,
    output_proj,
    router,
    expert_proj,
    expert_ids,
):
    f32, bf16 = jnp.float32, jnp.bfloat16
    tp_count = lax.axis_size("tp")
    rep_count = lax.axis_size("rep")
    count = tp_count * rep_count
    rep_index = lax.axis_index("rep")
    tok_dev, width = tokens.shape
    slice_dev = width // count
    token_count = tok_dev * count
    req = tok_dev * tp_count
    inner_all = input_proj.shape[2]
    inner_dev = ssm_state.shape[2]
    state_count = ssm_state.shape[1]
    step_rank = step_proj.shape[0] * count
    expert_total = router.shape[1]
    window_count = expert_proj.shape[1]

    pieces = tokens.reshape(tok_dev, count, slice_dev).transpose(1, 0, 2)
    ids = jnp.pad(expert_ids.astype(bf16), ((0, 0), (0, LANES - 2)))
    packed = jnp.concatenate([conv_weight, conv_skip, step_bias[None], decay_log], axis=0)
    packed_rows = packed.shape[0]
    packed = jnp.pad(packed, ((0, -packed_rows % 16), (0, 0)))
    proj, tok_all, ids_all, packed, step_rows, select_rows = first_stage(
        pieces, ids, norm_gains[:1], packed, step_proj, select_proj.T, input_proj,
        rep_count, tp_count, inner_dev,
    )
    conv_input, gate_z = proj[:req], proj[req:]
    tok_slice = tok_all.reshape(token_count, slice_dev).astype(f32)
    ids_all = ids_all.reshape(token_count, LANES)[:, :2].astype(jnp.int32)
    select_rows = select_rows.reshape(-1, inner_dev)
    step_rows = step_rows.reshape(step_rank, inner_dev)
    packed = packed.transpose(1, 0, 2).reshape(-1, inner_dev)[:packed_rows].astype(f32)
    gains = norm_gains.astype(f32)

    window = jnp.arange(window_count, dtype=jnp.int32)
    names_first = ids_all[:, 0:1] == window[None, :]
    names_second = ids_all[:, 1:2] == window[None, :]
    routed = (names_first | names_second).astype(jnp.int32)
    routed = routed.reshape(count, tok_dev, window_count)
    position = jnp.cumsum(routed, axis=1) - routed
    slot_of = (position[..., None] == jnp.arange(CAPACITY, dtype=jnp.int32)) & (
        routed[..., None] > 0
    )
    slot_of = slot_of.astype(f32)
    slot_of, ids_all, tok_slice, packed = lax.optimization_barrier(
        (slot_of, ids_all, tok_slice, packed)
    )

    taps = conv_weight.shape[0]
    conv_taps = packed[:taps]
    skip_rows = packed[taps : taps + 2]
    shift_dev = packed[taps + 2]
    decay_dev = packed[taps + 3 :]
    history = conv_state.astype(f32)
    conv_mix = (
        jnp.sum(conv_taps[:-1, None, :] * history, axis=0)
        + conv_taps[-1] * conv_input
        + skip_rows[0]
    )
    conv_next = jnp.concatenate([conv_state[1:], conv_input.astype(bf16)[None]], axis=0)
    activated = jax.nn.silu(conv_mix)
    select_part = lax.dot_general(
        activated.astype(bf16), select_rows, (((1,), (1,)), ((), ())), preferred_element_type=f32
    )
    selected = jnp.sum(gather(select_part, "tp", 1), axis=0)
    step_low = selected[:, :step_rank].astype(bf16)
    input_map = selected[:, step_rank : step_rank + state_count]
    output_map = selected[:, step_rank + state_count :]
    step_size = jax.nn.softplus(
        jnp.dot(step_low, step_rows, preferred_element_type=f32) + shift_dev
    )
    decay_rate = -jnp.exp(decay_dev)
    factor = jnp.exp(step_size[:, None, :] * decay_rate[None])
    ssm_next = factor * ssm_state + (step_size * activated)[:, None, :] * input_map[:, :, None]
    readout = jnp.sum(ssm_next * output_map[:, :, None], axis=1) + skip_rows[1] * activated
    gated_out = (readout * jax.nn.silu(gate_z)).astype(bf16)

    gated_all = gather(gated_out, "rep", 2).reshape(token_count, inner_dev)
    gated_all = gather(gated_all, "tp", 3)
    gated_all = gated_all.transpose(1, 0, 2).reshape(token_count, inner_all)
    mixer_out = jnp.dot(gated_all, output_proj, preferred_element_type=f32)
    residual = tok_slice + mixer_out
    home = residual.astype(bf16).reshape(count, tok_dev, slice_dev)

    gained = residual * gains[1]
    logit_part = jnp.dot(
        gained, router.astype(f32), preferred_element_type=f32, precision=lax.Precision.HIGHEST
    )
    square_part = jnp.sum(residual * residual, axis=1, keepdims=True)
    stat = jnp.concatenate([logit_part, square_part], axis=1)
    stat = jnp.pad(stat, ((0, 0), (0, LANES - stat.shape[1]))).reshape(rep_count, req, LANES)
    blocks_x = gained.astype(bf16).reshape(count, tok_dev, slice_dev).astype(f32)
    slot_x = jnp.sum(slot_of[..., None] * blocks_x[:, :, None, None, :], axis=1).astype(bf16)
    rows_of = slot_x.transpose(1, 0, 2, 3).reshape(window_count, count * CAPACITY, slice_dev)
    hidden_dev = expert_proj.shape[3] // tp_count
    gate_up, home, stats = last_stage(
        rows_of, home, stat, expert_proj, rep_count, tp_count, hidden_dev
    )
    mamba_out = home.transpose(1, 0, 2).reshape(tok_dev, width)

    summed = jnp.sum(stats, axis=0)
    scale_two = lax.rsqrt(summed[:, expert_total : expert_total + 1] / width + epsilon)
    logits = summed[:, :expert_total] * scale_two
    ids_own = lax.dynamic_slice_in_dim(ids_all, rep_index * req, req, 0)
    choose = (
        ids_own[:, :, None] == jnp.arange(expert_total, dtype=jnp.int32)[None, None, :]
    ).astype(f32)
    picked = jnp.sum(choose * logits[:, None, :], axis=2)
    first_gate = jax.nn.sigmoid(picked[:, 0] - picked[:, 1])
    second_gate = jax.nn.sigmoid(picked[:, 1] - picked[:, 0])
    zero = jnp.zeros((), f32)
    gate_w = jnp.where(ids_own[:, 0:1] == window[None, :], first_gate[:, None], zero) + jnp.where(
        ids_own[:, 1:2] == window[None, :], second_gate[:, None], zero
    )
    slot_own = lax.dynamic_slice_in_dim(slot_of, rep_index * tp_count, tp_count, 0)
    gate_own = jnp.sum(
        slot_own * gate_w.reshape(tp_count, tok_dev, window_count)[..., None], axis=1
    ).astype(bf16).astype(f32)
    scale_own = jnp.sum(slot_own * scale_two.reshape(tp_count, tok_dev, 1, 1), axis=1)
    own = tp_count * CAPACITY
    gate_up = gate_up.reshape(window_count, 2, own, hidden_dev)
    scale_own = scale_own.transpose(1, 0, 2).reshape(window_count, own, 1)
    gate_own = gate_own.transpose(1, 0, 2).reshape(window_count, own, 1)
    hidden = gate_own * jax.nn.silu(gate_up[:, 0] * scale_own) * (gate_up[:, 1] * scale_own)
    hidden = hidden.astype(bf16).reshape(window_count, tp_count, CAPACITY, hidden_dev)
    expert_hidden = hidden.transpose(1, 0, 2, 3).reshape(window_count * own, hidden_dev)
    return (mamba_out, conv_next, ssm_next, expert_hidden)


def solution(mesh):
    in_specs = (
        P(("rep", "tp"), None),
        P(None, "rep", "tp"),
        P("rep", None, "tp"),
        P(None, ("rep", "tp")),
        P(None, ("rep", "tp")),
        P(None, ("rep", "tp")),
        P(("rep", "tp")),
        P(None, ("rep", "tp")),
        P(("rep", "tp"), None, None),
        P("tp", "rep"),
        P(("rep", "tp"), None),
        P(None, ("rep", "tp")),
        P(("rep", "tp"), None),
        P(("rep", "tp"), None, None, None),
        P(("rep", "tp"), None),
    )
    out_specs = (P(("rep", "tp"), None), P(None, "rep", "tp"), P("rep", None, "tp"), P("rep", "tp"))
    return jax.shard_map(shards, mesh=mesh, in_specs=in_specs, out_specs=out_specs, check_vma=False)
```

time: 347 us -> 175 us (0.50)
  Pallas kernels: 212 us -> 140 us
  local copies, waits for them, and re-layouts: 56.9 us -> 17.5 us
  other arithmetic: 33.1 us -> 12.9 us
  matrix products: 15.9 us -> 2.64 us
  starting transfers between devices: 12.2 us -> 0 us
  blocking collectives: 7.95 us -> 0 us
  waiting for transfers between devices: 5.64 us -> 0 us
    pallas_call x9 -> x3, Pallas kernels: 212 us -> 26 us  [send(): pl.pallas_call(functools.partial(send_kernel, tuple(plan)), out_shape=sha...]
    pallas_call x0 -> x2, Pallas kernels: none -> 114 us  [the longest x1 66.6 us: first_stage(): pl.pallas_call(functools.partial(first_kernel, red, tuple(scratch)), out_...]
    reshape x5 -> x2, local copies, waits for them, and re-layouts: 33.5 us -> 1.31 us  [the longest x1 0.68 us: shards(): hidden.transpose(1, 0, 2, 3).reshape(window_count * own, hidden_dev)]
    dot_general x2 -> x0, matrix products: 12.6 us -> none  [the longest x1 8.35 us: shards(): jnp.dot(wide.reshape(pairs * rows, slice_dev * pairs), expert_proj.reshap...]
    all_to_all x2 -> x0, starting transfers between devices: 12.2 us -> none  [the longest x1 7.33 us: shards(): got = lax.all_to_all(sent, both, split_axis=0, concat_axis=0, tiled=True)]
    convert_element_type x14 -> x5, other arithmetic: 14.6 us -> 2.94 us  [the longest x1 1.34 us: shards(): tok_slice = tok_all.reshape(token_count, slice_dev).astype(f32)]
    psum x1 -> x0, blocking collectives: 7.95 us -> none  [shards(): selected = lax.psum(select_part.astype(bf16), 'tp').astype(f32)]
    all_to_all x2 -> x0, waiting for transfers between devices: 5.64 us -> none  [the longest x1 5.63 us: shards(): home = lax.all_to_all(home, both, split_axis=0, concat_axis=0, tiled=True)]
  transfers between devices with their start and end apart: 2 -> 0, of which waited for: 1 -> 0; matrix products, arithmetic and copies ran while one was open for 10% -> 0% of each run, Pallas kernels for 0% -> 0%
where the time goes in v1:
time: 175 us
  Pallas kernels  140 us (80%)
  local copies, waits for them, and re-layouts  17.5 us (10%)
  other arithmetic  12.9 us (7%)
  matrix products  2.64 us (2%)
    pallas_call x1, Pallas kernels, first_stage(): pl.pallas_call(functools.partial(first_kernel, red, tuple(scratch)), out_...  66.6 us
    pallas_call x1, Pallas kernels, last_stage(): pl.pallas_call(functools.partial(last_kernel, red, tuple(scratch), begin,...  47.9 us
    pallas_call x3, Pallas kernels, send(): pl.pallas_call(functools.partial(send_kernel, tuple(plan)), out_shape=sha...  26 us
    dynamic_update_slice x3, local copies, waits for them, and re-layouts, all_of(): lax.dynamic_update_index_in_dim(got, own_piece(*item), lax.axis_index(ite...  4.33 us

profile of v1, /device:TPU:0, one launch (start us, length us, event | category | flops | bytes accessed | tf_op | source)
XLA Modules:
  0.0 174.5 jit_solution(1808601100171091875)
XLA Ops:
  0.6 1.2 bitcast_convert_fusion
  1.9 0.7 convert_element_type.98
  2.6 0.5 pad.12.ids_ref
  3.1 0.7 broadcast_in_dim.62
  3.7 1.3 fusion.15.packed_ref
  5.1 66.6 %first_stage.1 = (f32[16,2048]{1,0:T(8,128)}, bf16[32,2,128]{2,1,0:T(2,128)(2,1)}, bf16[32,2,128]{2,1,0:T(2,128)(2,1)}, bf16[8,32,256]{2,1,0:T(8,128)(2,1)}, bf1...) custom-call(bf16[32,2,128]{2,1,0:T(2,128)(2,1)} %bitcast.80, bf16[2,128]{1,0:T(2,128)(2,1)} %pad.12.ids_ref, ...), custom_call_target="tpu_custom_call" | custom-call | tf_op jit(solution)/shard_map/first_stage/pallas_call | solution.py:676
  71.7 0.9 copy.95
  72.6 0.6 copy-done.11
  73.4 0.1 eq.120
  73.6 1.3 convert.10
  74.9 0.9 slice_convert_fusion
  75.9 0.7 copy.100
  76.7 0.3 reshape.195
  77.0 0.9 slice.94
  77.9 0.9 multiply_reduce_fusion.1
  78.9 1.6 fusion.22
  80.5 0.9 divide_multiply_fusion.1
  81.4 1.1 fusion.8.refs_0_
  82.4 4.1 %shard_map.174 = f32[4,8,288]{2,1,0:T(8,128)} custom-call(f32[8,288]{1,0:T(8,128)} %fusion.8.refs_0_), custom_call_target="tpu_custom_call" | custom-call | tf_op jit(solution)/shard_map/pallas_call | solution.py:69
  86.5 1.3 bitcast_dynamic-update-slice_fusion.2
  87.8 0.8 reduce_sum.82
  88.7 0.3 fusion.24
  89.0 1.5 multiply_reduce_fusion
  90.5 0.6 multiply_convert_fusion.refs_0_
  91.2 9.2 %shard_map.175 = bf16[8,8,2048]{2,1,0:T(8,128)(2,1)} custom-call(bf16[8,2048]{1,0:T(8,128)(2,1)} %multiply_convert_fusion.refs_0_), custom_call_target="tpu_custom_call" | custom-call | tf_op jit(solution)/shard_map/pallas_call | solution.py:69
  100.4 1.4 bitcast_dynamic-update-slice_fusion.1
  101.8 12.7 %shard_map.176 = bf16[4,64,2048]{2,1,0:T(8,128)(2,1)} custom-call(bf16[64,2048]{1,0:T(8,128)(2,1)} %bitcast.61), custom_call_target="tpu_custom_call" | custom-call | tf_op jit(solution)/shard_map/pallas_call | solution.py:69
  114.5 1.7 bitcast_dynamic-update-slice_fusion
  116.2 1.3 copy.99
  117.5 1.2 multiply_reduce_fusion.3
  118.7 0.1 multiply_reduce_fusion.2
  118.8 0.6 copy.83
  119.5 0.1 fusion.10
  119.7 0.6 pad_bitcast_fusion.stat_ref
  120.3 47.9 %last_stage.1 = (f32[2,16,3072]{2,1,0:T(8,128)}, bf16[32,2,128]{2,1,0:T(2,128)(2,1)}, f32[32,8,128]{2,1,0:T(8,128)}) custom-call(bf16[2,64,128]{2,1,0:T(8,128)(2,1)} %bitcast.71, bf16[32,2,128]{2,1,0:T(2,128)(2,1)} %bitcast.75, f32[8,8,128]{2,1,0:T(8,128)} %pad_bitcast_fusion.stat_ref, bf16[128,2,2,12288]{3,2,1,0:T(2,128)(2,1)} %w_ref.3), custom_call_target="tpu_custom_call" | custom-call | tf_op jit(solution)/shard_map/last_stage/pallas_call | solution.py:777
  168.3 0.7 pad_maximum_fusion
  168.9 1.0 fusion.21
  170.0 0.2 copy.97
  170.1 0.9 reduce_sum.86
  171.1 0.2 rsqrt_reduce_fusion
  171.4 0.2 select_reduce_fusion
  171.7 0.1 copy.88
  171.9 0.1 copy.87
  172.1 0.1 copy.86
  172.6 0.2 copy.96
  172.8 0.3 fusion.2
  173.2 0.7 reshape.204
  173.9 0.6 copy.117
  (58 shorter events, 1.7 us)
Async XLA Ops:
  0.6 118.8 %copy-start = (bf16[128,16]{0,1:T(8,128)(2,1)S(1)}, bf16[128,16]{0,1:T(8,128)(2,1)}, u32[]{:S(2)}) copy-start(bf16[128,16]{0,1:T(8,128)(2,1)} %param.27) | copy-start | bytes 12292
  71.7 5.0 %copy-start.2 = (bf16[8,36,2048]{2,1,0:T(8,128)(2,1)S(1)}, bf16[8,36,2048]{2,1,0:T(8,128)(2,1)}, u32[]{:S(2)}) copy-start(bf16[8,36,2048]{2,1,0:T(8,128)(2,1)} %get-tuple-element.24) | copy-start | bytes 3538948
  72.6 0.6 copy-start.11
  76.7 12.0 %copy-start.4 = (bf16[8,4,8,2048]{3,2,1,0:T(8,128)(2,1)S(1)}, bf16[8,4,8,2048]{3,2,1,0:T(8,128)(2,1)}, u32[]{:S(2)}) copy-start(bf16[8,4,8,2048]{3,2,1,0:T(8,128)(2,1)} %get-tuple-element.25) | copy-start | bytes 3145732
  77.0 12.0 %copy-start.5 = (f32[3,8,8,256]{3,1,2,0:T(8,128)S(1)}, f32[3,8,8,256]{3,1,2,0:T(8,128)}, u32[]{:S(2)}) copy-start(f32[3,8,8,256]{3,1,2,0:T(8,128)} %copy.100) | copy-start | bytes 589828
  77.0 12.0 %copy-start.3 = (f32[8,16,2048]{2,1,0:T(8,128)S(1)}, f32[8,16,2048]{2,1,0:T(8,128)}, u32[]{:S(2)}) copy-start(f32[8,16,2048]{2,1,0:T(8,128)} %param.17) | copy-start | bytes 3145732
  82.4 8.1 %copy-start.6 = (f32[16,2048]{1,0:T(8,128)S(1)}, f32[16,2048]{1,0:T(8,128)}, u32[]{:S(2)}) copy-start(f32[16,2048]{1,0:T(8,128)} %get-tuple-element.23) | copy-start | bytes 393220
  82.4 8.1 %copy-start.8 = (f32[1,2048]{1,0:T(1,128)S(1)}, f32[1,2048]{1,0:T(1,128)}, u32[]{:S(2)}) copy-start(f32[1,2048]{1,0:T(1,128)} %get-tuple-element.42) | copy-start | bytes 24580
  91.2 26.3 %copy-start.1 = (bf16[8192,128]{1,0:T(8,128)(2,1)S(1)}, bf16[8192,128]{1,0:T(8,128)(2,1)}, u32[]{:S(2)}) copy-start(bf16[8192,128]{1,0:T(8,128)(2,1)} %param.26) | copy-start | bytes 6291460
  91.2 26.3 %copy-start.7 = (f32[64,128]{1,0:T(8,128)S(1)}, f32[64,128]{1,0:T(8,128)}, u32[]{:S(2)}) copy-start(f32[64,128]{1,0:T(8,128)} %convert.10) | copy-start | bytes 98308
  91.2 26.3 %copy-start.10 = (f32[128]{0:T(128)S(1)}, f32[128]{0:T(128)}, u32[]{:S(2)}) copy-start(f32[128]{0:T(128)} %get-tuple-element.51) | copy-start | bytes 1540
  120.3 47.9 %slice-start = ((bf16[3,8,2048]{2,1,0:T(8,128)(2,1)}), bf16[2,8,2048]{2,1,0:T(8,128)(2,1)S(1)}, s32[]{:S(2)}) async-start(bf16[3,8,2048]{2,1,0:T(8,128)(2,1)} %param.16), calls=%async_computation | async-start | bytes 131072 | tf_op jit(solution)/shard_map/slice | solution.py:876
  120.3 51.0 %copy-start.12 = (s32[64,2]{0,1:T(2,128)S(1)}, s32[64,2]{0,1:T(2,128)}, u32[]{:S(2)}) copy-start(s32[64,2]{0,1:T(2,128)} %copy-done.11) | copy-start | bytes 1540
  168.2 5.7 %copy-start.9 = (bf16[32,2,128]{2,1,0:T(2,128)(2,1)S(1)}, bf16[32,2,128]{2,1,0:T(2,128)(2,1)}, u32[]{:S(2)}) copy-start(bf16[32,2,128]{2,1,0:T(2,128)(2,1)} %get-tuple-element.26) | copy-start | bytes 49156

commit v2 on v1

v2 whole, which is shorter than its diff:
```python
import functools

import jax
import jax.numpy as jnp
from jax import lax
from jax.experimental import pallas as pl
from jax.experimental.pallas import tpu as pltpu
from jax.sharding import PartitionSpec as P

CAPACITY = 2
LANES = 128


epsilon = 1e-05
MESH = pl.DeviceIdType.MESH


CORES = 2
LANE_PAIR = 2
ROOM = 40 * 2**20


def split_of(rep_count, tp_count):
    return rep_count // CORES, CORES, tp_count // CORES, CORES


def start_all(copies):
    for copy in copies:
        copy.start()


class Reduce:
    def __init__(self, rep_count, tp_count, rows, dev_cols, total_chunks):
        self.z, self.x, self.y, self.c = split_of(rep_count, tp_count)
        self.rows = rows
        self.half = 2 * LANES if dev_cols % (4 * LANES) == 0 else LANES
        self.per = dev_cols // (2 * self.half)
        self.dev_cols = dev_cols
        self.chunks = total_chunks
        self.blocks = self.z * self.x * self.y

    def chunk_bytes(self):
        return self.c * 2 * self.blocks * self.rows * self.half * 2 * 2

    def scratch(self, depth):
        n, z, x, y, rows, half = self.chunks, self.z, self.x, self.y, self.rows, self.half
        bf16 = jnp.bfloat16
        groups = self.c * y * 2 * (half // LANES)
        dma = pltpu.SemaphoreType.DMA
        buffers = dict(
            w=pltpu.VMEM((n, groups, depth // 2, 2, LANES), bf16),
            b0=pltpu.VMEM((n, self.c, 2, self.blocks, rows, half), bf16),
            r0=pltpu.VMEM((n, 2, self.blocks, rows, half), bf16),
            r1a=pltpu.VMEM((n, y - 1, x * z, rows, half), bf16),
            r1b=pltpu.VMEM((n, x - 1, y * z, rows, half), bf16),
            r2a=pltpu.VMEM((n, x - 1, z, rows, half), bf16),
            r2b=pltpu.VMEM((n, y - 1, z, rows, half), bf16),
            b3=pltpu.VMEM((n, z, 2, rows, half), bf16),
            r3=pltpu.VMEM((n, z - 1, 2, rows, half), bf16),
            ws=dma((n,)),
            s0=dma((2, n)),
            s1a=dma((2, n, y - 1)),
            s1b=dma((2, n, x - 1)),
            s2a=dma((2, n, x - 1)),
            s2b=dma((2, n, y - 1)),
            s3=dma((2, n, z - 1)),
        )
        return buffers

    def place(self):
        rep, tp = lax.axis_index("rep"), lax.axis_index("tp")
        self.rep, self.tp = rep, tp
        self.mz, self.mx = lax.div(rep, self.x), lax.rem(rep, self.x)
        self.my, self.mc = lax.div(tp, self.c), lax.rem(tp, self.c)

    def peer_z(self, to):
        return {"rep": to * self.x + self.mx}

    def peer_x(self, to):
        return {"rep": self.mz * self.x + to}

    def peer_y(self, to):
        return {"tp": to * self.c + self.mc}

    def peer_c(self):
        return {"tp": self.my * self.c + 1 - self.mc}

    def peers(self):
        out = [self.peer_c()]
        out += [self.peer_y(lax.rem(self.my + s, self.y)) for s in range(1, self.y)]
        out += [self.peer_x(lax.rem(self.mx + s, self.x)) for s in range(1, self.x)]
        out += [self.peer_z(lax.rem(self.mz + s, self.z)) for s in range(1, self.z)]
        return out

    def exchange(self, source, count, me, size, target, sems, i, peer):
        copies = []
        for step in range(1, count):
            to = lax.rem(me + step, count)
            copies.append(
                pltpu.make_async_remote_copy(
                    src_ref=source.at[pl.ds(to * size, size)],
                    dst_ref=target.at[i, step - 1],
                    send_sem=sems.at[0, i, step - 1],
                    recv_sem=sems.at[1, i, step - 1],
                    device_id=peer(to),
                    device_id_type=MESH,
                )
            )
        return copies

    def copies(self, s, i, stage):
        z, x, y = self.z, self.x, self.y
        if stage == 0:
            return [
                pltpu.make_async_remote_copy(
                    src_ref=s["b0"].at[i, 1 - self.mc],
                    dst_ref=s["r0"].at[i],
                    send_sem=s["s0"].at[0, i],
                    recv_sem=s["s0"].at[1, i],
                    device_id=self.peer_c(),
                    device_id_type=MESH,
                )
            ]
        if stage == 1:
            return self.exchange(
                s["r0"].at[i, 0], y, self.my, x * z, s["r1a"], s["s1a"], i, self.peer_y
            ) + self.exchange(
                s["r0"].at[i, 1], x, self.mx, y * z, s["r1b"], s["s1b"], i, self.peer_x
            )
        if stage == 2:
            return self.exchange(
                s["r1a"].at[i, 0], x, self.mx, z, s["r2a"], s["s2a"], i, self.peer_x
            ) + self.exchange(
                s["r1b"].at[i, 0], y, self.my, z, s["r2b"], s["s2b"], i, self.peer_y
            )
        third = []
        for step in range(1, z):
            to = lax.rem(self.mz + step, z)
            third.append(
                pltpu.make_async_remote_copy(
                    src_ref=s["b3"].at[i, to],
                    dst_ref=s["r3"].at[i, step - 1],
                    send_sem=s["s3"].at[0, i, step - 1],
                    recv_sem=s["s3"].at[1, i, step - 1],
                    device_id=self.peer_z(to),
                    device_id_type=MESH,
                )
            )
        return third

    def fetch(self, s, w_ref, i, column, pick):
        wide = 2 * self.half
        for y in range(self.y):
            for c in range(self.c):
                for k in range(wide // LANES):
                    at = (y * self.c + c) * self.dev_cols + column + k * LANES
                    at = pl.ds(pl.multiple_of(at, LANES), LANES)
                    pltpu.make_async_copy(
                        pick(w_ref, at),
                        s["w"].at[i, (y * self.c + c) * (wide // LANES) + k],
                        s["ws"].at[i],
                    ).start()

    def multiply(self, s, i, left):
        w = s["w"]
        pltpu.make_async_copy(w.at[i], w.at[i], s["ws"].at[i]).wait()
        depth = w.shape[2] * 2
        pieces = self.half // LANES
        for y in range(self.y):
            for c in range(self.c):
                for h in range(2):
                    first = ((y * self.c + c) * 2 + h) * pieces
                    right = [
                        w.at[i, first + k].reshape(depth, LANES)[...] for k in range(pieces)
                    ]
                    right = jnp.concatenate(right, axis=1) if pieces > 1 else right[0]
                    got = jnp.dot(left, right, preferred_element_type=jnp.float32)
                    got = got.astype(jnp.bfloat16)
                    got = got.reshape(self.z, self.x, self.rows, self.half)
                    for x in range(self.x):
                        at = (y * self.x + x) if h == 0 else (x * self.y + y)
                        s["b0"][i, c, h, at * self.z : (at + 1) * self.z] = got[:, x]
        start_all(self.copies(s, i, 0))

    def add(self, target, others):
        def piece(k, _):
            total = target[k].astype(jnp.float32)
            for other in others:
                total += other[k].astype(jnp.float32)
            target[k] = total.astype(jnp.bfloat16)
            return 0

        lax.fori_loop(0, target.shape[0], piece, 0, unroll=min(4, target.shape[0]))

    def after_core(self, s, i):
        for copy in self.copies(s, i, 0):
            copy.wait_recv()
        for h in range(2):
            self.add(s["r0"].at[i, h], [s["b0"].at[i, self.mc, h]])
        start_all(self.copies(s, i, 1))

    def after_first(self, s, i):
        for copy in self.copies(s, i, 1):
            copy.wait_recv()
        z = self.z
        for h, name, me, size, count in (
            (0, "r1a", self.my, self.x * z, self.y),
            (1, "r1b", self.mx, self.y * z, self.x),
        ):
            others = [s[name].at[i, k] for k in range(1, count - 1)]
            others.append(s["r0"].at[i, h, pl.ds(me * size, size)])
            self.add(s[name].at[i, 0], others)
        start_all(self.copies(s, i, 2))

    def after_second(self, s, i):
        for copy in self.copies(s, i, 2):
            copy.wait_recv()
        for h, name, came, me, count in (
            (0, "r2a", "r1a", self.mx, self.x),
            (1, "r2b", "r1b", self.my, self.y),
        ):
            for k in range(self.z):
                total = s[came][i, 0, me * self.z + k].astype(jnp.float32)
                for j in range(count - 1):
                    total += s[name][i, j, k].astype(jnp.float32)
                s["b3"][i, k, h] = total.astype(jnp.bfloat16)
        start_all(self.copies(s, i, 3))

    def after_third(self, s, i, store, done):
        for copy in self.copies(s, i, 3):
            copy.wait_recv()
        for h in range(2):
            total = s["b3"][i, self.mz, h].astype(jnp.float32)
            for k in range(self.z - 1):
                total += s["r3"][i, k, h].astype(jnp.float32)
            store(i, h, total)
        done(i)

    def finish(self, s):
        def one(i, _):
            for stage in range(4):
                for copy in self.copies(s, i, stage):
                    copy.wait_send()
            return 0

        lax.fori_loop(0, self.chunks, one, 0)

    def run(self, s, left_of, store, lags, extras=(), done=lambda i: None):
        n = self.chunks
        stages = (
            (lags[3], lambda i: self.after_third(s, i, store, done)),
            (lags[2], lambda i: self.after_second(s, i)),
            (lags[1], lambda i: self.after_first(s, i)),
            (lags[0], lambda i: self.after_core(s, i)),
            (0, lambda i: self.multiply(s, i, left_of(i))),
        )

        def step(t, _):
            for lag, work in stages:
                @pl.when((t >= lag) & (t < n + lag))
                def _(lag=lag, work=work):
                    work(t - lag)
            for when, work in extras:
                pl.when(t == when)(work)
            return 0

        lax.fori_loop(0, n + lags[3], step, 0)
        self.finish(s)


def spread(rows, per, pairs):
    count, depth = rows.shape
    lane = lax.broadcasted_iota(jnp.int32, (depth, depth * pairs), 1)
    source = lax.broadcasted_iota(jnp.int32, (depth, depth * pairs), 0)
    parts = []
    for j in range(pairs):
        moves = (lane == source * pairs + j).astype(jnp.bfloat16)
        part = jnp.dot(rows, moves, preferred_element_type=jnp.float32)
        parts.append(part.reshape(count // per, 1, per, depth * pairs))
    wide = jnp.concatenate(parts, axis=1)
    return wide.reshape(count * pairs, depth * pairs).astype(jnp.bfloat16)


def greet(ids):
    barrier = pltpu.get_barrier_semaphore()
    for device in ids:
        pl.semaphore_signal(barrier, inc=1, device_id=device, device_id_type=MESH)
    pl.semaphore_wait(barrier, len(ids))


def device_of(index, tp_count):
    return {"rep": lax.div(index, tp_count), "tp": lax.rem(index, tp_count)}


def greet_all(count, me, tp_count):
    barrier = pltpu.get_barrier_semaphore()

    def one(step, _):
        to = device_of(lax.rem(me + step, count), tp_count)
        pl.semaphore_signal(barrier, inc=1, device_id=to, device_id_type=MESH)
        return 0

    lax.fori_loop(1, count, one, 0)
    pl.semaphore_wait(barrier, count - 1)


def scatter_start(source, target, sems, count, me, tp_count):
    whole = len(source.shape) == len(target.shape) - 1

    def one(step, _):
        to = lax.rem(me + step, count)
        pltpu.make_async_remote_copy(
            src_ref=source if whole else source.at[to],
            dst_ref=target.at[me],
            send_sem=sems.at[0],
            recv_sem=sems.at[1],
            device_id=device_of(to, tp_count),
            device_id_type=MESH,
        ).start()
        return 0

    lax.fori_loop(1, count, one, 0)


def scatter_wait(target, sems, which, count):
    part = target.at[pl.ds(0, count - 1)]
    pltpu.make_async_copy(part, part, sems.at[which]).wait()


def in_vmem(count):
    return [pl.BlockSpec(memory_space=pltpu.VMEM)] * count


def remote(source, target, send_sem, recv_sem, device):
    return pltpu.make_async_remote_copy(
        src_ref=source,
        dst_ref=target,
        send_sem=send_sem,
        recv_sem=recv_sem,
        device_id=device,
        device_id_type=MESH,
    )


def silu(v):
    return v / (1.0 + jnp.exp(-v))


def softplus(v):
    return jnp.maximum(v, 0.0) + jnp.log1p(jnp.exp(-jnp.abs(v)))


def column_iota(shape, axis):
    return lax.broadcasted_iota(jnp.int32, shape, axis)


def named(ids, lane):
    ids = ids.astype(jnp.float32).astype(jnp.int32)
    return ids[:, :1] == lane, ids[:, 1:2] == lane


def slot_maps(ids, experts, tok_dev):
    rows = ids.shape[0]
    first, second = named(ids, column_iota((rows, LANES), 1))
    routed = (first | second).astype(jnp.float32)
    later, earlier = column_iota((rows, rows), 0), column_iota((rows, rows), 1)
    before = (earlier < later) & (lax.div(earlier, tok_dev) == lax.div(later, tok_dev))
    position = jnp.dot(
        before.astype(jnp.bfloat16), routed.astype(jnp.bfloat16), preferred_element_type=jnp.float32
    )
    slots = rows // tok_dev * CAPACITY
    row, slot = column_iota((rows, slots), 0), column_iota((rows, slots), 1)
    block = lax.div(row, tok_dev) == lax.div(slot, CAPACITY)
    seat = lax.rem(slot, CAPACITY).astype(jnp.float32)
    maps = []
    for e in range(experts):
        taken = block & (routed[:, e : e + 1] > 0.5) & (position[:, e : e + 1] == seat)
        maps.append(taken.astype(jnp.float32))
    return maps


def mixer_kernel(
    red, names, experts,
    tok_ref, ids_ref, gains_ref, packed_ref, sel_ref, history_ref, router_ref,
    step_ref, w_ref, state_ref, out_w_ref,
    next_ref, state_out_ref, home_ref, stat_ref, slots_ref, idsall_ref, *scratch
):
    f32, bf16 = jnp.float32, jnp.bfloat16
    s = dict(zip(names, scratch))
    red.place()
    z, x, y, c = red.z, red.x, red.y, red.c
    mz, mx, my, mc = red.mz, red.mx, red.my, red.mc
    tp_count, rep_count = y * c, z * x
    count = tp_count * rep_count
    rep, tp = red.rep, red.tp
    me = rep * tp_count + tp
    inner_dev = red.dev_cols
    req = red.rows // 2
    tok_dev, slice_dev = tok_ref.shape[1:]
    tokall, packall, stepall = s["tokall"], s["packall"], s["stepall"]
    taps = history_ref.shape[0] + 1
    states = state_ref.shape[1]

    state_in = pltpu.make_async_copy(state_ref, s["state"], s["own"].at[1])
    out_in = pltpu.make_async_copy(out_w_ref, s["outw"], s["own"].at[2])
    for i in range(red.chunks):
        red.fetch(s, w_ref, i, i * 2 * red.half, lambda w, at: w.at[:, :, at])
    columns = pl.ds(pl.multiple_of(tp * inner_dev, LANES), inner_dev)
    own_step = pltpu.make_async_copy(step_ref.at[:, columns], stepall.at[rep, tp], s["own"].at[0])
    own_step.start()
    state_in.start()
    out_in.start()
    tok = tok_ref[...].astype(f32)
    width = tok.shape[0] * tok.shape[2]
    square = jnp.sum(jnp.sum(tok * tok, axis=0), axis=-1, keepdims=True)
    s["scale"][...] = jnp.broadcast_to(lax.rsqrt(square / width + epsilon), s["scale"].shape)
    greet_all(count, me, tp_count)
    scatter_start(tok_ref, tokall, s["toks"], count, me, tp_count)
    tokall[me] = tok_ref[me]
    slot = lax.rem(me, rep_count)
    home_tp = lax.div(me, rep_count)

    def pack_copy(to_rep):
        return remote(
            packed_ref, packall.at[slot], s["pks"].at[0, to_rep], s["pks"].at[1, slot],
            {"rep": to_rep, "tp": home_tp},
        )

    def is_me(to_rep):
        return (to_rep == rep) & (home_tp == tp)

    def pack_start(to_rep, _):
        @pl.when(is_me(to_rep))
        def _():
            packall[slot] = packed_ref[...]

        @pl.when(jnp.logical_not(is_me(to_rep)))
        def _():
            pack_copy(to_rep).start()

        return 0

    lax.fori_loop(0, rep_count, pack_start, 0)
    scale_copies, step_copies = [], []
    for k in range(tp_count - 1):
        to = lax.rem(tp + k + 1, tp_count)
        scale_copies.append(
            remote(
                s["scale"], s["scales"].at[tp], s["scs"].at[0, k], s["scs"].at[1, k], {"tp": to}
            )
        )
        columns = pl.ds(pl.multiple_of(to * inner_dev, LANES), inner_dev)
        step_copies.append(
            remote(
                step_ref.at[:, columns], stepall.at[rep, tp],
                s["sts"].at[0, k], s["sts"].at[1, k], {"tp": to},
            )
        )
    start_all(scale_copies)
    s["scales"][tp] = s["scale"][...]
    start_all(step_copies)
    scatter_start(ids_ref, idsall_ref, s["idss"], count, me, tp_count)
    idsall_ref[me] = ids_ref[...]
    to_x = {"rep": mz * x + lax.rem(mx + 1, x)}

    def relay(source_z, device, which):
        block = stepall.at[source_z * x + mx]
        return remote(block, block, s["tzs"].at[0, which], s["tzs"].at[1, which], device)

    def up(k):
        return relay(mz - k + 1, {"rep": (mz + 1) * x + mx}, k - 1)

    def down(k):
        return relay(mz + k - 1, {"rep": (mz - 1) * x + mx}, z - 1 + k - 1)

    def round_start(k):
        @pl.when((mz - k + 1 >= 0) & (mz + 1 < z))
        def _():
            up(k).start()

        @pl.when((mz + k - 1 < z) & (mz - 1 >= 0))
        def _():
            down(k).start()

    def round_sent(k):
        @pl.when((mz - k + 1 >= 0) & (mz + 1 < z))
        def _():
            up(k).wait_send()

        @pl.when((mz + k - 1 < z) & (mz - 1 >= 0))
        def _():
            down(k).wait_send()

    def step_x(source_z):
        return remote(
            stepall.at[source_z * x + mx], stepall.at[source_z * x + mx],
            s["txs"].at[0, source_z], s["txs"].at[1, source_z], to_x,
        )

    def round_came(k):
        @pl.when(mz - k >= 0)
        def _():
            relay(mz - k, to_x, k - 1).wait_recv()
            step_x(mz - k).start()

        @pl.when(mz + k < z)
        def _():
            relay(mz + k, to_x, z - 1 + k - 1).wait_recv()
            step_x(mz + k).start()

    s["sel"][...] = jnp.zeros(s["sel"].shape, bf16)
    part_cols = sel_ref.shape[0]
    s["sel"][:part_cols] = sel_ref[...]
    s["router"][...] = jnp.zeros(s["router"].shape, f32)
    s["router"][:, : router_ref.shape[1]] = router_ref[...].astype(f32)
    next_ref[: taps - 2] = history_ref[1:]

    scatter_wait(tokall, s["toks"], 1, count)
    tok_all = tokall.reshape(count * tok_dev, slice_dev)
    gain = gains_ref[...].astype(f32)
    x_rows = (tok_all[...].astype(f32) * gain[:1]).astype(bf16)
    s["left"][...] = spread(x_rows, req, 2)

    def step_first():
        own_step.wait()
        for copy in step_copies:
            copy.wait_recv()
        round_start(1)
        step_x(mz).start()

    def params():
        for copy in scale_copies:
            copy.wait_recv()

        def pack_came(k, _):
            @pl.when(tp * rep_count + k != me)
            def _():
                pltpu.make_async_copy(packall.at[k], packall.at[k], s["pks"].at[1, k]).wait()

            return 0

        lax.fori_loop(0, rep_count, pack_came, 0)
        own = packed_ref.shape[1]
        for k in range(rep_count):
            s["par"][:, k * own : (k + 1) * own] = packall[k].astype(f32)

    def maps():
        scatter_wait(idsall_ref, s["idss"], 1, count)
        ids = idsall_ref.reshape(count * tok_dev, LANES)[...]
        for e, taken in enumerate(slot_maps(ids, experts, tok_dev)):
            s["maps"][e] = taken.astype(bf16)

    def next_round(k):
        def work():
            round_came(k - 1)
            round_start(k)

        return work

    def store(i, h, total):
        at = pl.ds(pl.multiple_of(i * 2 * red.half + h * red.half, LANES), red.half)
        scale = s["scales"].reshape(req, LANES)[:, :1]
        conv_input = total[:req] * scale
        s["gate"][:, at] = total[req:] * scale
        next_ref[taps - 2, :, at] = conv_input.astype(bf16)
        par = s["par"]
        mix = par[taps - 1 : taps, at] * conv_input + par[taps : taps + 1, at]
        for k in range(taps - 1):
            mix += par[k : k + 1, at] * history_ref[k, :, at].astype(f32)
        act = silu(mix)
        s["act"][:, at] = act
        s["actall"][rep, :, at] = act.astype(bf16)

    def act_copies(i):
        at = pl.ds(pl.multiple_of(i * 2 * red.half, LANES), 2 * red.half)
        block = s["actall"].at[rep, :, at]
        return [
            remote(
                block, block, s["acs"].at[0, i, k], s["acs"].at[1, i, k],
                {"rep": lax.rem(rep + k + 1, rep_count)},
            )
            for k in range(rep_count - 1)
        ]

    lags = (1, 2, 3, 4)
    last = red.chunks + lags[3] - 1
    extras = [(0, step_first), (1, params), (2, maps)]
    for k in range(2, z):
        extras.append((min(last, 2 * k - 1), next_round(k)))
    red.run(
        s, lambda i: s["left"][...], store, lags, extras, lambda i: start_all(act_copies(i))
    )
    round_came(z - 1)

    def act_came(i, _):
        for copy in act_copies(i):
            copy.wait_recv()
        return 0

    lax.fori_loop(0, red.chunks, act_came, 0)
    every = s["actall"].reshape(rep_count * req, inner_dev)[...]
    part = lax.dot_general(
        every, s["sel"][...], (((1,), (1,)), ((), ())), preferred_element_type=f32
    )
    s["part"][...] = part.astype(bf16).reshape(rep_count, req, LANES)

    def part_start(step, _):
        to = lax.rem(me + step, count)
        remote(
            s["part"].at[lax.div(to, tp_count)], s["parts"].at[me],
            s["pts"].at[0], s["pts"].at[1], device_of(to, tp_count),
        ).start()
        return 0

    lax.fori_loop(1, count, part_start, 0)
    s["parts"][me] = s["part"][rep]
    scatter_wait(s["parts"], s["pts"], 1, count)
    total_cols = part_cols * rep_count
    tiles = [jnp.zeros((req, LANES), f32) for _ in range(-(-total_cols // LANES))]
    lane = column_iota((req, LANES), 1)
    for r in range(rep_count):
        cols = s["parts"][r * tp_count].astype(f32)
        for p in range(1, tp_count):
            cols += s["parts"][r * tp_count + p].astype(f32)
        tile, shift = divmod(r * part_cols, LANES)
        if shift:
            cols = pltpu.roll(cols, shift, 1)
        tiles[tile] += jnp.where(lane >= shift, cols, 0.0)
        if shift + part_cols > LANES:
            tiles[tile + 1] += jnp.where(lane < shift + part_cols - LANES, cols, 0.0)
    rank = total_cols - 2 * states
    low_tiles = rank // LANES
    low = jnp.concatenate(tiles[:low_tiles], axis=1).astype(bf16)
    both_maps = jnp.concatenate(
        [tiles[low_tiles], jnp.zeros((LANES - req, LANES), f32)], axis=0
    ).T
    s["bc"][...] = both_maps
    for k in range(z):
        step_x(k).wait_recv()
    if step_ref.shape[0] % 8 == 0:
        step_rows = stepall.reshape(rank, inner_dev)[...]
    else:
        step_rows = stepall[...].reshape(rank, inner_dev)
    step_pre = jnp.dot(low, step_rows, preferred_element_type=f32)
    s["step"][...] = softplus(step_pre + s["par"][taps + 2 : taps + 3])
    state_in.wait()
    wide = 2 * LANES
    ways = CORES
    piece = inner_dev // ways
    gall = s["gall"]

    def scan_block(b, _):
        at = pl.ds(pl.multiple_of(b * wide, LANES), wide)
        decay = -jnp.exp(s["par"][taps + 3 : taps + 3 + states, at])
        step, act = s["step"][:, at], s["act"][:, at]
        for t in range(req):
            row = step[t : t + 1]
            now = jnp.exp(row * decay) * s["state"][t, :, at]
            now += (row * act[t : t + 1]) * s["bc"][:states, t : t + 1]
            s["state"][t, :, at] = now
            s["read"][t : t + 1, at] = jnp.sum(
                now * s["bc"][states : 2 * states, t : t + 1], axis=0, keepdims=True
            )
        read = s["read"][:, at] + s["par"][taps + 1 : taps + 2, at] * act
        gall[my, mc, mz, mx, :, at] = (read * silu(s["gate"][:, at])).astype(bf16)
        return 0

    def along_z(h):
        at = pl.ds(h * piece, piece)
        block = gall.at[my, mc, mz, mx, :, at]
        return [
            remote(
                block, block, s["gzs"].at[0, h, k], s["gzs"].at[1, h, k],
                red.peer_z(lax.rem(mz + k + 1, z)),
            )
            for k in range(z - 1)
        ]

    def along_xy(h):
        at = pl.ds(h * piece, piece)
        block = gall.at[my, mc, :, mx, :, at]
        out = []
        for k in range(1, x * y):
            dx, dy = k % x, k // x
            device = {
                "rep": mz * x + lax.rem(mx + dx, x),
                "tp": lax.rem(my + dy, y) * c + mc,
            }
            out.append(
                remote(block, block, s["gxs"].at[0, h, k - 1], s["gxs"].at[1, h, k - 1], device)
            )
        return out

    def along_core(h):
        block = gall.at[:, mc, :, :, :, pl.ds(h * piece, piece)]
        return remote(block, block, s["gcs"].at[0, h], s["gcs"].at[1, h], red.peer_c())

    blocks = piece // wide
    for h in range(ways):
        lax.fori_loop(h * blocks, (h + 1) * blocks, scan_block, 0)
        start_all(along_z(h))
    state_out = pltpu.make_async_copy(s["state"], state_out_ref, s["own"].at[3])
    state_out.start()
    for h in range(ways):
        for copy in along_z(h):
            copy.wait_recv()
        start_all(along_xy(h))
    for h in range(ways):
        for copy in along_xy(h):
            copy.wait_recv()
        along_core(h).start()
    out_in.wait()

    def product(core):
        total = jnp.zeros((rep_count * req, slice_dev), f32)
        for k in range(y):
            rows = gall.at[k, core].reshape(rep_count * req, inner_dev)[...]
            at = pl.multiple_of((k * c + core) * inner_dev, LANES)
            total += jnp.dot(rows, s["outw"][pl.ds(at, inner_dev)], preferred_element_type=f32)
        return total

    mixed = product(mc)
    for h in range(ways):
        along_core(h).wait_recv()
    residual = tok_all[...].astype(f32) + mixed + product(1 - mc)
    home_ref.reshape(count * tok_dev, slice_dev)[...] = residual.astype(bf16)
    gained = residual * gain[1:2]
    stat = jnp.dot(
        gained, s["router"][...], preferred_element_type=f32, precision=lax.Precision.HIGHEST
    )
    squares = jnp.sum(residual * residual, axis=1, keepdims=True)
    lane = column_iota(stat.shape, 1)
    stat = jnp.where(lane == router_ref.shape[1], squares, stat)
    stat_ref[...] = stat.reshape(rep_count, req, LANES)
    for e in range(experts):
        slots_ref[e] = lax.dot_general(
            s["maps"][e], gained.astype(bf16), (((0,), (0,)), ((), ())), preferred_element_type=f32
        ).astype(bf16)

    for k in range(1, z):
        round_sent(k)
    for k in range(z):
        step_x(k).wait_send()
    for copy in step_copies + scale_copies:
        copy.wait_send()

    def pack_sent(k, _):
        @pl.when(jnp.logical_not(is_me(k)))
        def _():
            pack_copy(k).wait_send()

        return 0

    lax.fori_loop(0, rep_count, pack_sent, 0)

    def act_sent(i, _):
        for copy in act_copies(i):
            copy.wait_send()
        return 0

    lax.fori_loop(0, red.chunks, act_sent, 0)
    for h in range(ways):
        for copy in along_z(h) + along_xy(h) + [along_core(h)]:
            copy.wait_send()
    scatter_wait(idsall_ref, s["idss"], 0, count)
    scatter_wait(tokall, s["toks"], 0, count)
    scatter_wait(s["parts"], s["pts"], 0, count)
    state_out.wait()


def mixer(args, rep_count, tp_count, experts):
    tok, ids, gains, packed, sel, history, router, step_proj, w, state, out_w = args
    f32, bf16 = jnp.float32, jnp.bfloat16
    count, tok_dev, slice_dev = tok.shape
    req, states, inner_dev = state.shape
    red = Reduce(rep_count, tp_count, 2 * req, inner_dev, 0)
    n = red.chunks = red.per
    dma = pltpu.SemaphoreType.DMA
    vmem = pltpu.VMEM
    z, x, y, c = red.z, red.x, red.y, red.c
    tokens = count * tok_dev
    scratch = red.scratch(2 * slice_dev)
    scratch.update(
        left=vmem((2 * tokens, 2 * slice_dev), bf16),
        scale=vmem((tok_dev, LANES), f32),
        scales=vmem((tp_count, tok_dev, LANES), f32),
        tokall=vmem(tok.shape, bf16),
        packall=vmem((rep_count,) + packed.shape, bf16),
        par=vmem((packed.shape[0], inner_dev), f32),
        stepall=vmem((rep_count, tp_count, step_proj.shape[0], inner_dev), bf16),
        sel=vmem((LANES, inner_dev), bf16),
        router=vmem((slice_dev, LANES), f32),
        maps=vmem((experts, tokens, count * CAPACITY), bf16),
        gate=vmem((req, inner_dev), f32),
        act=vmem((req, inner_dev), f32),
        actall=vmem((rep_count, req, inner_dev), bf16),
        part=vmem((rep_count, req, LANES), bf16),
        parts=vmem((count, req, LANES), bf16),
        bc=vmem((LANES, LANES), f32),
        step=vmem((req, inner_dev), f32),
        read=vmem((req, inner_dev), f32),
        state=vmem(state.shape, f32),
        outw=vmem(out_w.shape, bf16),
        gall=vmem((y, c, z, x, req, inner_dev), bf16),
        toks=dma((2,)),
        idss=dma((2,)),
        pts=dma((2,)),
        scs=dma((2, tp_count - 1)),
        sts=dma((2, tp_count - 1)),
        pks=dma((2, rep_count)),
        own=dma((4,)),
        txs=dma((2, z)),
        tzs=dma((2, 2 * (z - 1))),
        acs=dma((2, n, rep_count - 1)),
        gzs=dma((2, CORES, z - 1)),
        gxs=dma((2, CORES, x * y - 1)),
        gcs=dma((2, CORES)),
    )
    shape = jax.ShapeDtypeStruct
    anywhere = pl.BlockSpec(memory_space=pl.ANY)
    return pl.pallas_call(
        functools.partial(mixer_kernel, red, tuple(scratch), experts),
        out_shape=[
            shape(history.shape, bf16),
            shape(state.shape, f32),
            shape(tok.shape, bf16),
            shape((rep_count, req, LANES), f32),
            shape((experts, count * CAPACITY, slice_dev), bf16),
            shape((count,) + ids.shape, bf16),
        ],
        in_specs=in_vmem(7) + [anywhere] * 4,
        out_specs=in_vmem(1) + [anywhere] + in_vmem(4),
        scratch_shapes=list(scratch.values()),
        compiler_params=pltpu.CompilerParams(
            collective_id=0, has_side_effects=True, vmem_limit_bytes=62 * 2**20
        ),
        name="mixer",
    )(*args)


def last_kernel(
    red, names, begin, extra, experts_all, width, x_ref, home_ref, stat_ref, ids_ref, w_ref, hid_ref, *refs
):
    outs = 1 if extra else 0
    s = dict(zip(names, refs[outs:]))
    red.place()
    tp_count, rep_count = red.y * red.c, red.z * red.x
    count = tp_count * rep_count
    rep, tp = red.rep, red.tp
    me = rep * tp_count + tp
    wide = 2 * red.half
    for i in range(red.chunks):
        expert, column = divmod(begin + i, red.per)
        red.fetch(
            s, w_ref, i, column * wide, lambda w, at, expert=expert: w.at[:, expert, :, at]
        )
    for expert in range(x_ref.shape[0]):
        s["left"][expert] = spread(x_ref[expert], red.rows // 2, 2)
    if extra:
        homes_ref = refs[0]
    greet_all(count, me, tp_count)

    def left_of(i):
        return s["left"][lax.div(begin + i, red.per)]

    req = red.rows // 2
    stats_ref = s["stats"]
    tok_dev = home_ref.shape[1]
    experts = x_ref.shape[0]

    def gates():
        for which in range(2):
            scatter_wait(stats_ref, s["sas"], which, count)
        summed = stats_ref[0]
        for k in range(1, count):
            summed += stats_ref[k]
        tokens = tp_count * tok_dev
        ids = ids_ref[pl.ds(pl.multiple_of(rep * tokens, 8), tokens)]
        lane = lax.broadcasted_iota(jnp.int32, (tokens, LANES), 1)
        first, second = named(ids, lane)
        scale = lax.rsqrt(summed[:, experts_all : experts_all + 1] / width + epsilon)
        logits = summed * scale
        one = jnp.sum(jnp.where(first, logits, 0.0), axis=1, keepdims=True)
        two = jnp.sum(jnp.where(second, logits, 0.0), axis=1, keepdims=True)
        gate = jnp.where(first, 1.0 / (1.0 + jnp.exp(two - one)), 0.0)
        gate += jnp.where(second, 1.0 / (1.0 + jnp.exp(one - two)), 0.0)
        gate = jnp.where(lane == LANES - 1, scale, gate)
        for e, taken in enumerate(slot_maps(ids, experts, tok_dev)):
            row = lax.dot_general(
                taken, gate, (((0,), (0,)), ((), ())), preferred_element_type=jnp.float32,
                precision=lax.Precision.HIGHEST,
            )
            seat = row[:, e : e + 1].astype(jnp.bfloat16).astype(jnp.float32)
            s["seat"][e] = jnp.broadcast_to(seat, s["seat"].shape[1:])
            s["size"][e] = jnp.broadcast_to(row[:, LANES - 1 :], s["size"].shape[1:])

    def store(i, h, total):
        expert = lax.div(begin + i, red.per)
        column = lax.rem(begin + i, red.per) * wide + h * red.half
        size = s["size"][expert][:, :1]
        up = total[req:] * size
        hidden = s["seat"][expert][:, :1] * silu(total[:req] * size) * up
        at = pl.ds(pl.multiple_of(column, LANES), red.half)
        hid_ref[expert, :, at] = hidden.astype(jnp.bfloat16)

    def send_home():
        scatter_start(home_ref, homes_ref, s["hos"], count, me, tp_count)
        homes_ref[me] = home_ref[me]

    def send_stats():

        def one(step, _):
            to = lax.rem(me + step, count)
            pltpu.make_async_remote_copy(
                src_ref=stat_ref.at[lax.div(to, tp_count)],
                dst_ref=stats_ref.at[me],
                send_sem=s["sas"].at[0],
                recv_sem=s["sas"].at[1],
                device_id=device_of(to, tp_count),
                device_id_type=MESH,
            ).start()
            return 0

        lax.fori_loop(1, count, one, 0)
        stats_ref[me] = stat_ref[rep]

    lags = (1, 3, 5, 7)
    extras = [(0, send_stats), (lags[3] - 1, gates)]
    if extra:
        extras.append((2, send_home))
    red.run(s, left_of, store, lags, extras)
    if extra:
        for which in range(2):
            scatter_wait(homes_ref, s["hos"], which, count)


def last_stage(slots, home, stat, ids, w, experts_all, width, rep_count, tp_count, hidden_dev):
    f32, bf16 = jnp.float32, jnp.bfloat16
    experts, total_rows, slice_dev = slots.shape
    rows = 2 * total_rows // rep_count
    shape = jax.ShapeDtypeStruct
    dma = pltpu.SemaphoreType.DMA
    full = Reduce(rep_count, tp_count, rows, hidden_dev, 0)
    total = full.per * experts
    weights = w.size // experts // full.per * experts * 2 // experts
    most = max(1, ROOM // (full.chunk_bytes() + weights))
    begin, ups = 0, None
    while begin < total:
        red = Reduce(rep_count, tp_count, rows, hidden_dev, min(most, total - begin))
        extra = begin == 0
        scratch = red.scratch(2 * slice_dev)
        scratch["left"] = pltpu.VMEM((experts, rep_count * rows, 2 * slice_dev), bf16)
        scratch["sas"] = dma((2,))
        scratch["stats"] = pltpu.VMEM((rep_count * tp_count,) + stat.shape[1:], f32)
        scratch["seat"] = pltpu.VMEM((experts, rows // 2, LANES), f32)
        scratch["size"] = pltpu.VMEM((experts, rows // 2, LANES), f32)
        outs = [shape((experts, rows // 2, hidden_dev), bf16)]
        if extra:
            scratch["hos"] = dma((2,))
            outs += [shape(home.shape, bf16)]
        got = pl.pallas_call(
            functools.partial(last_kernel, red, tuple(scratch), begin, extra, experts_all, width),
            out_shape=outs,
            in_specs=in_vmem(4) + [pl.BlockSpec(memory_space=pl.ANY)],
            out_specs=in_vmem(len(outs)),
            scratch_shapes=list(scratch.values()),
            compiler_params=pltpu.CompilerParams(
                collective_id=10 + begin, has_side_effects=True, vmem_limit_bytes=62 * 2**20
            ),
            name="last_stage",
        )(slots, home, stat, ids, w)
        if extra:
            ups, homes = got
        else:
            edge = begin // full.per
            column = (begin % full.per) * 2 * full.half
            at = lax.broadcasted_iota(jnp.int32, (experts, 1, hidden_dev), 2)
            order = lax.broadcasted_iota(jnp.int32, (experts, 1, hidden_dev), 0)
            older = (order < edge) | ((order == edge) & (at < column))
            ups = jnp.where(older, ups, got[0])
        begin += red.chunks
    return ups, homes


def shards(
    tokens,
    conv_state,
    ssm_state,
    norm_gains,
    conv_weight,
    conv_skip,
    step_bias,
    decay_log,
    input_proj,
    select_proj,
    step_proj,
    output_proj,
    router,
    expert_proj,
    expert_ids,
):
    bf16 = jnp.bfloat16
    tp_count = lax.axis_size("tp")
    rep_count = lax.axis_size("rep")
    count = tp_count * rep_count
    tok_dev, width = tokens.shape
    slice_dev = width // count
    experts = expert_proj.shape[1]
    hidden_dev = expert_proj.shape[3] // tp_count

    pieces = tokens.reshape(tok_dev, count, slice_dev).transpose(1, 0, 2)
    ids = jnp.pad(expert_ids.astype(bf16), ((0, 0), (0, LANES - 2)))
    packed = jnp.concatenate([conv_weight, conv_skip, step_bias[None], decay_log], axis=0)
    packed = jnp.pad(packed, ((0, -packed.shape[0] % 16), (0, 0)))
    args = (
        pieces, ids, norm_gains, packed, select_proj.T, conv_state, router,
        step_proj, input_proj, ssm_state, output_proj,
    )
    conv_next, ssm_next, home, stat, slots, ids = mixer(args, rep_count, tp_count, experts)
    hidden, home = last_stage(
        slots, home, stat, ids.reshape(count * tok_dev, LANES), expert_proj,
        router.shape[1], width, rep_count, tp_count, hidden_dev,
    )
    mamba_out = home.transpose(1, 0, 2).reshape(tok_dev, width)
    hidden = hidden.reshape(experts, tp_count, CAPACITY, hidden_dev).transpose(1, 0, 2, 3)
    expert_hidden = hidden.reshape(experts * tp_count * CAPACITY, hidden_dev)
    return (mamba_out, conv_next, ssm_next, expert_hidden)


def solution(mesh):
    in_specs = (
        P(("rep", "tp"), None),
        P(None, "rep", "tp"),
        P("rep", None, "tp"),
        P(None, ("rep", "tp")),
        P(None, ("rep", "tp")),
        P(None, ("rep", "tp")),
        P(("rep", "tp")),
        P(None, ("rep", "tp")),
        P(("rep", "tp"), None, None),
        P("tp", "rep"),
        P(("rep", "tp"), None),
        P(None, ("rep", "tp")),
        P(("rep", "tp"), None),
        P(("rep", "tp"), None, None, None),
        P(("rep", "tp"), None),
    )
    out_specs = (P(("rep", "tp"), None), P(None, "rep", "tp"), P("rep", None, "tp"), P("rep", "tp"))
    return jax.shard_map(shards, mesh=mesh, in_specs=in_specs, out_specs=out_specs, check_vma=False)
```

time: 175 us -> 124 us (0.71)
  Pallas kernels: 140 us -> 114 us
  other arithmetic: 12.9 us -> 2.02 us
  local copies, waits for them, and re-layouts: 17.5 us -> 7.21 us
  matrix products: 2.64 us -> 0 us
    pallas_call x4 -> x1, Pallas kernels: 92.6 us -> 68.1 us  [mixer(): pl.pallas_call(functools.partial(mixer_kernel, red, tuple(scratch), exper...]
    reduce_sum x7 -> x0, other arithmetic: 4.53 us -> none  [the longest x1 1.5 us: shards(): jnp.sum(ssm_next * output_map[:, :, None], axis=1)]
    dynamic_update_slice x3 -> x0, local copies, waits for them, and re-layouts: 4.33 us -> none  [all_of(): lax.dynamic_update_index_in_dim(got, own_piece(*item), lax.axis_index(ite...]
    slice x8 -> x0, local copies, waits for them, and re-layouts: 3.73 us -> none  [the longest x1 1.62 us: shards(): skip_rows[1] * activated]
    convert_element_type x6 -> x0, other arithmetic: 2.91 us -> none  [the longest x1 1.34 us: shards(): tok_slice = tok_all.reshape(token_count, slice_dev).astype(f32)]
    dot_general x4 -> x0, matrix products: 2.64 us -> none  [the longest x1 1.21 us: shards(): mixer_out = jnp.dot(gated_all, output_proj, preferred_element_type=f32)]
    pallas_call x1, Pallas kernels: 47.9 us -> 45.5 us  [last_stage(): pl.pallas_call(functools.partial(last_kernel, red, tuple(scratch), begin,...]
    mul x3 -> x0, other arithmetic: 2.2 us -> none  [the longest x1 1.24 us: shards(): gained = residual * gains[1]]
where the time goes in v2:
time: 124 us; the launch traced here: 123 us
  Pallas kernels  114 us (92%)
  local copies, waits for them, and re-layouts  7.21 us (6%)
  other arithmetic  2.02 us (2%)
    pallas_call x1, Pallas kernels, mixer(): pl.pallas_call(functools.partial(mixer_kernel, red, tuple(scratch), exper...  68.1 us
    pallas_call x1, Pallas kernels, last_stage(): pl.pallas_call(functools.partial(last_kernel, red, tuple(scratch), begin,...  45.5 us
    unnamed x8, local copies, waits for them, and re-layouts  4.35 us

profile of v2, /device:TPU:0, one launch (start us, length us, event | category | flops | bytes accessed | tf_op | source)
XLA Modules:
  0.0 123.5 jit_solution(1819933883413485441)
XLA Ops:
  0.6 0.7 convert_element_type.7
  1.3 0.5 pad.8.ids_ref
  1.8 0.7 broadcast_in_dim.3
  2.5 1.3 %fusion.6.packed_ref = bf16[32,256]{1,0:T(8,128)(2,1)} fusion(bf16[16,256]{1,0:T(8,128)(2,1)} %param.22, bf16[1,256]{1,0:T(2,128)(2,1)S(1)} %broadcast_in_dim.3, bf16[2,256]{1,0:T(2,128)(2,1)} %param.20, bf16[4,256]{1,0:T(4,128)(2,1)} %param.19), kind=kLoop, calls=%fused_computation.7 | loop fusion | flops 106496 | bytes 28160 | tf_op jit(solution)/shard_map/concatenate | solution.py:1013
  3.8 1.4 %copy.19.router_ref = bf16[128,16]{1,0:T(8,128)(2,1)} copy(bf16[128,16]{0,1:T(8,128)(2,1)} %param.27) | data formatting | bytes 8192 | tf_op args[12]
  5.2 68.1 %mixer.1 = (bf16[3,8,2048]{2,1,0:T(8,128)(2,1)}, f32[8,16,2048]{2,1,0:T(8,128)}, bf16[32,2,128]{2,1,0:T(2,128)(2,1)}, f32[8,8,128]{2,1,0:T(8,128)}, bf16[2,64,12...) custom-call(bf16[32,2,128]{2,1,0:T(2,128)(2,1)} %bitcast.11, bf16[2,128]{1,0:T(2,128)(2,1)} %pad.8.ids_ref, ...), custom_call_target="tpu_custom_call" | custom-call | tf_op jit(solution)/shard_map/mixer/pallas_call | solution.py:821
  73.3 0.0 copy-start.1
  73.3 0.0 copy-start
  73.3 45.5 %last_stage.1 = (bf16[2,8,3072]{2,1,0:T(8,128)(2,1)}, bf16[32,2,128]{2,1,0:T(2,128)(2,1)}) custom-call(bf16[2,64,128]{2,1,0:T(8,128)(2,1)} %get-tuple-element.12.x_ref, bf16[32,2,128]{2,1,0:T(2,128)(2,1)} %get-tuple-element.13.home_ref, f32[8,8,128]{2,1,0:T(8,128)} %get-tuple-element.14.stat_ref, bf16[64,128]{1,0:T(8,128)(2,1)} %bitcast.12, ...), custom_call_target="tpu_custom_call" | custom-call | tf_op jit(solution)/shard_map/last_stage/pallas_call | solution.py:961
  118.9 0.9 reshape.26
  119.8 0.1 copy.20
  119.9 0.7 reshape.27
  120.5 1.3 %copy.24 = bf16[2,4096]{1,0:T(2,128)(2,1)} copy(bf16[2,4096]{1,0:T(2,128)(2,1)} %bitcast.13) | data formatting | bytes 32768
  121.9 0.0 copy-done.1
  121.9 0.6 copy.25
  122.5 0.0 copy-done
  122.5 1.0 copy.26
Async XLA Ops:
  73.3 48.6 %copy-start.1 = (bf16[3,8,2048]{2,1,0:T(8,128)(2,1)S(1)}, bf16[3,8,2048]{2,1,0:T(8,128)(2,1)}, u32[]{:S(2)}) copy-start(bf16[3,8,2048]{2,1,0:T(8,128)(2,1)} %get-tuple-element.25) | copy-start | bytes 294916
  73.3 49.2 %copy-start = (f32[8,16,2048]{2,1,0:T(8,128)S(1)}, f32[8,16,2048]{2,1,0:T(8,128)}, u32[]{:S(2)}) copy-start(f32[8,16,2048]{2,1,0:T(8,128)} %get-tuple-element.26) | copy-start | bytes 3145732

commit v3 on v2

--- a/solution.py
+++ b/solution.py
@@ -381,7 +381,8 @@
 
 def mixer_kernel(
     red, names, experts,
-    tok_ref, ids_ref, gains_ref, packed_ref, sel_ref, history_ref, router_ref,
+    tok_in_ref, ids_in_ref, gains_ref, weight_ref, skip_ref, bias_ref, decay_ref, sel_ref,
+    history_ref, router_ref,
     step_ref, w_ref, state_ref, out_w_ref,
     next_ref, state_out_ref, home_ref, stat_ref, slots_ref, idsall_ref, *scratch
 ):
@@ -396,10 +397,11 @@
     me = rep * tp_count + tp
     inner_dev = red.dev_cols
     req = red.rows // 2
+    tok_ref, ids_ref, packed_ref = s["tok"], s["ids"], s["packed"]
     tok_dev, slice_dev = tok_ref.shape[1:]
     tokall, packall, stepall = s["tokall"], s["packall"], s["stepall"]
     taps = history_ref.shape[0] + 1
-    states = state_ref.shape[1]
+    states = tap0 = state_ref.shape[1]
 
     state_in = pltpu.make_async_copy(state_ref, s["state"], s["own"].at[1])
     out_in = pltpu.make_async_copy(out_w_ref, s["outw"], s["own"].at[2])
@@ -410,9 +412,18 @@
     own_step.start()
     state_in.start()
     out_in.start()
-    tok = tok_ref[...].astype(f32)
-    width = tok.shape[0] * tok.shape[2]
-    square = jnp.sum(jnp.sum(tok * tok, axis=0), axis=-1, keepdims=True)
+    for k in range(count):
+        tok_ref[k] = tok_in_ref[:, k * slice_dev : (k + 1) * slice_dev]
+    ids = ids_in_ref[...].astype(f32)
+    ids = jnp.concatenate([ids, jnp.zeros((tok_dev, LANES - ids.shape[1]), f32)], axis=1)
+    ids_ref[...] = ids.astype(bf16)
+    rows = [ref[...].astype(f32) for ref in (decay_ref, weight_ref, skip_ref, bias_ref)]
+    spare = packed_ref.shape[0] - sum(row.shape[0] for row in rows)
+    rows.append(jnp.zeros((spare, packed_ref.shape[1]), f32))
+    packed_ref[...] = jnp.concatenate(rows, axis=0).astype(bf16)
+    tok = tok_in_ref[...].astype(f32)
+    width = tok.shape[1]
+    square = jnp.sum(tok * tok, axis=-1, keepdims=True)
     s["scale"][...] = jnp.broadcast_to(lax.rsqrt(square / width + epsilon), s["scale"].shape)
     greet_all(count, me, tp_count)
     scatter_start(tok_ref, tokall, s["toks"], count, me, tp_count)
@@ -463,56 +474,21 @@
     idsall_ref[me] = ids_ref[...]
     to_x = {"rep": mz * x + lax.rem(mx + 1, x)}
 
-    def relay(source_z, device, which):
+    def step_z(k):
+        block = stepall.at[rep]
+        return remote(
+            block, block, s["tzs"].at[0, k], s["tzs"].at[1, k], red.peer_z(lax.rem(mz + k + 1, z))
+        )
+
+    def step_x(source_z):
         block = stepall.at[source_z * x + mx]
-        return remote(block, block, s["tzs"].at[0, which], s["tzs"].at[1, which], device)
-
-    def up(k):
-        return relay(mz - k + 1, {"rep": (mz + 1) * x + mx}, k - 1)
-
-    def down(k):
-        return relay(mz + k - 1, {"rep": (mz - 1) * x + mx}, z - 1 + k - 1)
-
-    def round_start(k):
-        @pl.when((mz - k + 1 >= 0) & (mz + 1 < z))
-        def _():
-            up(k).start()
-
-        @pl.when((mz + k - 1 < z) & (mz - 1 >= 0))
-        def _():
-            down(k).start()
-
-    def round_sent(k):
-        @pl.when((mz - k + 1 >= 0) & (mz + 1 < z))
-        def _():
-            up(k).wait_send()
-
-        @pl.when((mz + k - 1 < z) & (mz - 1 >= 0))
-        def _():
-            down(k).wait_send()
-
-    def step_x(source_z):
-        return remote(
-            stepall.at[source_z * x + mx], stepall.at[source_z * x + mx],
-            s["txs"].at[0, source_z], s["txs"].at[1, source_z], to_x,
-        )
-
-    def round_came(k):
-        @pl.when(mz - k >= 0)
-        def _():
-            relay(mz - k, to_x, k - 1).wait_recv()
-            step_x(mz - k).start()
-
-        @pl.when(mz + k < z)
-        def _():
-            relay(mz + k, to_x, z - 1 + k - 1).wait_recv()
-            step_x(mz + k).start()
+        return remote(block, block, s["txs"].at[0, source_z], s["txs"].at[1, source_z], to_x)
 
     s["sel"][...] = jnp.zeros(s["sel"].shape, bf16)
     part_cols = sel_ref.shape[0]
     s["sel"][:part_cols] = sel_ref[...]
     s["router"][...] = jnp.zeros(s["router"].shape, f32)
-    s["router"][:, : router_ref.shape[1]] = router_ref[...].astype(f32)
+    s["router"][: router_ref.shape[0]] = router_ref[...].astype(f32)
     next_ref[: taps - 2] = history_ref[1:]
 
     scatter_wait(tokall, s["toks"], 1, count)
@@ -525,8 +501,14 @@
         own_step.wait()
         for copy in step_copies:
             copy.wait_recv()
-        round_start(1)
-        step_x(mz).start()
+        for k in range(z - 1):
+            step_z(k).start()
+
+    def step_second():
+        for k in range(z - 1):
+            step_z(k).wait_recv()
+        for k in range(z // 2):
+            step_x(k).start()
 
     def params():
         for copy in scale_copies:
@@ -549,13 +531,6 @@
         ids = idsall_ref.reshape(count * tok_dev, LANES)[...]
         for e, taken in enumerate(slot_maps(ids, experts, tok_dev)):
             s["maps"][e] = taken.astype(bf16)
-
-    def next_round(k):
-        def work():
-            round_came(k - 1)
-            round_start(k)
-
-        return work
 
     def store(i, h, total):
         at = pl.ds(pl.multiple_of(i * 2 * red.half + h * red.half, LANES), red.half)
@@ -564,9 +539,10 @@
         s["gate"][:, at] = total[req:] * scale
         next_ref[taps - 2, :, at] = conv_input.astype(bf16)
         par = s["par"]
-        mix = par[taps - 1 : taps, at] * conv_input + par[taps : taps + 1, at]
+        mix = par[tap0 + taps - 1 : tap0 + taps, at] * conv_input
+        mix += par[tap0 + taps : tap0 + taps + 1, at]
         for k in range(taps - 1):
-            mix += par[k : k + 1, at] * history_ref[k, :, at].astype(f32)
+            mix += par[tap0 + k : tap0 + k + 1, at] * history_ref[k, :, at].astype(f32)
         act = silu(mix)
         s["act"][:, at] = act
         s["actall"][rep, :, at] = act.astype(bf16)
@@ -582,15 +558,14 @@
             for k in range(rep_count - 1)
         ]
 
-    lags = (1, 2, 3, 4)
-    last = red.chunks + lags[3] - 1
-    extras = [(0, step_first), (1, params), (2, maps)]
-    for k in range(2, z):
-        extras.append((min(last, 2 * k - 1), next_round(k)))
+    n = red.chunks
+    lags = (1, n, n + 2, n + 4)
+    extras = [(1, step_first), (2, params), (2, maps), (2 * n + 1, step_second)]
     red.run(
         s, lambda i: s["left"][...], store, lags, extras, lambda i: start_all(act_copies(i))
     )
-    round_came(z - 1)
+    for k in range(z // 2, z):
+        step_x(k).start()
 
     def act_came(i, _):
         for copy in act_copies(i):
@@ -642,7 +617,7 @@
     else:
         step_rows = stepall[...].reshape(rank, inner_dev)
     step_pre = jnp.dot(low, step_rows, preferred_element_type=f32)
-    s["step"][...] = softplus(step_pre + s["par"][taps + 2 : taps + 3])
+    s["step"][...] = softplus(step_pre + s["par"][tap0 + taps + 2 : tap0 + taps + 3])
     state_in.wait()
     wide = 2 * LANES
     ways = CORES
@@ -651,7 +626,7 @@
 
     def scan_block(b, _):
         at = pl.ds(pl.multiple_of(b * wide, LANES), wide)
-        decay = -jnp.exp(s["par"][taps + 3 : taps + 3 + states, at])
+        decay = -jnp.exp(s["par"][:states, at])
         step, act = s["step"][:, at], s["act"][:, at]
         for t in range(req):
             row = step[t : t + 1]
@@ -661,7 +636,7 @@
             s["read"][t : t + 1, at] = jnp.sum(
                 now * s["bc"][states : 2 * states, t : t + 1], axis=0, keepdims=True
             )
-        read = s["read"][:, at] + s["par"][taps + 1 : taps + 2, at] * act
+        read = s["read"][:, at] + s["par"][tap0 + taps + 1 : tap0 + taps + 2, at] * act
         gall[my, mc, mz, mx, :, at] = (read * silu(s["gate"][:, at])).astype(bf16)
         return 0
 
@@ -725,20 +700,21 @@
     residual = tok_all[...].astype(f32) + mixed + product(1 - mc)
     home_ref.reshape(count * tok_dev, slice_dev)[...] = residual.astype(bf16)
     gained = residual * gain[1:2]
-    stat = jnp.dot(
-        gained, s["router"][...], preferred_element_type=f32, precision=lax.Precision.HIGHEST
+    stat = lax.dot_general(
+        gained, s["router"][...], (((1,), (1,)), ((), ())), preferred_element_type=f32,
+        precision=lax.Precision.HIGHEST,
     )
     squares = jnp.sum(residual * residual, axis=1, keepdims=True)
     lane = column_iota(stat.shape, 1)
-    stat = jnp.where(lane == router_ref.shape[1], squares, stat)
+    stat = jnp.where(lane == router_ref.shape[0], squares, stat)
     stat_ref[...] = stat.reshape(rep_count, req, LANES)
     for e in range(experts):
         slots_ref[e] = lax.dot_general(
             s["maps"][e], gained.astype(bf16), (((0,), (0,)), ((), ())), preferred_element_type=f32
         ).astype(bf16)
 
-    for k in range(1, z):
-        round_sent(k)
+    for k in range(z - 1):
+        step_z(k).wait_send()
     for k in range(z):
         step_x(k).wait_send()
     for copy in step_copies + scale_copies:
@@ -769,9 +745,15 @@
 
 
 def mixer(args, rep_count, tp_count, experts):
-    tok, ids, gains, packed, sel, history, router, step_proj, w, state, out_w = args
+    tok, ids, gains, weight, skip, bias, decay, sel, history, router = args[:-4]
+    step_proj, w, state, out_w = args[-4:]
     f32, bf16 = jnp.float32, jnp.bfloat16
-    count, tok_dev, slice_dev = tok.shape
+    count = rep_count * tp_count
+    tok_dev = tok.shape[0]
+    slice_dev = tok.shape[1] // count
+    pieces = (count, tok_dev, slice_dev)
+    packed_rows = weight.shape[0] + skip.shape[0] + bias.shape[0] + decay.shape[0]
+    packed = (packed_rows + -packed_rows % 16, decay.shape[1])
     req, states, inner_dev = state.shape
     red = Reduce(rep_count, tp_count, 2 * req, inner_dev, 0)
     n = red.chunks = red.per
@@ -784,12 +766,15 @@
         left=vmem((2 * tokens, 2 * slice_dev), bf16),
         scale=vmem((tok_dev, LANES), f32),
         scales=vmem((tp_count, tok_dev, LANES), f32),
-        tokall=vmem(tok.shape, bf16),
-        packall=vmem((rep_count,) + packed.shape, bf16),
-        par=vmem((packed.shape[0], inner_dev), f32),
+        tok=vmem(pieces, bf16),
+        ids=vmem((tok_dev, LANES), bf16),
+        packed=vmem(packed, bf16),
+        tokall=vmem(pieces, bf16),
+        packall=vmem((rep_count,) + packed, bf16),
+        par=vmem((packed[0], inner_dev), f32),
         stepall=vmem((rep_count, tp_count, step_proj.shape[0], inner_dev), bf16),
         sel=vmem((LANES, inner_dev), bf16),
-        router=vmem((slice_dev, LANES), f32),
+        router=vmem((LANES, slice_dev), f32),
         maps=vmem((experts, tokens, count * CAPACITY), bf16),
         gate=vmem((req, inner_dev), f32),
         act=vmem((req, inner_dev), f32),
@@ -810,7 +795,7 @@
         pks=dma((2, rep_count)),
         own=dma((4,)),
         txs=dma((2, z)),
-        tzs=dma((2, 2 * (z - 1))),
+        tzs=dma((2, z - 1)),
         acs=dma((2, n, rep_count - 1)),
         gzs=dma((2, CORES, z - 1)),
         gxs=dma((2, CORES, x * y - 1)),
@@ -823,12 +808,12 @@
         out_shape=[
             shape(history.shape, bf16),
             shape(state.shape, f32),
-            shape(tok.shape, bf16),
+            shape(pieces, bf16),
             shape((rep_count, req, LANES), f32),
             shape((experts, count * CAPACITY, slice_dev), bf16),
-            shape((count,) + ids.shape, bf16),
+            shape((count, tok_dev, LANES), bf16),
         ],
-        in_specs=in_vmem(7) + [anywhere] * 4,
+        in_specs=in_vmem(10) + [anywhere] * 4,
         out_specs=in_vmem(1) + [anywhere] + in_vmem(4),
         scratch_shapes=list(scratch.values()),
         compiler_params=pltpu.CompilerParams(
@@ -857,7 +842,7 @@
     for expert in range(x_ref.shape[0]):
         s["left"][expert] = spread(x_ref[expert], red.rows // 2, 2)
     if extra:
-        homes_ref = refs[0]
+        mamba_ref, homes_ref = refs[0], s["homes"]
     greet_all(count, me, tp_count)
 
     def left_of(i):
@@ -924,7 +909,7 @@
         lax.fori_loop(1, count, one, 0)
         stats_ref[me] = stat_ref[rep]
 
-    lags = (1, 3, 5, 7)
+    lags = (2, 4, 6, 8)
     extras = [(0, send_stats), (lags[3] - 1, gates)]
     if extra:
         extras.append((2, send_home))
@@ -932,6 +917,9 @@
     if extra:
         for which in range(2):
             scatter_wait(homes_ref, s["hos"], which, count)
+        slice_dev = homes_ref.shape[2]
+        for k in range(count):
+            mamba_ref[:, k * slice_dev : (k + 1) * slice_dev] = homes_ref[k]
 
 
 def last_stage(slots, home, stat, ids, w, experts_all, width, rep_count, tp_count, hidden_dev):
@@ -957,7 +945,8 @@
         outs = [shape((experts, rows // 2, hidden_dev), bf16)]
         if extra:
             scratch["hos"] = dma((2,))
-            outs += [shape(home.shape, bf16)]
+            scratch["homes"] = pltpu.VMEM(home.shape, bf16)
+            outs += [shape((home.shape[1], width), bf16)]
         got = pl.pallas_call(
             functools.partial(last_kernel, red, tuple(scratch), begin, extra, experts_all, width),
             out_shape=outs,
@@ -999,29 +988,22 @@
     expert_proj,
     expert_ids,
 ):
-    bf16 = jnp.bfloat16
     tp_count = lax.axis_size("tp")
     rep_count = lax.axis_size("rep")
     count = tp_count * rep_count
     tok_dev, width = tokens.shape
-    slice_dev = width // count
     experts = expert_proj.shape[1]
     hidden_dev = expert_proj.shape[3] // tp_count
 
-    pieces = tokens.reshape(tok_dev, count, slice_dev).transpose(1, 0, 2)
-    ids = jnp.pad(expert_ids.astype(bf16), ((0, 0), (0, LANES - 2)))
-    packed = jnp.concatenate([conv_weight, conv_skip, step_bias[None], decay_log], axis=0)
-    packed = jnp.pad(packed, ((0, -packed.shape[0] % 16), (0, 0)))
     args = (
-        pieces, ids, norm_gains, packed, select_proj.T, conv_state, router,
-        step_proj, input_proj, ssm_state, output_proj,
+        tokens, expert_ids, norm_gains, conv_weight, conv_skip, step_bias[None], decay_log,
+        select_proj.T, conv_state, router.T, step_proj, input_proj, ssm_state, output_proj,
     )
     conv_next, ssm_next, home, stat, slots, ids = mixer(args, rep_count, tp_count, experts)
-    hidden, home = last_stage(
+    hidden, mamba_out = last_stage(
         slots, home, stat, ids.reshape(count * tok_dev, LANES), expert_proj,
         router.shape[1], width, rep_count, tp_count, hidden_dev,
     )
-    mamba_out = home.transpose(1, 0, 2).reshape(tok_dev, width)
     hidden = hidden.reshape(experts, tp_count, CAPACITY, hidden_dev).transpose(1, 0, 2, 3)
     expert_hidden = hidden.reshape(experts * tp_count * CAPACITY, hidden_dev)
     return (mamba_out, conv_next, ssm_next, expert_hidden)

time: 124 us -> 118 us (0.952)
  Pallas kernels: 114 us -> 111 us
  other arithmetic: 2.02 us -> 0 us
  local copies, waits for them, and re-layouts: 7.21 us -> 5.86 us
    pallas_call x1, Pallas kernels: 68.1 us -> 65.2 us  [mixer(): pl.pallas_call(functools.partial(mixer_kernel, red, tuple(scratch), exper...]
    unnamed x8 -> x7, local copies, waits for them, and re-layouts: 4.35 us -> 2.95 us
    concatenate x1 -> x0, other arithmetic: 1.33 us -> none  [shards(): jnp.concatenate([conv_weight, conv_skip, step_bias[None], decay_log], axi...]
where the time goes in v3:
time: 118 us
  Pallas kernels  111 us (94%)
  local copies, waits for them, and re-layouts  5.86 us (5%)
    pallas_call x1, Pallas kernels, mixer(): pl.pallas_call(functools.partial(mixer_kernel, red, tuple(scratch), exper...  65.2 us
    pallas_call x1, Pallas kernels, last_stage(): pl.pallas_call(functools.partial(last_kernel, red, tuple(scratch), begin,...  45.8 us
    unnamed x7, local copies, waits for them, and re-layouts  2.95 us

profile of v3, /device:TPU:0, one launch (start us, length us, event | category | flops | bytes accessed | tf_op | source)
XLA Modules:
  0.0 117.6 jit_solution(15324935648605259874)
XLA Ops:
  0.6 1.2 %broadcast_in_dim.3.bias_ref = bf16[1,256]{1,0:T(2,128)(2,1)} reshape(bf16[256]{0:T(256)(128)(2,1)} %param.21) | data formatting | bytes 1024 | tf_op jit(solution)/shard_map/broadcast_in_dim | solution.py:999
  1.9 65.2 %mixer.1 = (bf16[3,8,2048]{2,1,0:T(8,128)(2,1)}, f32[8,16,2048]{2,1,0:T(8,128)}, bf16[32,2,128]{2,1,0:T(2,128)(2,1)}, f32[8,8,128]{2,1,0:T(8,128)}, bf16[2,64,12...) custom-call(bf16[2,4096]{1,0:T(2,128)(2,1)} %tok_in_ref.1, s32[2,2]{1,0:T(2,128)} %ids_in_ref.1, bf16[2,128]{1,0:T(2,128)(2,1)} %gains_ref.1, ...), custom_call_target="tpu_custom_call" | custom-call | tf_op jit(solution)/shard_map/mixer/pallas_call | solution.py:806
  67.1 0.0 copy-start.1
  67.1 0.0 copy-start
  67.1 45.8 %last_stage.1 = (bf16[2,8,3072]{2,1,0:T(8,128)(2,1)}, bf16[2,4096]{1,0:T(2,128)(2,1)}) custom-call(bf16[2,64,128]{2,1,0:T(8,128)(2,1)} %get-tuple-element.12.x_ref, bf16[32,2,128]{2,1,0:T(2,128)(2,1)} %get-tuple-element.13.home_ref, f32[8,8,128]{2,1,0:T(8,128)} %get-tuple-element.14.stat_ref, bf16[64,128]{1,0:T(8,128)(2,1)} %bitcast.6, ...), custom_call_target="tpu_custom_call" | custom-call | tf_op jit(solution)/shard_map/last_stage/pallas_call | solution.py:950
  112.9 0.9 reshape.18
  113.8 0.1 copy.19
  113.9 0.7 reshape.19
  114.6 1.3 %copy.23 = bf16[2,4096]{1,0:T(2,128)(2,1)} copy(bf16[2,4096]{1,0:T(2,128)(2,1)} %get-tuple-element.24) | data formatting | bytes 32768
  115.9 0.0 copy-done.1
  115.9 0.6 copy.24
  116.6 0.0 copy-done
  116.6 1.0 copy.25
Async XLA Ops:
  67.1 48.8 %copy-start.1 = (bf16[3,8,2048]{2,1,0:T(8,128)(2,1)S(1)}, bf16[3,8,2048]{2,1,0:T(8,128)(2,1)}, u32[]{:S(2)}) copy-start(bf16[3,8,2048]{2,1,0:T(8,128)(2,1)} %get-tuple-element.25) | copy-start | bytes 294916
  67.1 49.5 %copy-start = (f32[8,16,2048]{2,1,0:T(8,128)S(1)}, f32[8,16,2048]{2,1,0:T(8,128)}, u32[]{:S(2)}) copy-start(f32[8,16,2048]{2,1,0:T(8,128)} %get-tuple-element.26) | copy-start | bytes 3145732

commit v4 on v3

--- a/solution.py
+++ b/solution.py
@@ -379,16 +379,27 @@
     return maps
 
 
-def mixer_kernel(
-    red, names, experts,
-    tok_in_ref, ids_in_ref, gains_ref, weight_ref, skip_ref, bias_ref, decay_ref, sel_ref,
-    history_ref, router_ref,
-    step_ref, w_ref, state_ref, out_w_ref,
-    next_ref, state_out_ref, home_ref, stat_ref, slots_ref, idsall_ref, *scratch
-):
+def mixer_kernel(red, names, experts, tail, *refs):
+    (
+        tok_in_ref, ids_in_ref, gains_ref, weight_ref, skip_ref, bias_ref, decay_ref, sel_ref,
+        history_ref, router_ref, step_ref, w_ref, state_ref, out_w_ref,
+    ) = refs[:14]
+    refs = refs[14:]
+    if tail:
+        expert_red, expert_names, experts_all = tail
+        expert_w_ref, next_ref, state_out_ref, hid_ref, mamba_ref = refs[:5]
+        scratch, expert_refs = refs[5 : 5 + len(names)], refs[5 + len(names) :]
+    else:
+        next_ref, state_out_ref, home_ref, stat_ref, slots_ref, idsall_ref = refs[:6]
+        scratch = refs[6:]
     f32, bf16 = jnp.float32, jnp.bfloat16
     s = dict(zip(names, scratch))
     red.place()
+    if tail:
+        es = dict(zip(expert_names, expert_refs))
+        expert_red.place()
+        home_ref, stat_ref, slots_ref = s["home"], s["stat"], s["slots"]
+        idsall_ref = s["idsall"]
     z, x, y, c = red.z, red.x, red.y, red.c
     mz, mx, my, mc = red.mz, red.mx, red.my, red.mc
     tp_count, rep_count = y * c, z * x
@@ -491,6 +502,8 @@
     s["router"][: router_ref.shape[0]] = router_ref[...].astype(f32)
     next_ref[: taps - 2] = history_ref[1:]
 
+    if tail:
+        expert_fetch(expert_red, es, 0, expert_w_ref)
     scatter_wait(tokall, s["toks"], 1, count)
     tok_all = tokall.reshape(count * tok_dev, slice_dev)
     gain = gains_ref[...].astype(f32)
@@ -620,7 +633,7 @@
     s["step"][...] = softplus(step_pre + s["par"][tap0 + taps + 2 : tap0 + taps + 3])
     state_in.wait()
     wide = 2 * LANES
-    ways = CORES
+    ways = s["gcs"].shape[1]
     piece = inner_dev // ways
     gall = s["gall"]
 
@@ -713,6 +726,11 @@
             s["maps"][e], gained.astype(bf16), (((0,), (0,)), ((), ())), preferred_element_type=f32
         ).astype(bf16)
 
+    if tail:
+        expert_part(
+            expert_red, es, 0, experts_all, width, slots_ref, home_ref, stat_ref,
+            idsall_ref.reshape(count * tok_dev, LANES), hid_ref, mamba_ref,
+        )
     for k in range(z - 1):
         step_z(k).wait_send()
     for k in range(z):
@@ -744,9 +762,10 @@
     state_out.wait()
 
 
-def mixer(args, rep_count, tp_count, experts):
-    tok, ids, gains, weight, skip, bias, decay, sel, history, router = args[:-4]
-    step_proj, w, state, out_w = args[-4:]
+def mixer(args, expert_w, experts_all, rep_count, tp_count):
+    tok, ids, gains, weight, skip, bias, decay, sel, history, router = args[:10]
+    step_proj, w, state, out_w = args[10:]
+    experts, hidden_dev = expert_w.shape[1], expert_w.shape[3] // tp_count
     f32, bf16 = jnp.float32, jnp.bfloat16
     count = rep_count * tp_count
     tok_dev = tok.shape[0]
@@ -761,6 +780,12 @@
     vmem = pltpu.VMEM
     z, x, y, c = red.z, red.x, red.y, red.c
     tokens = count * tok_dev
+    ways = 4 if inner_dev % (8 * LANES) == 0 else 2
+    expert_rows = 2 * count * CAPACITY // rep_count
+    expert_red = Reduce(rep_count, tp_count, expert_rows, hidden_dev, 0)
+    expert_red.chunks = expert_red.per * experts
+    held = sum(r.chunks * r.chunk_bytes() for r in (red, expert_red)) + 2 * (w.size + expert_w.size)
+    fused = held <= ROOM
     scratch = red.scratch(2 * slice_dev)
     scratch.update(
         left=vmem((2 * tokens, 2 * slice_dev), bf16),
@@ -797,30 +822,61 @@
         txs=dma((2, z)),
         tzs=dma((2, z - 1)),
         acs=dma((2, n, rep_count - 1)),
-        gzs=dma((2, CORES, z - 1)),
-        gxs=dma((2, CORES, x * y - 1)),
-        gcs=dma((2, CORES)),
+        gzs=dma((2, ways, z - 1)),
+        gxs=dma((2, ways, x * y - 1)),
+        gcs=dma((2, ways)),
     )
     shape = jax.ShapeDtypeStruct
     anywhere = pl.BlockSpec(memory_space=pl.ANY)
-    return pl.pallas_call(
-        functools.partial(mixer_kernel, red, tuple(scratch), experts),
-        out_shape=[
-            shape(history.shape, bf16),
-            shape(state.shape, f32),
-            shape(pieces, bf16),
-            shape((rep_count, req, LANES), f32),
-            shape((experts, count * CAPACITY, slice_dev), bf16),
-            shape((count, tok_dev, LANES), bf16),
-        ],
-        in_specs=in_vmem(10) + [anywhere] * 4,
-        out_specs=in_vmem(1) + [anywhere] + in_vmem(4),
-        scratch_shapes=list(scratch.values()),
+    home, stat = pieces, (rep_count, req, LANES)
+    slots = (experts, count * CAPACITY, slice_dev)
+    idsall = (count, tok_dev, LANES)
+    outs = [shape(history.shape, bf16), shape(state.shape, f32)]
+    tail, names = None, tuple(scratch)
+    if fused:
+        scratch["home"] = vmem(home, bf16)
+        scratch["stat"] = vmem(stat, f32)
+        scratch["slots"] = vmem(slots, bf16)
+        scratch["idsall"] = vmem(idsall, bf16)
+        names = tuple(scratch)
+        more = expert_scratch(expert_red, 2 * slice_dev, experts, stat, home)
+        tail = (expert_red, tuple(more), experts_all)
+        outs += [
+            shape((experts, expert_rows // 2, hidden_dev), bf16), shape(tok.shape, bf16)
+        ]
+        args = args + (expert_w,)
+        spaces = list(scratch.values()) + list(more.values())
+    else:
+        outs += [shape(home, bf16), shape(stat, f32), shape(slots, bf16), shape(idsall, bf16)]
+        spaces = list(scratch.values())
+    got = pl.pallas_call(
+        functools.partial(mixer_kernel, red, names, experts, tail),
+        out_shape=outs,
+        in_specs=in_vmem(10) + [anywhere] * (len(args) - 10),
+        out_specs=in_vmem(1) + [anywhere] + in_vmem(len(outs) - 2),
+        scratch_shapes=spaces,
         compiler_params=pltpu.CompilerParams(
             collective_id=0, has_side_effects=True, vmem_limit_bytes=62 * 2**20
         ),
         name="mixer",
     )(*args)
+    if fused:
+        return got
+    home, stat, slots, idsall = got[2:]
+    hidden, mamba = last_stage(
+        slots, home, stat, idsall.reshape(tokens, LANES), expert_w, experts_all,
+        tok.shape[1], rep_count, tp_count, hidden_dev,
+    )
+    return got[0], got[1], hidden, mamba
+
+
+def expert_fetch(red, s, begin, w_ref):
+    for i in range(red.chunks):
+        expert, column = divmod(begin + i, red.per)
+        red.fetch(
+            s, w_ref, i, column * 2 * red.half,
+            lambda w, at, expert=expert: w.at[:, expert, :, at],
+        )
 
 
 def last_kernel(
@@ -829,21 +885,27 @@
     outs = 1 if extra else 0
     s = dict(zip(names, refs[outs:]))
     red.place()
+    expert_fetch(red, s, begin, w_ref)
+    count = red.z * red.x * red.y * red.c
+    greet_all(count, red.rep * red.y * red.c + red.tp, red.y * red.c)
+    mamba_ref = refs[0] if extra else None
+    expert_part(
+        red, s, begin, experts_all, width, x_ref, home_ref, stat_ref, ids_ref, hid_ref, mamba_ref
+    )
+
+
+def expert_part(
+    red, s, begin, experts_all, width, x_ref, home_ref, stat_ref, ids_ref, hid_ref, mamba_ref
+):
+    extra = mamba_ref is not None
     tp_count, rep_count = red.y * red.c, red.z * red.x
     count = tp_count * rep_count
     rep, tp = red.rep, red.tp
     me = rep * tp_count + tp
     wide = 2 * red.half
-    for i in range(red.chunks):
-        expert, column = divmod(begin + i, red.per)
-        red.fetch(
-            s, w_ref, i, column * wide, lambda w, at, expert=expert: w.at[:, expert, :, at]
-        )
+    homes_ref = s["homes"] if extra else None
     for expert in range(x_ref.shape[0]):
         s["left"][expert] = spread(x_ref[expert], red.rows // 2, 2)
-    if extra:
-        mamba_ref, homes_ref = refs[0], s["homes"]
-    greet_all(count, me, tp_count)
 
     def left_of(i):
         return s["left"][lax.div(begin + i, red.per)]
@@ -893,7 +955,6 @@
         homes_ref[me] = home_ref[me]
 
     def send_stats():
-
         def one(step, _):
             to = lax.rem(me + step, count)
             pltpu.make_async_remote_copy(
@@ -922,30 +983,39 @@
             mamba_ref[:, k * slice_dev : (k + 1) * slice_dev] = homes_ref[k]
 
 
+def expert_scratch(red, depth, experts, stat, home):
+    bf16, f32 = jnp.bfloat16, jnp.float32
+    dma = pltpu.SemaphoreType.DMA
+    rep_count, tp_count = red.z * red.x, red.y * red.c
+    scratch = red.scratch(depth)
+    scratch["left"] = pltpu.VMEM((experts, rep_count * red.rows, depth), bf16)
+    scratch["sas"] = dma((2,))
+    scratch["stats"] = pltpu.VMEM((rep_count * tp_count,) + stat[1:], f32)
+    scratch["seat"] = pltpu.VMEM((experts, red.rows // 2, LANES), f32)
+    scratch["size"] = pltpu.VMEM((experts, red.rows // 2, LANES), f32)
+    if home is not None:
+        scratch["hos"] = dma((2,))
+        scratch["homes"] = pltpu.VMEM(home, bf16)
+    return scratch
+
+
 def last_stage(slots, home, stat, ids, w, experts_all, width, rep_count, tp_count, hidden_dev):
-    f32, bf16 = jnp.float32, jnp.bfloat16
+    bf16 = jnp.bfloat16
     experts, total_rows, slice_dev = slots.shape
     rows = 2 * total_rows // rep_count
     shape = jax.ShapeDtypeStruct
-    dma = pltpu.SemaphoreType.DMA
     full = Reduce(rep_count, tp_count, rows, hidden_dev, 0)
     total = full.per * experts
-    weights = w.size // experts // full.per * experts * 2 // experts
-    most = max(1, ROOM // (full.chunk_bytes() + weights))
+    most = max(1, ROOM // (full.chunk_bytes() + 2 * w.size // total))
     begin, ups = 0, None
     while begin < total:
         red = Reduce(rep_count, tp_count, rows, hidden_dev, min(most, total - begin))
         extra = begin == 0
-        scratch = red.scratch(2 * slice_dev)
-        scratch["left"] = pltpu.VMEM((experts, rep_count * rows, 2 * slice_dev), bf16)
-        scratch["sas"] = dma((2,))
-        scratch["stats"] = pltpu.VMEM((rep_count * tp_count,) + stat.shape[1:], f32)
-        scratch["seat"] = pltpu.VMEM((experts, rows // 2, LANES), f32)
-        scratch["size"] = pltpu.VMEM((experts, rows // 2, LANES), f32)
+        scratch = expert_scratch(
+            red, 2 * slice_dev, experts, stat.shape, home.shape if extra else None
+        )
         outs = [shape((experts, rows // 2, hidden_dev), bf16)]
         if extra:
-            scratch["hos"] = dma((2,))
-            scratch["homes"] = pltpu.VMEM(home.shape, bf16)
             outs += [shape((home.shape[1], width), bf16)]
         got = pl.pallas_call(
             functools.partial(last_kernel, red, tuple(scratch), begin, extra, experts_all, width),
@@ -971,6 +1041,53 @@
     return ups, homes
 
 
+def finish_kernel(
+    experts, next_ref, mamba_ref, hid_ref, state_ref,
+    next_out, mamba_out, hid_out, state_out, held, sems
+):
+    parts = sems.shape[1]
+    size = state_ref.shape[0] // parts
+
+    def move(k, which):
+        at = pl.ds(k * size, size)
+        if which == 0:
+            return pltpu.make_async_copy(state_ref.at[at], held.at[at], sems.at[0, k])
+        return pltpu.make_async_copy(held.at[at], state_out.at[at], sems.at[1, k])
+
+    for k in range(parts):
+        move(k, 0).start()
+    next_out[...] = next_ref[...]
+    mamba_out[...] = mamba_ref[...]
+    rows = hid_out.shape[0]
+    to, source = column_iota((rows, rows), 0), column_iota((rows, rows), 1)
+    block, seat = lax.div(to, experts * CAPACITY), lax.rem(to, CAPACITY)
+    expert = lax.rem(lax.div(to, CAPACITY), experts)
+    moves = source == expert * (rows // experts) + block * CAPACITY + seat
+    hid_out[...] = jnp.dot(
+        moves.astype(jnp.bfloat16), hid_ref[...], preferred_element_type=jnp.float32
+    ).astype(jnp.bfloat16)
+    for k in range(parts):
+        move(k, 0).wait()
+        move(k, 1).start()
+    for k in range(parts):
+        move(k, 1).wait()
+
+
+def finish(conv_next, mamba, hidden, state, experts):
+    anywhere = pl.BlockSpec(memory_space=pl.ANY)
+    arrays = (conv_next, mamba, hidden, state)
+    return pl.pallas_call(
+        functools.partial(finish_kernel, experts),
+        out_shape=[jax.ShapeDtypeStruct(array.shape, array.dtype) for array in arrays],
+        in_specs=in_vmem(3) + [anywhere],
+        out_specs=in_vmem(3) + [anywhere],
+        scratch_shapes=[
+            pltpu.VMEM(state.shape, state.dtype), pltpu.SemaphoreType.DMA((2, 4))
+        ],
+        name="finish",
+    )(*arrays)
+
+
 def shards(
     tokens,
     conv_state,
@@ -990,22 +1107,17 @@
 ):
     tp_count = lax.axis_size("tp")
     rep_count = lax.axis_size("rep")
-    count = tp_count * rep_count
-    tok_dev, width = tokens.shape
-    experts = expert_proj.shape[1]
-    hidden_dev = expert_proj.shape[3] // tp_count
-
     args = (
         tokens, expert_ids, norm_gains, conv_weight, conv_skip, step_bias[None], decay_log,
         select_proj.T, conv_state, router.T, step_proj, input_proj, ssm_state, output_proj,
     )
-    conv_next, ssm_next, home, stat, slots, ids = mixer(args, rep_count, tp_count, experts)
-    hidden, mamba_out = last_stage(
-        slots, home, stat, ids.reshape(count * tok_dev, LANES), expert_proj,
-        router.shape[1], width, rep_count, tp_count, hidden_dev,
+    conv_next, ssm_next, hidden, mamba = mixer(
+        args, expert_proj, router.shape[1], rep_count, tp_count
     )
-    hidden = hidden.reshape(experts, tp_count, CAPACITY, hidden_dev).transpose(1, 0, 2, 3)
-    expert_hidden = hidden.reshape(experts * tp_count * CAPACITY, hidden_dev)
+    hidden = hidden.reshape(-1, hidden.shape[2])
+    conv_next, mamba_out, expert_hidden, ssm_next = finish(
+        conv_next, mamba, hidden, ssm_next, expert_proj.shape[1]
+    )
     return (mamba_out, conv_next, ssm_next, expert_hidden)
 
 

time: 118 us -> 112 us (0.949)
  local copies, waits for them, and re-layouts: 5.86 us -> 1.22 us
    unnamed x7 -> x0, local copies, waits for them, and re-layouts: 2.95 us -> none
    reshape x2 -> x0, local copies, waits for them, and re-layouts: 1.61 us -> none  [the longest x1 0.93 us: shards(): hidden.reshape(experts, tp_count, CAPACITY, hidden_dev)]
    pallas_call x2, Pallas kernels: 111 us -> 110 us  [the longest x1 106 us: mixer(): pl.pallas_call(functools.partial(mixer_kernel, red, names, experts, tail)...]
where the time goes in v4:
time: 112 us; the launch traced here: 111 us
  Pallas kernels  110 us (98%)
  local copies, waits for them, and re-layouts  1.22 us (1%)
    pallas_call x1, Pallas kernels, mixer(): pl.pallas_call(functools.partial(mixer_kernel, red, names, experts, tail)...  106 us
    pallas_call x1, Pallas kernels, finish(): pl.pallas_call(functools.partial(finish_kernel, experts), out_shape=[jax....  3.62 us

profile of v4, /device:TPU:0, one launch (start us, length us, event | category | flops | bytes accessed | tf_op | source)
XLA Modules:
  0.0 111.4 jit_solution(14483921699757019908)
XLA Ops:
  0.6 1.2 %broadcast_in_dim.3.refs_5_ = bf16[1,256]{1,0:T(2,128)(2,1)} reshape(bf16[256]{0:T(256)(128)(2,1)} %param.21) | data formatting | bytes 1024 | tf_op jit(solution)/shard_map/broadcast_in_dim | solution.py:1111
  1.9 105.9 %mixer.1 = (bf16[3,8,2048]{2,1,0:T(8,128)(2,1)}, f32[8,16,2048]{2,1,0:T(8,128)}, bf16[2,8,3072]{2,1,0:T(8,128)(2,1)}, bf16[2,4096]{1,0:T(2,128)(2,1)}) custom-call(bf16[2,4096]{1,0:T(2,128)(2,1)} %refs_0_.1, s32[2,2]{1,0:T(2,128)} %refs_1_.1, bf16[2,128]{1,0:T(2,128)(2,1)} %refs_2_.1, bf16[4,256]{1,0:T(4,128)(2,1)} %refs_3_.1, bf16[2,256]{1,0:T(2,128)(2,1)} %refs_4_.1, ...), custom_call_target="tpu_custom_call" | custom-call | tf_op jit(solution)/shard_map/mixer/pallas_call | solution.py:852
  107.7 3.6 %finish.1 = (bf16[3,8,2048]{2,1,0:T(8,128)(2,1)}, bf16[2,4096]{1,0:T(2,128)(2,1)}, bf16[16,3072]{1,0:T(8,128)(2,1)}, f32[8,16,2048]{2,1,0:T(8,128)}) custom-call(bf16[3,8,2048]{2,1,0:T(8,128)(2,1)} %get-tuple-element.12.next_ref, bf16[2,4096]{1,0:T(2,128)(2,1)} %get-tuple-element.13.mamba_ref, bf16[16,3072]{1,0:T(8,128)(2,1)} %bitcast.4, ...), custom_call_target="tpu_custom_call" | custom-call | tf_op jit(solution)/shard_map/finish/pallas_call | solution.py:1079

commit v5 on v4

--- a/solution.py
+++ b/solution.py
@@ -410,7 +410,10 @@
     req = red.rows // 2
     tok_ref, ids_ref, packed_ref = s["tok"], s["ids"], s["packed"]
     tok_dev, slice_dev = tok_ref.shape[1:]
-    tokall, packall, stepall = s["tokall"], s["packall"], s["stepall"]
+    tokall, packall, stepz = s["tokall"], s["packall"], s["stepz"]
+    step_dev, part_cols = step_ref.shape[0], sel_ref.shape[0]
+    group_cols = part_cols * x
+    owners = group_cols // step_dev
     taps = history_ref.shape[0] + 1
     states = tap0 = state_ref.shape[1]
 
@@ -418,9 +421,6 @@
     out_in = pltpu.make_async_copy(out_w_ref, s["outw"], s["own"].at[2])
     for i in range(red.chunks):
         red.fetch(s, w_ref, i, i * 2 * red.half, lambda w, at: w.at[:, :, at])
-    columns = pl.ds(pl.multiple_of(tp * inner_dev, LANES), inner_dev)
-    own_step = pltpu.make_async_copy(step_ref.at[:, columns], stepall.at[rep, tp], s["own"].at[0])
-    own_step.start()
     state_in.start()
     out_in.start()
     for k in range(count):
@@ -428,7 +428,8 @@
     ids = ids_in_ref[...].astype(f32)
     ids = jnp.concatenate([ids, jnp.zeros((tok_dev, LANES - ids.shape[1]), f32)], axis=1)
     ids_ref[...] = ids.astype(bf16)
-    rows = [ref[...].astype(f32) for ref in (decay_ref, weight_ref, skip_ref, bias_ref)]
+    rows = [ref[...].astype(f32) for ref in (decay_ref, weight_ref, skip_ref)]
+    rows.append(bias_ref[...].astype(f32).reshape(1, -1))
     spare = packed_ref.shape[0] - sum(row.shape[0] for row in rows)
     rows.append(jnp.zeros((spare, packed_ref.shape[1]), f32))
     packed_ref[...] = jnp.concatenate(rows, axis=0).astype(bf16)
@@ -436,6 +437,7 @@
     width = tok.shape[1]
     square = jnp.sum(tok * tok, axis=-1, keepdims=True)
     s["scale"][...] = jnp.broadcast_to(lax.rsqrt(square / width + epsilon), s["scale"].shape)
+    stepz[...] = jnp.zeros(stepz.shape, bf16)
     greet_all(count, me, tp_count)
     scatter_start(tok_ref, tokall, s["toks"], count, me, tp_count)
     tokall[me] = tok_ref[me]
@@ -463,7 +465,7 @@
         return 0
 
     lax.fori_loop(0, rep_count, pack_start, 0)
-    scale_copies, step_copies = [], []
+    scale_copies = []
     for k in range(tp_count - 1):
         to = lax.rem(tp + k + 1, tp_count)
         scale_copies.append(
@@ -471,33 +473,53 @@
                 s["scale"], s["scales"].at[tp], s["scs"].at[0, k], s["scs"].at[1, k], {"tp": to}
             )
         )
-        columns = pl.ds(pl.multiple_of(to * inner_dev, LANES), inner_dev)
-        step_copies.append(
-            remote(
-                step_ref.at[:, columns], stepall.at[rep, tp],
-                s["sts"].at[0, k], s["sts"].at[1, k], {"tp": to},
-            )
-        )
     start_all(scale_copies)
     s["scales"][tp] = s["scale"][...]
-    start_all(step_copies)
     scatter_start(ids_ref, idsall_ref, s["idss"], count, me, tp_count)
     idsall_ref[me] = ids_ref[...]
-    to_x = {"rep": mz * x + lax.rem(mx + 1, x)}
-
-    def step_z(k):
-        block = stepall.at[rep]
+    sel_copies = [
+        remote(
+            sel_ref, s["sel"].at[mx], s["sxs"].at[0, k], s["sxs"].at[1, k],
+            red.peer_x(lax.rem(mx + k + 1, x)),
+        )
+        for k in range(x - 1)
+    ]
+    start_all(sel_copies)
+    step_slot, step_home = lax.rem(me, owners), lax.div(me, owners)
+
+    def step_target(k):
+        return step_home * x + lax.div(k, tp_count), lax.rem(k, tp_count)
+
+    def step_is_me(k):
+        to_rep, to_tp = step_target(k)
+        return (to_rep == rep) & (to_tp == tp)
+
+    def step_source(to_tp):
+        return step_ref.at[:, pl.ds(pl.multiple_of(to_tp * inner_dev, LANES), inner_dev)]
+
+    def step_copy(k):
+        to_rep, to_tp = step_target(k)
         return remote(
-            block, block, s["tzs"].at[0, k], s["tzs"].at[1, k], red.peer_z(lax.rem(mz + k + 1, z))
+            step_source(to_tp), stepz.at[step_slot],
+            s["sts"].at[0, k], s["sts"].at[1, step_slot], {"rep": to_rep, "tp": to_tp},
         )
 
-    def step_x(source_z):
-        block = stepall.at[source_z * x + mx]
-        return remote(block, block, s["txs"].at[0, source_z], s["txs"].at[1, source_z], to_x)
-
-    s["sel"][...] = jnp.zeros(s["sel"].shape, bf16)
-    part_cols = sel_ref.shape[0]
-    s["sel"][:part_cols] = sel_ref[...]
+    own_step = pltpu.make_async_copy(step_source(tp), stepz.at[step_slot], s["own"].at[0])
+
+    def step_start(k, _):
+        @pl.when(step_is_me(k))
+        def _():
+            own_step.start()
+
+        @pl.when(jnp.logical_not(step_is_me(k)))
+        def _():
+            step_copy(k).start()
+
+        return 0
+
+    lax.fori_loop(0, x * tp_count, step_start, 0)
+
+    s["sel"][mx] = sel_ref[...]
     s["router"][...] = jnp.zeros(s["router"].shape, f32)
     s["router"][: router_ref.shape[0]] = router_ref[...].astype(f32)
     next_ref[: taps - 2] = history_ref[1:]
@@ -510,18 +532,24 @@
     x_rows = (tok_all[...].astype(f32) * gain[:1]).astype(bf16)
     s["left"][...] = spread(x_rows, req, 2)
 
-    def step_first():
-        own_step.wait()
-        for copy in step_copies:
+    def weights():
+        for copy in sel_copies:
             copy.wait_recv()
-        for k in range(z - 1):
-            step_z(k).start()
-
-    def step_second():
-        for k in range(z - 1):
-            step_z(k).wait_recv()
-        for k in range(z // 2):
-            step_x(k).start()
+
+        def step_came(k, _):
+            @pl.when((mz * owners + k != me) & (mz * owners + k < count))
+            def _():
+                pltpu.make_async_copy(stepz.at[k], stepz.at[k], s["sts"].at[1, k]).wait()
+
+            return 0
+
+        lax.fori_loop(0, owners, step_came, 0)
+
+        def own_came(k, _):
+            pl.when(step_is_me(k))(own_step.wait)
+            return 0
+
+        lax.fori_loop(0, x * tp_count, own_came, 0)
 
     def params():
         for copy in scale_copies:
@@ -558,78 +586,85 @@
             mix += par[tap0 + k : tap0 + k + 1, at] * history_ref[k, :, at].astype(f32)
         act = silu(mix)
         s["act"][:, at] = act
-        s["actall"][rep, :, at] = act.astype(bf16)
+        s["actall"][mz, :, at] = act.astype(bf16)
 
     def act_copies(i):
         at = pl.ds(pl.multiple_of(i * 2 * red.half, LANES), 2 * red.half)
-        block = s["actall"].at[rep, :, at]
+        block = s["actall"].at[mz, :, at]
         return [
             remote(
                 block, block, s["acs"].at[0, i, k], s["acs"].at[1, i, k],
-                {"rep": lax.rem(rep + k + 1, rep_count)},
+                red.peer_z(lax.rem(mz + k + 1, z)),
             )
-            for k in range(rep_count - 1)
+            for k in range(z - 1)
         ]
 
     n = red.chunks
     lags = (1, n, n + 2, n + 4)
-    extras = [(1, step_first), (2, params), (2, maps), (2 * n + 1, step_second)]
+    extras = [(2, params), (2, maps), (n, weights)]
     red.run(
         s, lambda i: s["left"][...], store, lags, extras, lambda i: start_all(act_copies(i))
     )
-    for k in range(z // 2, z):
-        step_x(k).start()
-
     def act_came(i, _):
         for copy in act_copies(i):
             copy.wait_recv()
         return 0
 
     lax.fori_loop(0, red.chunks, act_came, 0)
-    every = s["actall"].reshape(rep_count * req, inner_dev)[...]
-    part = lax.dot_general(
-        every, s["sel"][...], (((1,), (1,)), ((), ())), preferred_element_type=f32
+    every = s["actall"].reshape(z * req, inner_dev)[...]
+    part = jnp.zeros((z * req, LANES), f32)
+    for k in range(x):
+        cols = lax.dot_general(
+            every, s["sel"][k], (((1,), (1,)), ((), ())), preferred_element_type=f32
+        )
+        spare = jnp.zeros((z * req, LANES - part_cols), f32)
+        cols = jnp.concatenate([cols, spare], axis=1)
+        part += pltpu.roll(cols, k * part_cols, 1) if k else cols
+    s["parts"][tp] = part.astype(bf16)
+    part_copies = [
+        remote(
+            s["parts"].at[tp], s["parts"].at[tp], s["pts"].at[0, k], s["pts"].at[1, k],
+            {"tp": lax.rem(tp + k + 1, tp_count)},
+        )
+        for k in range(tp_count - 1)
+    ]
+    start_all(part_copies)
+    for copy in part_copies:
+        copy.wait_recv()
+    selected = s["parts"][0].astype(f32)
+    for k in range(1, tp_count):
+        selected += s["parts"][k].astype(f32)
+    s["picks"][...] = selected.reshape(z, req, LANES)
+    if step_dev % 8 == 0:
+        step_rows = stepz.reshape(LANES, inner_dev)[...]
+    else:
+        step_rows = stepz[...].reshape(LANES, inner_dev)
+    pre = jnp.dot(selected.astype(bf16), step_rows, preferred_element_type=f32)
+    s["pre"][...] = pre.astype(bf16).reshape(z, req, inner_dev)
+    pre_copies = []
+    for k in range(z - 1):
+        to = lax.rem(mz + k + 1, z)
+        for name, slots, sems in (("picks", "picked", "mzs"), ("pre", "preall", "pzs")):
+            pre_copies.append(
+                remote(
+                    s[name].at[to], s[slots].at[mz], s[sems].at[0, k], s[sems].at[1, k],
+                    red.peer_z(to),
+                )
+            )
+    start_all(pre_copies)
+    s["picked"][mz] = s["picks"][mz]
+    s["preall"][mz] = s["pre"][mz]
+    for copy in pre_copies:
+        copy.wait_recv()
+    rank = step_dev * count
+    maps_z, maps_lane = divmod(rank, group_cols)
+    both = jnp.concatenate(
+        [s["picked"][maps_z], jnp.zeros((LANES - req, LANES), f32)], axis=0
     )
-    s["part"][...] = part.astype(bf16).reshape(rep_count, req, LANES)
-
-    def part_start(step, _):
-        to = lax.rem(me + step, count)
-        remote(
-            s["part"].at[lax.div(to, tp_count)], s["parts"].at[me],
-            s["pts"].at[0], s["pts"].at[1], device_of(to, tp_count),
-        ).start()
-        return 0
-
-    lax.fori_loop(1, count, part_start, 0)
-    s["parts"][me] = s["part"][rep]
-    scatter_wait(s["parts"], s["pts"], 1, count)
-    total_cols = part_cols * rep_count
-    tiles = [jnp.zeros((req, LANES), f32) for _ in range(-(-total_cols // LANES))]
-    lane = column_iota((req, LANES), 1)
-    for r in range(rep_count):
-        cols = s["parts"][r * tp_count].astype(f32)
-        for p in range(1, tp_count):
-            cols += s["parts"][r * tp_count + p].astype(f32)
-        tile, shift = divmod(r * part_cols, LANES)
-        if shift:
-            cols = pltpu.roll(cols, shift, 1)
-        tiles[tile] += jnp.where(lane >= shift, cols, 0.0)
-        if shift + part_cols > LANES:
-            tiles[tile + 1] += jnp.where(lane < shift + part_cols - LANES, cols, 0.0)
-    rank = total_cols - 2 * states
-    low_tiles = rank // LANES
-    low = jnp.concatenate(tiles[:low_tiles], axis=1).astype(bf16)
-    both_maps = jnp.concatenate(
-        [tiles[low_tiles], jnp.zeros((LANES - req, LANES), f32)], axis=0
-    ).T
-    s["bc"][...] = both_maps
-    for k in range(z):
-        step_x(k).wait_recv()
-    if step_ref.shape[0] % 8 == 0:
-        step_rows = stepall.reshape(rank, inner_dev)[...]
-    else:
-        step_rows = stepall[...].reshape(rank, inner_dev)
-    step_pre = jnp.dot(low, step_rows, preferred_element_type=f32)
+    s["bc"][...] = (pltpu.roll(both, LANES - maps_lane, 1) if maps_lane else both).T
+    step_pre = s["preall"][0].astype(f32)
+    for k in range(1, z):
+        step_pre += s["preall"][k].astype(f32)
     s["step"][...] = softplus(step_pre + s["par"][tap0 + taps + 2 : tap0 + taps + 3])
     state_in.wait()
     wide = 2 * LANES
@@ -731,12 +766,17 @@
             expert_red, es, 0, experts_all, width, slots_ref, home_ref, stat_ref,
             idsall_ref.reshape(count * tok_dev, LANES), hid_ref, mamba_ref,
         )
-    for k in range(z - 1):
-        step_z(k).wait_send()
-    for k in range(z):
-        step_x(k).wait_send()
-    for copy in step_copies + scale_copies:
+    for copy in sel_copies + scale_copies + part_copies + pre_copies:
         copy.wait_send()
+
+    def step_sent(k, _):
+        @pl.when(jnp.logical_not(step_is_me(k)))
+        def _():
+            step_copy(k).wait_send()
+
+        return 0
+
+    lax.fori_loop(0, x * tp_count, step_sent, 0)
 
     def pack_sent(k, _):
         @pl.when(jnp.logical_not(is_me(k)))
@@ -758,7 +798,6 @@
             copy.wait_send()
     scatter_wait(idsall_ref, s["idss"], 0, count)
     scatter_wait(tokall, s["toks"], 0, count)
-    scatter_wait(s["parts"], s["pts"], 0, count)
     state_out.wait()
 
 
@@ -771,7 +810,7 @@
     tok_dev = tok.shape[0]
     slice_dev = tok.shape[1] // count
     pieces = (count, tok_dev, slice_dev)
-    packed_rows = weight.shape[0] + skip.shape[0] + bias.shape[0] + decay.shape[0]
+    packed_rows = weight.shape[0] + skip.shape[0] + 1 + decay.shape[0]
     packed = (packed_rows + -packed_rows % 16, decay.shape[1])
     req, states, inner_dev = state.shape
     red = Reduce(rep_count, tp_count, 2 * req, inner_dev, 0)
@@ -780,7 +819,7 @@
     vmem = pltpu.VMEM
     z, x, y, c = red.z, red.x, red.y, red.c
     tokens = count * tok_dev
-    ways = 4 if inner_dev % (8 * LANES) == 0 else 2
+    ways = CORES
     expert_rows = 2 * count * CAPACITY // rep_count
     expert_red = Reduce(rep_count, tp_count, expert_rows, hidden_dev, 0)
     expert_red.chunks = expert_red.per * experts
@@ -797,15 +836,18 @@
         tokall=vmem(pieces, bf16),
         packall=vmem((rep_count,) + packed, bf16),
         par=vmem((packed[0], inner_dev), f32),
-        stepall=vmem((rep_count, tp_count, step_proj.shape[0], inner_dev), bf16),
-        sel=vmem((LANES, inner_dev), bf16),
+        stepz=vmem((LANES // step_proj.shape[0], step_proj.shape[0], inner_dev), bf16),
+        sel=vmem((x,) + sel.shape, bf16),
         router=vmem((LANES, slice_dev), f32),
         maps=vmem((experts, tokens, count * CAPACITY), bf16),
         gate=vmem((req, inner_dev), f32),
         act=vmem((req, inner_dev), f32),
-        actall=vmem((rep_count, req, inner_dev), bf16),
-        part=vmem((rep_count, req, LANES), bf16),
-        parts=vmem((count, req, LANES), bf16),
+        actall=vmem((z, req, inner_dev), bf16),
+        parts=vmem((tp_count, z * req, LANES), bf16),
+        picks=vmem((z, req, LANES), f32),
+        picked=vmem((z, req, LANES), f32),
+        pre=vmem((z, req, inner_dev), bf16),
+        preall=vmem((z, req, inner_dev), bf16),
         bc=vmem((LANES, LANES), f32),
         step=vmem((req, inner_dev), f32),
         read=vmem((req, inner_dev), f32),
@@ -814,14 +856,15 @@
         gall=vmem((y, c, z, x, req, inner_dev), bf16),
         toks=dma((2,)),
         idss=dma((2,)),
-        pts=dma((2,)),
+        pts=dma((2, tp_count - 1)),
+        mzs=dma((2, z - 1)),
+        pzs=dma((2, z - 1)),
         scs=dma((2, tp_count - 1)),
-        sts=dma((2, tp_count - 1)),
+        sts=dma((2, max(x * tp_count, x * sel.shape[0] // step_proj.shape[0]))),
+        sxs=dma((2, x - 1)),
         pks=dma((2, rep_count)),
         own=dma((4,)),
-        txs=dma((2, z)),
-        tzs=dma((2, z - 1)),
-        acs=dma((2, n, rep_count - 1)),
+        acs=dma((2, n, z - 1)),
         gzs=dma((2, ways, z - 1)),
         gxs=dma((2, ways, x * y - 1)),
         gcs=dma((2, ways)),
@@ -1108,7 +1151,7 @@
     tp_count = lax.axis_size("tp")
     rep_count = lax.axis_size("rep")
     args = (
-        tokens, expert_ids, norm_gains, conv_weight, conv_skip, step_bias[None], decay_log,
+        tokens, expert_ids, norm_gains, conv_weight, conv_skip, step_bias, decay_log,
         select_proj.T, conv_state, router.T, step_proj, input_proj, ssm_state, output_proj,
     )
     conv_next, ssm_next, hidden, mamba = mixer(

time: 112 us -> 107 us (0.955)
  Pallas kernels: 110 us -> 106 us
  local copies, waits for them, and re-layouts: 1.22 us -> 0 us
    pallas_call x1, Pallas kernels: 106 us -> 102 us  [mixer(): pl.pallas_call(functools.partial(mixer_kernel, red, names, experts, tail)...]
    broadcast_in_dim x1 -> x0, local copies, waits for them, and re-layouts: 1.22 us -> none  [shards(): step_bias[None]]
where the time goes in v5:
time: 107 us
  Pallas kernels  106 us (99%)
    pallas_call x1, Pallas kernels, mixer(): pl.pallas_call(functools.partial(mixer_kernel, red, names, experts, tail)...  102 us
    pallas_call x1, Pallas kernels, finish(): pl.pallas_call(functools.partial(finish_kernel, experts), out_shape=[jax....  3.62 us

profile of v5, /device:TPU:0, one launch (start us, length us, event | category | flops | bytes accessed | tf_op | source)
XLA Modules:
  0.0 106.8 jit_solution(9974822301750529369)
XLA Ops:
  0.6 102.5 %mixer.1 = (bf16[3,8,2048]{2,1,0:T(8,128)(2,1)}, f32[8,16,2048]{2,1,0:T(8,128)}, bf16[2,8,3072]{2,1,0:T(8,128)(2,1)}, bf16[2,4096]{1,0:T(2,128)(2,1)}) custom-call(bf16[2,4096]{1,0:T(2,128)(2,1)} %refs_0_.1, s32[2,2]{1,0:T(2,128)} %refs_1_.1, bf16[2,128]{1,0:T(2,128)(2,1)} %refs_2_.1, bf16[4,256]{1,0:T(4,128)(2,1)} %refs_3_.1, bf16[2,256]{1,0:T(2,128)(2,1)} %refs_4_.1, ...), custom_call_target="tpu_custom_call" | custom-call | tf_op jit(solution)/shard_map/mixer/pallas_call | solution.py:895
  103.1 3.6 %finish.1 = (bf16[3,8,2048]{2,1,0:T(8,128)(2,1)}, bf16[2,4096]{1,0:T(2,128)(2,1)}, bf16[16,3072]{1,0:T(8,128)(2,1)}, f32[8,16,2048]{2,1,0:T(8,128)}) custom-call(bf16[3,8,2048]{2,1,0:T(8,128)(2,1)} %get-tuple-element.12.next_ref, bf16[2,4096]{1,0:T(2,128)(2,1)} %get-tuple-element.13.mamba_ref, bf16[16,3072]{1,0:T(8,128)(2,1)} %bitcast.4, ...), custom_call_target="tpu_custom_call" | custom-call | tf_op jit(solution)/shard_map/finish/pallas_call | solution.py:1122

commit v6 on v5

--- a/solution.py
+++ b/solution.py
@@ -37,6 +37,7 @@
         self.per = dev_cols // (2 * self.half)
         self.dev_cols = dev_cols
         self.chunks = total_chunks
+        self.mix = 0
         self.blocks = self.z * self.x * self.y
 
     def chunk_bytes(self):
@@ -65,7 +66,121 @@
             s2b=dma((2, n, y - 1)),
             s3=dma((2, n, z - 1)),
         )
+        if self.mix:
+            m, far = -(-n // self.mix), z // 2
+            buffers.update(
+                rz=pltpu.VMEM((m, 2, self.blocks // 2, rows, half), bf16),
+                q1a=pltpu.VMEM((m, x - 1, y * far, rows, half), bf16),
+                q1b=pltpu.VMEM((m, y - 1, x * far, rows, half), bf16),
+                q2a=pltpu.VMEM((m, y - 1, far, rows, half), bf16),
+                q2b=pltpu.VMEM((m, x - 1, far, rows, half), bf16),
+                c3=pltpu.VMEM((m, far, 2, rows, half), bf16),
+                d3=pltpu.VMEM((m, far - 1, 2, rows, half), bf16),
+                sz=dma((2, m, 2)),
+                t1a=dma((2, m, x - 1)),
+                t1b=dma((2, m, y - 1)),
+                t2a=dma((2, m, y - 1)),
+                t2b=dma((2, m, x - 1)),
+                t3=dma((2, m, far - 1)),
+            )
         return buffers
+
+    def mixed_copies(self, s, e, stage):
+        z, x, y = self.z, self.x, self.y
+        far, low, high = z // 2, lax.rem(self.mz, 2), lax.div(self.mz, 2)
+        if stage == 1:
+            size = self.blocks // 2
+            return [
+                remote(
+                    s["r0"].at[e * self.mix, h, pl.ds((1 - low) * size, size)],
+                    s["rz"].at[e, h], s["sz"].at[0, e, h], s["sz"].at[1, e, h],
+                    self.peer_z(high * 2 + 1 - low),
+                )
+                for h in range(2)
+            ]
+        if stage == 2:
+            return self.exchange(
+                s["rz"].at[e, 0], x, self.mx, y * far, s["q1a"], s["t1a"], e, self.peer_x
+            ) + self.exchange(
+                s["rz"].at[e, 1], y, self.my, x * far, s["q1b"], s["t1b"], e, self.peer_y
+            )
+        if stage == 3:
+            return self.exchange(
+                s["q1a"].at[e, 0], y, self.my, far, s["q2a"], s["t2a"], e, self.peer_y
+            ) + self.exchange(
+                s["q1b"].at[e, 0], x, self.mx, far, s["q2b"], s["t2b"], e, self.peer_x
+            )
+        out = []
+        for step in range(1, far):
+            to = lax.rem(high + step, far)
+            out.append(
+                remote(
+                    s["c3"].at[e, to], s["d3"].at[e, step - 1],
+                    s["t3"].at[0, e, step - 1], s["t3"].at[1, e, step - 1],
+                    self.peer_z(to * 2 + low),
+                )
+            )
+        return out
+
+    def mixed_core(self, s, i):
+        for copy in self.copies(s, i, 0):
+            copy.wait_recv()
+        for h in range(2):
+            self.add(s["r0"].at[i, h], [s["b0"].at[i, self.mc, h]])
+        start_all(self.mixed_copies(s, lax.div(i, self.mix), 1))
+
+    def mixed_near(self, s, i):
+        e = lax.div(i, self.mix)
+        for copy in self.mixed_copies(s, e, 1):
+            copy.wait_recv()
+        size, low = self.blocks // 2, lax.rem(self.mz, 2)
+        for h in range(2):
+            self.add(s["rz"].at[e, h], [s["r0"].at[i, h, pl.ds(low * size, size)]])
+        start_all(self.mixed_copies(s, e, 2))
+
+    def mixed_first(self, s, i):
+        e = lax.div(i, self.mix)
+        for copy in self.mixed_copies(s, e, 2):
+            copy.wait_recv()
+        far = self.z // 2
+        for h, name, me, size, count in (
+            (0, "q1a", self.mx, self.y * far, self.x),
+            (1, "q1b", self.my, self.x * far, self.y),
+        ):
+            others = [s[name].at[e, k] for k in range(1, count - 1)]
+            others.append(s["rz"].at[e, h, pl.ds(me * size, size)])
+            self.add(s[name].at[e, 0], others)
+        start_all(self.mixed_copies(s, e, 3))
+
+    def mixed_second(self, s, i):
+        e = lax.div(i, self.mix)
+        for copy in self.mixed_copies(s, e, 3):
+            copy.wait_recv()
+        far = self.z // 2
+        for h, name, came, me, count in (
+            (0, "q2a", "q1a", self.my, self.y),
+            (1, "q2b", "q1b", self.mx, self.x),
+        ):
+            for k in range(far):
+                total = s[came][e, 0, me * far + k].astype(jnp.float32)
+                for j in range(count - 1):
+                    total += s[name][e, j, k].astype(jnp.float32)
+                s["c3"][e, k, h] = total.astype(jnp.bfloat16)
+        start_all(self.mixed_copies(s, e, 4))
+
+    def mixed_last(self, s, i, store, done):
+        e = lax.div(i, self.mix)
+        for copy in self.mixed_copies(s, e, 4):
+            copy.wait_recv()
+        for h in range(2):
+            total = s["c3"][e, lax.div(self.mz, 2), h].astype(jnp.float32)
+            for k in range(self.z // 2 - 1):
+                total += s["d3"][e, k, h].astype(jnp.float32)
+            store(i, h, total)
+        done(i)
+
+    def is_mixed(self, i):
+        return lax.rem(i, self.mix) == 0
 
     def place(self):
         rep, tp = lax.axis_index("rep"), lax.axis_index("tp")
@@ -161,7 +276,7 @@
                         s["ws"].at[i],
                     ).start()
 
-    def multiply(self, s, i, left):
+    def multiply(self, s, i, left, mixed):
         w = s["w"]
         pltpu.make_async_copy(w.at[i], w.at[i], s["ws"].at[i]).wait()
         depth = w.shape[2] * 2
@@ -177,10 +292,22 @@
                     got = jnp.dot(left, right, preferred_element_type=jnp.float32)
                     got = got.astype(jnp.bfloat16)
                     got = got.reshape(self.z, self.x, self.rows, self.half)
-                    for x in range(self.x):
-                        at = (y * self.x + x) if h == 0 else (x * self.y + y)
-                        s["b0"][i, c, h, at * self.z : (at + 1) * self.z] = got[:, x]
+                    self.put(s, i, c, h, y, got, mixed)
         start_all(self.copies(s, i, 0))
+
+    def put(self, s, i, c, h, y, got, mixed):
+        if not mixed:
+            for x in range(self.x):
+                at = (y * self.x + x) if h == 0 else (x * self.y + y)
+                s["b0"][i, c, h, at * self.z : (at + 1) * self.z] = got[:, x]
+            return
+        far = self.z // 2
+        split = got.reshape(far, 2, self.x, self.rows, self.half)
+        for x in range(self.x):
+            pair = (x * self.y + y) if h == 0 else (y * self.x + x)
+            for low in range(2):
+                at = (low * self.x * self.y + pair) * far
+                s["b0"][i, c, h, at : at + far] = split[:, low, x]
 
     def add(self, target, others):
         def piece(k, _):
@@ -238,33 +365,69 @@
 
     def finish(self, s):
         def one(i, _):
-            for stage in range(4):
-                for copy in self.copies(s, i, stage):
-                    copy.wait_send()
+            for copy in self.copies(s, i, 0):
+                copy.wait_send()
+
+            def plain():
+                for stage in range(1, 4):
+                    for copy in self.copies(s, i, stage):
+                        copy.wait_send()
+
+            def mixed():
+                for stage in range(1, 5):
+                    for copy in self.mixed_copies(s, lax.div(i, self.mix), stage):
+                        copy.wait_send()
+
+            if not self.mix:
+                plain()
+            else:
+                pl.when(self.is_mixed(i))(mixed)
+                pl.when(jnp.logical_not(self.is_mixed(i)))(plain)
             return 0
 
         lax.fori_loop(0, self.chunks, one, 0)
 
     def run(self, s, left_of, store, lags, extras=(), done=lambda i: None):
         n = self.chunks
-        stages = (
-            (lags[3], lambda i: self.after_third(s, i, store, done)),
-            (lags[2], lambda i: self.after_second(s, i)),
-            (lags[1], lambda i: self.after_first(s, i)),
-            (lags[0], lambda i: self.after_core(s, i)),
-            (0, lambda i: self.multiply(s, i, left_of(i))),
+        plain = (
+            None,
+            lambda i: self.after_third(s, i, store, done),
+            lambda i: self.after_second(s, i),
+            lambda i: self.after_first(s, i),
+            lambda i: self.after_core(s, i),
         )
+        mixed = (
+            lambda i: self.mixed_last(s, i, store, done),
+            lambda i: self.mixed_second(s, i),
+            lambda i: self.mixed_first(s, i),
+            lambda i: self.mixed_near(s, i),
+            lambda i: self.mixed_core(s, i),
+        )
+        after = lags[3] + lags[3] - lags[2]
+        stages = []
+        for lag, one, two in zip((after,) + lags[::-1], plain, mixed):
+            if one is not None:
+                stages.append((lag, one, False))
+            if self.mix:
+                stages.append((lag, two, True))
+        stages.append((0, lambda i: self.multiply(s, i, left_of(i), False), False))
+        if self.mix:
+            stages.append((0, lambda i: self.multiply(s, i, left_of(i), True), True))
 
         def step(t, _):
-            for lag, work in stages:
-                @pl.when((t >= lag) & (t < n + lag))
+            for lag, work, kind in stages:
+                now = (t >= lag) & (t < n + lag)
+                if self.mix:
+                    now = now & (self.is_mixed(t - lag + self.mix * lag) == kind)
+
+                @pl.when(now)
                 def _(lag=lag, work=work):
                     work(t - lag)
             for when, work in extras:
                 pl.when(t == when)(work)
             return 0
 
-        lax.fori_loop(0, n + lags[3], step, 0)
+        lax.fori_loop(0, n + (after if self.mix else lags[3]), step, 0)
         self.finish(s)
 
 
@@ -823,6 +986,7 @@
     expert_rows = 2 * count * CAPACITY // rep_count
     expert_red = Reduce(rep_count, tp_count, expert_rows, hidden_dev, 0)
     expert_red.chunks = expert_red.per * experts
+    expert_red.mix = 3 if expert_red.z % 2 == 0 and expert_red.z > 2 else 0
     held = sum(r.chunks * r.chunk_bytes() for r in (red, expert_red)) + 2 * (w.size + expert_w.size)
     fused = held <= ROOM
     scratch = red.scratch(2 * slice_dev)
@@ -954,16 +1118,40 @@
         return s["left"][lax.div(begin + i, red.per)]
 
     req = red.rows // 2
-    stats_ref = s["stats"]
     tok_dev = home_ref.shape[1]
     experts = x_ref.shape[0]
 
+    def hop_copies(hop):
+        axis, count_on, mine = ("rep", rep_count, rep) if hop == 0 else ("tp", tp_count, tp)
+        out = []
+        for k in range(count_on - 1):
+            to = lax.rem(mine + k + 1, count_on)
+            source = stat_ref.at[to] if hop == 0 else s["own"].at[0]
+            target = s["stats" if hop == 0 else "stats_tp"].at[mine]
+            sems = s["sas" if hop == 0 else "sbs"]
+            out.append(remote(source, target, sems.at[0, k], sems.at[1, k], {axis: to}))
+        return out
+
+    def send_stats():
+        start_all(hop_copies(0))
+        s["stats"][rep] = stat_ref[rep]
+
+    def pass_stats():
+        for copy in hop_copies(0):
+            copy.wait()
+        summed = s["stats"][0]
+        for k in range(1, rep_count):
+            summed += s["stats"][k]
+        s["own"][0] = summed
+        s["stats_tp"][tp] = summed
+        start_all(hop_copies(1))
+
     def gates():
-        for which in range(2):
-            scatter_wait(stats_ref, s["sas"], which, count)
-        summed = stats_ref[0]
-        for k in range(1, count):
-            summed += stats_ref[k]
+        for copy in hop_copies(1):
+            copy.wait()
+        summed = s["stats_tp"][0]
+        for k in range(1, tp_count):
+            summed += s["stats_tp"][k]
         tokens = tp_count * tok_dev
         ids = ids_ref[pl.ds(pl.multiple_of(rep * tokens, 8), tokens)]
         lane = lax.broadcasted_iota(jnp.int32, (tokens, LANES), 1)
@@ -997,24 +1185,8 @@
         scatter_start(home_ref, homes_ref, s["hos"], count, me, tp_count)
         homes_ref[me] = home_ref[me]
 
-    def send_stats():
-        def one(step, _):
-            to = lax.rem(me + step, count)
-            pltpu.make_async_remote_copy(
-                src_ref=stat_ref.at[lax.div(to, tp_count)],
-                dst_ref=stats_ref.at[me],
-                send_sem=s["sas"].at[0],
-                recv_sem=s["sas"].at[1],
-                device_id=device_of(to, tp_count),
-                device_id_type=MESH,
-            ).start()
-            return 0
-
-        lax.fori_loop(1, count, one, 0)
-        stats_ref[me] = stat_ref[rep]
-
-    lags = (2, 4, 6, 8)
-    extras = [(0, send_stats), (lags[3] - 1, gates)]
+    lags = (2, 5, 8, 11)
+    extras = [(0, send_stats), (4, pass_stats), (lags[3] - 1, gates)]
     if extra:
         extras.append((2, send_home))
     red.run(s, left_of, store, lags, extras)
@@ -1032,8 +1204,11 @@
     rep_count, tp_count = red.z * red.x, red.y * red.c
     scratch = red.scratch(depth)
     scratch["left"] = pltpu.VMEM((experts, rep_count * red.rows, depth), bf16)
-    scratch["sas"] = dma((2,))
-    scratch["stats"] = pltpu.VMEM((rep_count * tp_count,) + stat[1:], f32)
+    scratch["sas"] = dma((2, rep_count - 1))
+    scratch["sbs"] = dma((2, tp_count - 1))
+    scratch["stats"] = pltpu.VMEM((rep_count,) + stat[1:], f32)
+    scratch["stats_tp"] = pltpu.VMEM((tp_count,) + stat[1:], f32)
+    scratch["own"] = pltpu.VMEM((1,) + stat[1:], f32)
     scratch["seat"] = pltpu.VMEM((experts, red.rows // 2, LANES), f32)
     scratch["size"] = pltpu.VMEM((experts, red.rows // 2, LANES), f32)
     if home is not None:
@@ -1084,49 +1259,61 @@
     return ups, homes
 
 
-def finish_kernel(
-    experts, next_ref, mamba_ref, hid_ref, state_ref,
-    next_out, mamba_out, hid_out, state_out, held, sems
-):
-    parts = sems.shape[1]
-    size = state_ref.shape[0] // parts
-
-    def move(k, which):
+def finish_kernel(experts, *refs):
+    sources, targets, held = refs[:4], refs[4:8], refs[8:12]
+    moved, sems, state_sems = refs[12:]
+    parts = state_sems.shape[1]
+    size = sources[3].shape[0] // parts
+
+    def load(k):
+        return pltpu.make_async_copy(sources[k], held[k], sems.at[0, k])
+
+    def save(k):
+        return pltpu.make_async_copy(moved if k == 2 else held[k], targets[k], sems.at[1, k])
+
+    def state(k, way):
         at = pl.ds(k * size, size)
-        if which == 0:
-            return pltpu.make_async_copy(state_ref.at[at], held.at[at], sems.at[0, k])
-        return pltpu.make_async_copy(held.at[at], state_out.at[at], sems.at[1, k])
+        if way == 0:
+            return pltpu.make_async_copy(sources[3].at[at], held[3].at[at], state_sems.at[0, k])
+        return pltpu.make_async_copy(held[3].at[at], targets[3].at[at], state_sems.at[1, k])
 
     for k in range(parts):
-        move(k, 0).start()
-    next_out[...] = next_ref[...]
-    mamba_out[...] = mamba_ref[...]
-    rows = hid_out.shape[0]
+        state(k, 0).start()
+    for k in range(3):
+        load(k).start()
+    rows = moved.shape[0]
     to, source = column_iota((rows, rows), 0), column_iota((rows, rows), 1)
     block, seat = lax.div(to, experts * CAPACITY), lax.rem(to, CAPACITY)
     expert = lax.rem(lax.div(to, CAPACITY), experts)
     moves = source == expert * (rows // experts) + block * CAPACITY + seat
-    hid_out[...] = jnp.dot(
-        moves.astype(jnp.bfloat16), hid_ref[...], preferred_element_type=jnp.float32
+    for k in range(parts):
+        state(k, 0).wait()
+        state(k, 1).start()
+    for k in range(2):
+        load(k).wait()
+        save(k).start()
+    load(2).wait()
+    moved[...] = jnp.dot(
+        moves.astype(jnp.bfloat16), held[2][...], preferred_element_type=jnp.float32
     ).astype(jnp.bfloat16)
+    save(2).start()
+    for k in range(3):
+        save(k).wait()
     for k in range(parts):
-        move(k, 0).wait()
-        move(k, 1).start()
-    for k in range(parts):
-        move(k, 1).wait()
+        state(k, 1).wait()
 
 
 def finish(conv_next, mamba, hidden, state, experts):
     anywhere = pl.BlockSpec(memory_space=pl.ANY)
     arrays = (conv_next, mamba, hidden, state)
+    dma = pltpu.SemaphoreType.DMA
     return pl.pallas_call(
         functools.partial(finish_kernel, experts),
         out_shape=[jax.ShapeDtypeStruct(array.shape, array.dtype) for array in arrays],
-        in_specs=in_vmem(3) + [anywhere],
-        out_specs=in_vmem(3) + [anywhere],
-        scratch_shapes=[
-            pltpu.VMEM(state.shape, state.dtype), pltpu.SemaphoreType.DMA((2, 4))
-        ],
+        in_specs=[anywhere] * 4,
+        out_specs=[anywhere] * 4,
+        scratch_shapes=[pltpu.VMEM(array.shape, array.dtype) for array in arrays]
+        + [pltpu.VMEM(hidden.shape, hidden.dtype), dma((2, 3)), dma((2, 4))],
         name="finish",
     )(*arrays)
 

time: 107 us -> 101 us (0.944)
  Pallas kernels: 106 us -> 100 us
    pallas_call x1, Pallas kernels: 102 us -> 97.9 us  [mixer(): pl.pallas_call(functools.partial(mixer_kernel, red, names, experts, tail)...]
    pallas_call x1, Pallas kernels: 3.62 us -> 2.18 us  [finish(): pl.pallas_call(functools.partial(finish_kernel, experts), out_shape=[jax....]
where the time goes in v6:
time: 101 us
  Pallas kernels  100 us (99%)
    pallas_call x1, Pallas kernels, mixer(): pl.pallas_call(functools.partial(mixer_kernel, red, names, experts, tail)...  97.9 us
    pallas_call x1, Pallas kernels, finish(): pl.pallas_call(functools.partial(finish_kernel, experts), out_shape=[jax....  2.18 us

profile of v6, /device:TPU:0, one launch (start us, length us, event | category | flops | bytes accessed | tf_op | source)
XLA Modules:
  0.0 100.7 jit_solution(7862219603612245491)
XLA Ops:
  0.6 97.9 %mixer.1 = (bf16[3,8,2048]{2,1,0:T(8,128)(2,1)}, f32[8,16,2048]{2,1,0:T(8,128)}, bf16[2,8,3072]{2,1,0:T(8,128)(2,1)}, bf16[2,4096]{1,0:T(2,128)(2,1)}) custom-call(bf16[2,4096]{1,0:T(2,128)(2,1)} %refs_0_.1, s32[2,2]{1,0:T(2,128)} %refs_1_.1, bf16[2,128]{1,0:T(2,128)(2,1)} %refs_2_.1, bf16[4,256]{1,0:T(4,128)(2,1)} %refs_3_.1, bf16[2,256]{1,0:T(2,128)(2,1)} %refs_4_.1, ...), custom_call_target="tpu_custom_call" | custom-call | tf_op jit(solution)/shard_map/mixer/pallas_call | solution.py:1059
  98.5 2.2 %finish.1 = (bf16[3,8,2048]{2,1,0:T(8,128)(2,1)}, bf16[2,4096]{1,0:T(2,128)(2,1)}, bf16[16,3072]{1,0:T(8,128)(2,1)}, f32[8,16,2048]{2,1,0:T(8,128)}) custom-call(bf16[3,8,2048]{2,1,0:T(8,128)(2,1)} %get-tuple-element.12.refs_0_, bf16[2,4096]{1,0:T(2,128)(2,1)} %get-tuple-element.13.refs_1_, bf16[16,3072]{1,0:T(8,128)(2,1)} %bitcast.4, ...), custom_call_target="tpu_custom_call" | custom-call | tf_op jit(solution)/shard_map/finish/pallas_call | solution.py:1310
